TPU v7x, 32 devices: a whole 2x2x4 slice. The times are simulated.
32 devices in a mesh: dp: 8 (over z, x), tensor: 4 (over y, core).
Axes of the slice: x: 2, y: 2, z: 4, core: 2. Of those that a mesh axis runs over, the one named last changes fastest.
Arguments:
- hidden: bfloat16 [2048, 14336], P('dp', 'tensor'), parts along dimension 0, may hold values from -16 to 16
- signs: int32 [14336], P('tensor'), may hold values 0 or 1
- packed: int32 [14336, 512], P('tensor'), may hold values from -2147483648 to 2147483646
- group_scales: int32 [112, 4096], P('tensor'), may hold values from 1 to 16
- residual: bfloat16 [2048, 4096], P(('dp', 'tensor')), parts along dimension 0, may hold values from -16 to 16
Outputs:
- new_residual: bfloat16 [2048, 4096], P(('dp', 'tensor')), parts along dimension 0
- normed: bfloat16 [2048, 4096], P(('dp', 'tensor')), parts along dimension 0
There are 8 independent parts, one for each index of `dp`. A program takes and returns all parts, laid end to end along the dimension named above; an argument that names none is the same for every part. Nothing has to cross between parts.
Inputs may be any that keep to these rules, and one draw needn't show every extreme that they name: `packed`: bits 4 k to 4 k + 3 of word j in row f hold the code of output feature k * 512 + j plus 8.
All inputs are finite; a program needn't handle non-finite values. No bound on the sum of `signs` on one device may be relied on, other than what follows from the above.
Results may differ from a plain program's by a relative error of at most 0.0054.
Values may be sent and summed in bfloat16 or wider, within the bound.
No kernel may reach another device: no remote copies, remote signals or barrier semaphores. Data moves between devices by JAX's collectives and lax.ppermute only.
A program may use at most 256 MiB of HBM per device.

v0:
```python
import math

import jax
import jax.numpy as jnp
import numpy as np
from jax import lax
from jax.sharding import PartitionSpec as P

FF = 14336


def paley_table():
    offsets = (np.arange(13)[None, :] - np.arange(13)[:, None]) % 13
    residues = np.zeros(13)
    residues[np.arange(1, 13) ** 2 % 13] = 1.0
    quadratic = np.where(offsets == 0, 0.0, np.where(residues[offsets] > 0, 1.0, -1.0))
    conference = np.zeros((14, 14))
    conference[0, 1:] = 1.0
    conference[1:, 0] = 1.0
    conference[1:, 1:] = quadratic
    upper = np.array([[1.0, 1.0], [1.0, -1.0]])
    lower = np.array([[1.0, -1.0], [-1.0, -1.0]])
    return np.kron(conference, upper) + np.kron(np.eye(14), lower)


def sylvester(order):
    first = lax.broadcasted_iota(jnp.int32, (order, order), 0)
    second = lax.broadcasted_iota(jnp.int32, (order, order), 1)
    common = first & second
    parity = jnp.zeros((order, order), jnp.int32)
    for bit in range(max(order.bit_length() - 1, 0)):
        parity = parity ^ jnp.right_shift(common, bit) & 1
    return (1 - 2 * parity).astype(jnp.float32)


def dequantize(packed, group_scales, local_width):
    word_cols = packed.shape[1]
    group_count = group_scales.shape[0]
    group_size = local_width // group_count
    pieces = []
    for nibble in range(8):
        codes = (jnp.right_shift(packed, 4 * nibble) & 15) - 8
        scales = group_scales[:, nibble * word_cols : (nibble + 1) * word_cols]
        weights = codes.reshape(group_count, group_size, word_cols) * scales[:, None, :]
        pieces.append(weights.reshape(local_width, word_cols).astype(jnp.bfloat16))
    return jnp.concatenate(pieces, axis=1)


def local(hidden, signs, packed, group_scales, residual):
    groups = lax.axis_size("tensor")
    local_width = hidden.shape[1]
    inner = jnp.asarray(paley_table(), jnp.float32)
    outer = sylvester(local_width // 28)
    table = (
        (outer[:, None, :, None] * inner[None, :, None, :])
        .reshape(local_width, local_width)
        .astype(jnp.bfloat16)
    )
    flips = (2 * signs - 1).astype(jnp.bfloat16)
    signed = hidden * flips[None, :]
    partial_rot = jnp.dot(signed, table, preferred_element_type=jnp.float32)
    unit = 1.0 / math.sqrt(FF)
    spread = lax.all_to_all(partial_rot, "tensor", split_axis=0, concat_axis=1, tiled=True)
    token_rows = spread.shape[0]
    stacked = spread.reshape(token_rows, groups, local_width)
    mixed = jnp.einsum("rpw,qp->rqw", stacked, sylvester(groups), precision=lax.Precision.HIGHEST)
    folded = (mixed * unit).astype(jnp.bfloat16).reshape(token_rows, groups * local_width)
    rotated = lax.all_to_all(folded, "tensor", split_axis=1, concat_axis=0, tiled=True)
    weights = dequantize(packed, group_scales, local_width)
    summed = lax.psum_scatter(
        jnp.dot(rotated, weights, preferred_element_type=jnp.float32),
        "tensor",
        scatter_dimension=0,
        tiled=True,
    )
    branch = summed * (1.0 / (45.0 * math.sqrt(FF)))
    new_residual = (residual.astype(jnp.float32) + branch).astype(jnp.bfloat16)
    values = new_residual.astype(jnp.float32)
    normed = values * lax.rsqrt(jnp.mean(values * values, axis=1, keepdims=True) + 1e-05)
    return (new_residual, normed.astype(jnp.bfloat16))


def solution(mesh):
    return jax.shard_map(
        local,
        mesh=mesh,
        in_specs=(
            P("dp", "tensor"),
            P("tensor"),
            P("tensor", None),
            P("tensor", None),
            P(("dp", "tensor"), None),
        ),
        out_specs=(P(("dp", "tensor"), None), P(("dp", "tensor"), None)),
        check_vma=False,
    )
```

profile of v0, /device:TPU:0, one launch (start us, length us, event | category | flops | bytes accessed | tf_op | source)
XLA Modules:
  0.0 432.5 jit_solution(5073815844837032405)
XLA Ops:
  7.2 0.1 subtract_convert_fusion
  7.2 0.7 add_convert_fusion.1
  8.0 37.3 %multiply_convert_fusion = bf16[128,28,128,28]{3,2,1,0:T(8,128)(2,1)} fusion(f32[28,28]{1,0:T(8,128)} %constant.59.clone, f32[128,128]{1,0:T(8,128)S(1)} %subtract_convert_fusion), kind=kLoop, calls=%fused_computation | loop fusion | flops 25690112 | bytes 25758784 | tf_op jit(solution)/shard_map/convert_element_type | solution.py:57
  45.3 0.0 copy-start.3
  45.3 214.7 %reshape.100 = bf16[3584,3584,1]{1,0,2:T(8,128)(2,1)} reshape(bf16[128,28,128,28]{3,2,1,0:T(8,128)(2,1)} %multiply_convert_fusion) | data formatting | bytes 51380224 | tf_op jit(solution)/shard_map/convert_element_type | solution.py:57
  260.0 0.0 copy-done.3
  260.0 0.1 broadcast_multiply_fusion
  260.2 13.6 %fusion.33 = f32[4,64,3584]{2,1,0:T(8,128)} fusion(bf16[4,64,3584]{2,1,0:T(8,128)(2,1)S(1)} %bitcast.51, bf16[3584,3584,1]{1,0,2:T(8,128)(2,1)} %reshape.100), kind=kOutput, calls=%fused_computation.58 | convolution fusion | flops 6576668672 | bytes 31195136 | tf_op jit(solution)/shard_map/dot_general | solution.py:61
  273.8 0.0 copy-start.5
  273.8 5.1 %all-to-all-start = ((f32[4,64,3584]{2,1,0:T(8,128)}), f32[4,64,3584]{2,1,0:T(8,128)}, u32[]{:S(2)}, u32[]{:S(2)}) async-start(f32[4,64,3584]{2,1,0:T(8,128)} %fusion.33), calls=%async_computation | async-start | bytes 7340032 | tf_op jit(solution)/shard_map/all_to_all | solution.py:63
  278.9 0.0 copy-done.5
  278.9 14.1 %fusion = (bf16[3584,512]{1,0:T(8,128)(2,1)}, bf16[3584,512]{1,0:T(8,128)(2,1)}, bf16[3584,512]{1,0:T(8,128)(2,1)S(1)}, bf16[3584,512]{1,0:T(8,128)(2,1)S(1)}, b...) fusion(s32[3584,512]{1,0:T(8,128)} %param.8, ...), kind=kLoop, calls=%fused_computation.2 | loop fusion | flops 73400320 | bytes 37158912 | tf_op jit(solution)/shard_map/convert_element_type | solution.py:45
  293.1 2.1 constant_dynamic-update-slice_fusion.7
  295.2 2.1 constant_dynamic-update-slice_fusion.6
  297.3 2.1 constant_dynamic-update-slice_fusion.5
  299.4 2.1 constant_dynamic-update-slice_fusion.4
  301.5 2.1 constant_dynamic-update-slice_fusion.3
  303.6 18.6 %all-to-all-done = f32[4,64,3584]{2,1,0:T(8,128)} async-done(((f32[4,64,3584]{2,1,0:T(8,128)}), f32[4,64,3584]{2,1,0:T(8,128)}, u32[]{:S(2)}, u32[]{:S(2)}) %all-to-all-start) | async-done | bytes 3670048 | tf_op jit(solution)/shard_map/all_to_all | solution.py:63
  322.2 11.6 %fusion.9 = bf16[64,4,3584]{2,1,0:T(4,128)(2,1)S(1)} fusion(f32[4,64,3584]{2,1,0:T(8,128)} %all-to-all-done), kind=kOutput, calls=%fused_computation.19 | convolution fusion | flops 45875344 | bytes 5505024 | tf_op jit(solution)/shard_map/rpw,qp->rqw/dot_general | solution.py:66
  333.8 1.6 copy.10
  335.4 3.6 all-to-all-start.1
  339.0 0.3 reduce-scatter.2.cloned.1.call-start
  339.3 0.0 copy-start.1
  339.3 0.0 copy-start
  339.3 4.3 constant_dynamic-update-slice_fusion.2
  343.6 0.0 copy-done.1
  343.6 2.1 constant_dynamic-update-slice_fusion.1
  345.7 0.0 copy-done
  345.7 2.1 constant_dynamic-update-slice_fusion
  347.8 14.0 %all-to-all-done.1 = bf16[64,4,3584]{2,0,1:T(8,128)(2,1)S(1)} async-done(((bf16[64,4,3584]{2,0,1:T(8,128)(2,1)}), bf16[64,4,3584]{2,0,1:T(8,128)(2,1)S(1)}, u32[]{:S(2)}, u32[]{:S(2)}) %all-to-all-start.1) | async-done | bytes 1835040 | tf_op jit(solution)/shard_map/all_to_all | solution.py:68
  361.8 0.0 copy-start.4
  361.8 15.6 %fusion.34 = f32[256,4096]{1,0:T(8,128)} fusion(bf16[256,3584]{1,0:T(8,128)(2,1)S(1)} %bitcast.50, bf16[3584,4096]{1,0:T(8,128)(2,1)} %constant_dynamic-update-slice_fusion), kind=kOutput, calls=%fused_computation.59 | convolution fusion | flops 7516192768 | bytes 35389440 | tf_op jit(solution)/shard_map/dot_general | solution.py:71
  377.5 0.0 reduce-scatter.2.cloned.1.call-update
  377.5 45.6 %reduce-scatter.2.cloned.1.call-done = f32[64,4096]{1,0:T(8,128)} async-done(((f32[256,4096]{1,0:T(8,128)}), f32[64,4096]{1,0:T(8,128)}) %reduce-scatter.2.cloned.1.call-update) | async-done | bytes 1048592 | tf_op jit(solution)/shard_map/reduce_scatter | solution.py:70
  423.1 0.0 copy-done.4
  423.1 1.5 fusion.12
  424.6 0.0 copy-start.2
  424.7 0.9 fusion.13
  425.6 0.0 copy-done.2
  (2 shorter events, 0.0 us)
Async XLA Ops:
  45.3 214.7 %copy-start.3 = (bf16[256,3584]{1,0:T(8,128)(2,1)S(1)}, bf16[256,3584]{1,0:T(8,128)(2,1)}, u32[]{:S(2)}) copy-start(bf16[256,3584]{1,0:T(8,128)(2,1)} %param.6) | copy-start | bytes 5505028
  273.8 5.1 %copy-start.5 = (s32[28,4096]{1,0:T(8,128)S(1)}, s32[28,4096]{1,0:T(8,128)}, u32[]{:S(2)}) copy-start(s32[28,4096]{1,0:T(8,128)} %param.9) | copy-start | bytes 1376260
  273.8 48.4 %all-to-all-start = ((f32[4,64,3584]{2,1,0:T(8,128)}), f32[4,64,3584]{2,1,0:T(8,128)}, u32[]{:S(2)}, u32[]{:S(2)}) async-start(f32[4,64,3584]{2,1,0:T(8,128)} %fusion.33), calls=%async_computation | async-start | bytes 7340032 | tf_op jit(solution)/shard_map/all_to_all | solution.py:63
  335.4 26.4 %all-to-all-start.1 = ((bf16[64,4,3584]{2,0,1:T(8,128)(2,1)}), bf16[64,4,3584]{2,0,1:T(8,128)(2,1)S(1)}, u32[]{:S(2)}, u32[]{:S(2)}) async-start(bf16[64,4,3584]{2,0,1:T(8,128)(2,1)} %copy.10), calls=%async_computation.1 | async-start | bytes 3670016 | tf_op jit(solution)/shard_map/all_to_all | solution.py:68
  339.0 84.1 %reduce-scatter.2.cloned.1.call-start = ((), (), s32[]{:S(2)}) async-start(), calls=%async_computation.3 | async-start | bytes 5242880 | tf_op jit(solution)/shard_map/reduce_scatter | solution.py:70
  339.3 4.3 %copy-start.1 = (bf16[3584,512]{1,0:T(8,128)(2,1)S(1)}, bf16[3584,512]{1,0:T(8,128)(2,1)}, u32[]{:S(2)}) copy-start(bf16[3584,512]{1,0:T(8,128)(2,1)} %get-tuple-element.11) | copy-start | bytes 11010052
  339.3 6.4 %copy-start = (bf16[3584,512]{1,0:T(8,128)(2,1)S(1)}, bf16[3584,512]{1,0:T(8,128)(2,1)}, u32[]{:S(2)}) copy-start(bf16[3584,512]{1,0:T(8,128)(2,1)} %get-tuple-element.4) | copy-start | bytes 11010052
  361.8 61.3 %copy-start.4 = (bf16[64,4096]{1,0:T(8,128)(2,1)S(1)}, bf16[64,4096]{1,0:T(8,128)(2,1)}, u32[]{:S(2)}) copy-start(bf16[64,4096]{1,0:T(8,128)(2,1)} %param.10) | copy-start | bytes 1572868
  424.6 1.0 copy-start.2
Sparse Core Ops, SparseCore 0:
  377.6 45.4 reduce-scatter.1
where the time goes:
time: 433 us; the launch traced here: 432 us
  local copies, waits for them, and re-layouts  235 us (54%)
  waiting for transfers between devices  78.3 us (18%)
  other arithmetic  54.8 us (13%)
  matrix products  40.9 us (9%)
  between operations  14.1 us (3%)
  starting transfers between devices  8.93 us (2%)
    convert_element_type x1, local copies, waits for them, and re-layouts, local(): table = (outer[:, None, :, None] * inner[None, :, None, :]).reshape(local...  215 us
    reduce_scatter x1, waiting for transfers between devices, local(): lax.psum_scatter(jnp.dot(rotated, weights, preferred_element_type=jnp.flo...  45.6 us
    convert_element_type x1, other arithmetic, local(): table = (outer[:, None, :, None] * inner[None, :, None, :]).reshape(local...  37.3 us
    all_to_all x1, waiting for transfers between devices, local(): lax.all_to_all(partial_rot, 'tensor', split_axis=0, concat_axis=1, tiled=...  18.6 us
    unnamed x19, local copies, waits for them, and re-layouts  17 us
    dot_general x1, matrix products, local(): jnp.dot(rotated, weights, preferred_element_type=jnp.float32)  15.6 us
    convert_element_type x1, other arithmetic, dequantize(): pieces.append(weights.reshape(local_width, word_cols).astype(jnp.bfloat16))  14.1 us
    all_to_all x1, waiting for transfers between devices, local(): lax.all_to_all(folded, 'tensor', split_axis=1, concat_axis=0, tiled=True)  14 us
  transfers between devices with their start and end apart: 3, of which 3 were waited for; matrix products, arithmetic and copies ran while one was open for 8% of the time, Pallas kernels for 0%

commit v1 on v0

v1 whole, which is shorter than its diff:
```python
import functools
import math

import jax
import jax.numpy as jnp
import numpy as np
from jax import lax
from jax.experimental import pallas as pl
from jax.experimental.pallas import tpu as pltpu
from jax.sharding import PartitionSpec as P

ORDER = 28
DENSE = 896
TILE_ROWS = 16
COLUMN_TILE = 512


def paley_table():
    offsets = (np.arange(13)[None, :] - np.arange(13)[:, None]) % 13
    residues = np.zeros(13)
    residues[np.arange(1, 13) ** 2 % 13] = 1.0
    quadratic = np.where(offsets == 0, 0.0, np.where(residues[offsets] > 0, 1.0, -1.0))
    conference = np.zeros((14, 14))
    conference[0, 1:] = 1.0
    conference[1:, 0] = 1.0
    conference[1:, 1:] = quadratic
    upper = np.array([[1.0, 1.0], [1.0, -1.0]])
    lower = np.array([[1.0, -1.0], [-1.0, -1.0]])
    return np.kron(conference, upper) + np.kron(np.eye(14), lower)


def sylvester(order):
    table = np.ones((1, 1))
    while table.shape[0] < order:
        table = np.kron(np.array([[1.0, 1.0], [1.0, -1.0]]), table)
    return table


def dense_table():
    return np.kron(sylvester(DENSE // ORDER), paley_table().T)


def dequantize_kernel(packed_ref, scales_ref, weights_ref):
    group_count = scales_ref.shape[0]
    group_size = packed_ref.shape[0] // group_count
    words = packed_ref.shape[1]

    @pl.loop(0, group_count)
    def _(group):
        rows = pl.ds(pl.multiple_of(group * group_size, group_size), group_size)
        word = packed_ref[rows, :] ^ np.int32(-2004318072)
        for nibble in range(8):
            columns = pl.ds(nibble * words, words)
            codes = jnp.right_shift(jnp.left_shift(word, 28 - 4 * nibble), 28)
            scale = scales_ref[pl.ds(group, 1), columns].astype(jnp.float32)
            weights_ref[rows, columns] = (codes.astype(jnp.float32) * scale).astype(jnp.bfloat16)


def dequantize(packed, group_scales):
    width, words = packed.shape
    return pl.pallas_call(
        dequantize_kernel,
        out_shape=pltpu.VMEM((width, 8 * words), jnp.bfloat16),
        in_specs=[pl.BlockSpec(memory_space=pltpu.VMEM)] * 2,
        out_specs=pl.BlockSpec(memory_space=pltpu.VMEM),
        compiler_params=pltpu.CompilerParams(vmem_limit_bytes=24 * 2**20),
        cost_estimate=pl.CostEstimate(
            flops=width * words * 8 * 4, bytes_accessed=width * words * 4, transcendentals=0
        ),
        name="dequantize",
    )(packed, group_scales)


def project_kernel(groups, unit, coef_ref, core_ref, *refs):
    parts = refs[:groups]
    table_ref, weights_ref, keep_ref, send_ref, rotated_ref = refs[groups:]
    rows, width = parts[0].shape
    blocks = width // DENSE
    mixed = []
    for block in range(blocks):
        columns = pl.ds(block * DENSE, DENSE)
        total = coef_ref[0] * parts[0][:, columns].astype(jnp.float32)
        for r in range(1, groups):
            total = total + coef_ref[r] * parts[r][:, columns].astype(jnp.float32)
        mixed.append(total)
    span = 1
    while span < blocks:
        for first in range(blocks):
            if not first & span:
                a, b = mixed[first], mixed[first + span]
                mixed[first], mixed[first + span] = a + b, a - b
        span *= 2
    for block in range(blocks):
        high = mixed[block].astype(jnp.bfloat16)
        low = (mixed[block] - high.astype(jnp.float32)).astype(jnp.bfloat16)
        both = jnp.dot(
            jnp.concatenate([high, low], axis=0), table_ref[...], preferred_element_type=jnp.float32
        )
        rotated_ref[:, pl.ds(block * DENSE, DENSE)] = (
            (both[:rows] + both[rows:]) * unit
        ).astype(jnp.bfloat16)
    half = rows // 2
    upper = core_ref[0] == 1

    @pl.loop(0, weights_ref.shape[1] // COLUMN_TILE)
    def _(tile):
        columns = pl.ds(pl.multiple_of(tile * COLUMN_TILE, COLUMN_TILE), COLUMN_TILE)
        product = jnp.dot(
            rotated_ref[...], weights_ref[:, columns], preferred_element_type=jnp.float32
        )
        first, second = product[:half], product[half:]
        keep_ref[:, columns] = jnp.where(upper, second, first)
        send_ref[:, columns] = jnp.where(upper, first, second).astype(jnp.bfloat16)


def project(parts, coef, core, table, weights, unit):
    groups = len(parts)
    rows, width = parts[0].shape
    features = weights.shape[1]
    vmem = pl.BlockSpec(memory_space=pltpu.VMEM)
    smem = pl.BlockSpec(memory_space=pltpu.SMEM)
    return pl.pallas_call(
        functools.partial(project_kernel, groups, unit),
        out_shape=(
            jax.ShapeDtypeStruct((rows // 2, features), jnp.float32),
            jax.ShapeDtypeStruct((rows // 2, features), jnp.bfloat16),
        ),
        in_specs=[smem, smem] + [vmem] * (groups + 2),
        out_specs=(vmem, vmem),
        scratch_shapes=[pltpu.VMEM((rows, width), jnp.bfloat16)],
        compiler_params=pltpu.CompilerParams(vmem_limit_bytes=24 * 2**20),
        cost_estimate=pl.CostEstimate(
            flops=2 * rows * width * (features + 2 * DENSE),
            bytes_accessed=2 * groups * rows * width,
            transcendentals=0,
        ),
        name="project",
    )(coef, core, *parts, table, pltpu.with_memory_space_constraint(weights, pltpu.VMEM))


def local(hidden, signs, packed, group_scales, residual):
    groups = lax.axis_size("tensor")
    bits = groups.bit_length() - 1
    me = lax.axis_index("tensor")
    width = hidden.shape[1]
    total_width = width * groups
    token_rows = residual.shape[0]
    chunks = token_rows // TILE_ROWS
    features = residual.shape[1]
    unit = 1.0 / math.sqrt(total_width)
    flips = (2 * signs - 1).astype(jnp.bfloat16)

    def swap(value, bit):
        return lax.ppermute(value, "tensor", [(i, i ^ (1 << bit)) for i in range(groups)])

    relative = jnp.arange(groups, dtype=jnp.int32)
    common = me & (me ^ relative)
    parity = jnp.zeros_like(common)
    for bit in range(bits):
        parity = parity ^ (jnp.right_shift(common, bit) & 1)
    coef = (1 - 2 * parity).astype(jnp.float32)
    core = (me & 1).reshape(1)

    by_rows = hidden.reshape((2,) * bits + (chunks, TILE_ROWS, width))
    own = []
    for chunk in range(chunks):
        piece = lax.index_in_dim(by_rows, chunk, axis=bits, keepdims=False)
        piece = jnp.transpose(piece, tuple(reversed(range(bits))) + (bits, bits + 1))
        own.append(piece.reshape(groups * TILE_ROWS, width) * flips[None, :])
    gathered = []
    for chunk in range(chunks):
        have = {0: own[chunk]}
        for bit in reversed(range(bits)):
            have.update({r ^ (1 << bit): swap(value, bit) for r, value in list(have.items())})
        gathered.append([have[r] for r in range(groups)])
    table = jnp.asarray(dense_table(), jnp.bfloat16)
    weights = dequantize(packed, group_scales)
    out_new, out_normed = [], []
    for chunk in range(chunks):
        value, send = project(gathered[chunk], coef, core, table, weights, unit)
        value = value + swap(send, 0).astype(jnp.float32)
        for bit in range(1, bits):
            half = value.shape[0] // 2
            upper = (jnp.right_shift(me, bit) & 1) == 1
            send = jnp.where(upper, value[:half], value[half:]).astype(jnp.bfloat16)
            value = jnp.where(upper, value[half:], value[:half]) + swap(send, bit).astype(jnp.float32)
        branch = value * (1.0 / (45.0 * math.sqrt(total_width)))
        start = residual[chunk * TILE_ROWS : (chunk + 1) * TILE_ROWS].astype(jnp.float32)
        new_residual = (start + branch).astype(jnp.bfloat16)
        values = new_residual.astype(jnp.float32)
        normed = values * lax.rsqrt(jnp.mean(values * values, axis=1, keepdims=True) + 1e-05)
        out_new.append(new_residual)
        out_normed.append(normed.astype(jnp.bfloat16))
    return jnp.concatenate(out_new, axis=0), jnp.concatenate(out_normed, axis=0)


def solution(mesh):
    return jax.shard_map(
        local,
        mesh=mesh,
        in_specs=(
            P("dp", "tensor"),
            P("tensor"),
            P("tensor", None),
            P("tensor", None),
            P(("dp", "tensor"), None),
        ),
        out_specs=(P(("dp", "tensor"), None), P(("dp", "tensor"), None)),
        check_vma=False,
    )
```

time: 433 us -> 120 us (0.28)
  local copies, waits for them, and re-layouts: 235 us -> 23.6 us
  waiting for transfers between devices: 78.3 us -> 25.2 us
  Pallas kernels: 0 us -> 52.2 us
  other arithmetic: 54.8 us -> 2.9 us
  matrix products: 40.9 us -> 0 us
  between operations: 14.1 us -> 0.83 us
  starting transfers between devices: 8.93 us -> 14.9 us
    convert_element_type x2 -> x0, local copies, waits for them, and re-layouts: 216 us -> none  [the longest x1 215 us: local(): table = (outer[:, None, :, None] * inner[None, :, None, :]).reshape(local...]
    pallas_call x0 -> x5, Pallas kernels: none -> 52.2 us  [the longest x4 40.3 us: project(): pl.pallas_call(functools.partial(project_kernel, groups, unit), out_shape...]
    convert_element_type x4 -> x7, other arithmetic: 52.5 us -> 0.35 us  [the longest x2 0.23 us: local(): out_normed.append(normed.astype(jnp.bfloat16))]
    reduce_scatter x1 -> x0, waiting for transfers between devices: 45.6 us -> none  [local(): lax.psum_scatter(jnp.dot(rotated, weights, preferred_element_type=jnp.flo...]
    dot_general x3 -> x0, matrix products: 40.9 us -> none  [the longest x1 15.6 us: local(): jnp.dot(rotated, weights, preferred_element_type=jnp.float32)]
    all_to_all x2 -> x0, waiting for transfers between devices: 32.6 us -> none  [the longest x1 18.6 us: local(): lax.all_to_all(partial_rot, 'tensor', split_axis=0, concat_axis=1, tiled=...]
    ppermute x0 -> x20, waiting for transfers between devices: none -> 25.2 us  [swap(): lax.ppermute(value, 'tensor', [(i, i ^ 1 << bit) for i in range(groups)])]
    ppermute x0 -> x20, starting transfers between devices: none -> 14.9 us  [swap(): lax.ppermute(value, 'tensor', [(i, i ^ 1 << bit) for i in range(groups)])]
  transfers between devices with their start and end apart: 3 -> 20, of which waited for: 3 -> 6; matrix products, arithmetic and copies ran while one was open for 8% -> 0% of each run, Pallas kernels for 0% -> 44%
where the time goes in v1:
time: 120 us
  Pallas kernels  52.2 us (44%)
  waiting for transfers between devices  25.2 us (21%)
  local copies, waits for them, and re-layouts  23.6 us (20%)
  starting transfers between devices  14.9 us (12%)
  other arithmetic  2.9 us (2%)
    pallas_call x4, Pallas kernels, project(): pl.pallas_call(functools.partial(project_kernel, groups, unit), out_shape...  40.3 us
    ppermute x20, waiting for transfers between devices, swap(): lax.ppermute(value, 'tensor', [(i, i ^ 1 << bit) for i in range(groups)])  25.2 us
    unnamed x30, local copies, waits for them, and re-layouts  22.1 us
    ppermute x20, starting transfers between devices, swap(): lax.ppermute(value, 'tensor', [(i, i ^ 1 << bit) for i in range(groups)])  14.9 us
    pallas_call x1, Pallas kernels, dequantize(): pl.pallas_call(dequantize_kernel, out_shape=pltpu.VMEM((width, 8 * words)...  11.9 us
  transfers between devices with their start and end apart: 20, of which 6 were waited for; matrix products, arithmetic and copies ran while one was open for 0% of the time, Pallas kernels for 44%

profile of v1, /device:TPU:0, one launch (start us, length us, event | category | flops | bytes accessed | tf_op | source)
XLA Modules:
  0.0 119.7 jit_solution(15781019856432968780)
XLA Ops:
  0.6 1.6 %fusion.8 = (bf16[2,2,1,16,3584]{4,3,2,1,0:T(8,128)(2,1)S(1)}, bf16[2,2,1,16,3584]{4,3,2,1,0:T(8,128)(2,1)S(1)}, bf16[2,2,1,16,3584]{4,3,2,1,0:T(8,128)(2,1)S(1)}, bf16[2,2,1,16,3584]{4,3,2,1,0:T(8,128)(2,1)S(1)}) fusion(bf16[2,2,4,16,3584]{4,3,2,1,0:T(8,128)(2,1)} %bitcast.26), kind=kLoop, calls=%fused_computation.40 | loop fusion | bytes 3670016 | tf_op jit(solution)/shard_map/slice | solution.py:167
  2.2 0.0 copy-start.12
  2.4 0.6 copy-done.12
  2.9 0.2 bitcast_multiply_fusion.3
  3.2 3.1 %collective-permute-start.16 = (bf16[64,3584]{1,0:T(8,128)(2,1)S(1)}, bf16[64,3584]{1,0:T(8,128)(2,1)}, u32[]{:S(2)}, u32[]{:S(2)}) collective-permute-start(bf16[64,3584]{1,0:T(8,128)(2,1)S(1)} %get-tuple-element.39.refs_0_), channel_id=1, source_target_pairs={{0,2},{1,3},{2,0},{3,1},{4,6},{5,7},{6,4},{7,5},{8,10},{9,11},{10,... | collective-permute-start | bytes 1376264 | tf_op jit(solution)/shard_map/ppermute | solution.py:154
  6.2 0.0 collective-permute-start.15
  6.3 0.2 collective-permute-start.11
  6.4 1.9 %collective-permute-start.6 = (bf16[64,3584]{1,0:T(8,128)(2,1)S(1)}, bf16[64,3584]{1,0:T(8,128)(2,1)S(1)}, u32[]{:S(2)}, u32[]{:S(2)}) collective-permute-start(bf16[64,3584]{1,0:T(8,128)(2,1)S(1)} %get-tuple-element.37.refs_0_), channel_id=1, source_target_pairs={{0,2},{1,3},{2,0},{3,1},{4,6},{5,7},{6,4},{7,5},{8,10},{9,11},{10,... | collective-permute-start | bytes 1376264 | tf_op jit(solution)/shard_map/ppermute | solution.py:154
  8.3 9.4 %collective-permute-done.16.refs_2_ = bf16[64,3584]{1,0:T(8,128)(2,1)} collective-permute-done((bf16[64,3584]{1,0:T(8,128)(2,1)S(1)}, bf16[64,3584]{1,0:T(8,128)(2,1)}, u32[]{:S(2)}, u32[]{:S(2)}) %collective-permute-start.16) | collective-permute-done | bytes 458784 | tf_op jit(solution)/shard_map/ppermute | solution.py:154
  17.7 0.0 collective-permute-start.17
  17.7 0.5 collective-permute-start.10
  18.2 0.0 collective-permute-done.15.refs_1_
  18.2 0.8 copy-done.3
  19.0 2.0 %collective-permute-start.1 = (bf16[64,3584]{1,0:T(8,128)(2,1)S(1)}, bf16[64,3584]{1,0:T(8,128)(2,1)S(1)}, u32[]{:S(2)}, u32[]{:S(2)}) collective-permute-start(bf16[64,3584]{1,0:T(8,128)(2,1)S(1)} %get-tuple-element.36.refs_0_), channel_id=1, source_target_pairs={{0,2},{1,3},{2,0},{3,1},{4,6},{5,7},{6,4},{7,5},{8,10},{9,11},{10,... | collective-permute-start | bytes 1376264 | tf_op jit(solution)/shard_map/ppermute | solution.py:154
  21.0 6.5 %collective-permute-done.11.refs_2_ = bf16[64,3584]{1,0:T(8,128)(2,1)} collective-permute-done((bf16[64,3584]{1,0:T(8,128)(2,1)S(1)}, bf16[64,3584]{1,0:T(8,128)(2,1)}, u32[]{:S(2)}, u32[]{:S(2)}) %collective-permute-start.11) | collective-permute-done | bytes 458784 | tf_op jit(solution)/shard_map/ppermute | solution.py:154
  27.6 0.0 collective-permute-start.12
  27.6 11.9 %dequantize.1.refs_5_ = bf16[3584,4096]{1,0:T(8,128)(2,1)S(1)} custom-call(s32[3584,512]{1,0:T(8,128)} %packed_ref.1, s32[28,4096]{1,0:T(8,128)S(1)} %copy-done.2), custom_call_target="tpu_custom_call" | custom-call | flops 58720256 | bytes 7340032 | tf_op jit(solution)/shard_map/dequantize/pallas_call | solution.py:61
  39.5 9.7 %copy-done = bf16[3584,4096]{1,0:T(8,128)(2,1)} copy-done((bf16[3584,4096]{1,0:T(8,128)(2,1)}, bf16[3584,4096]{1,0:T(8,128)(2,1)S(1)}, u32[]{:S(2)}) %copy-start) | copy-done | bytes 29360152
  49.2 0.0 collective-permute-done.6.refs_2_
  49.2 0.6 collective-permute-start.5
  49.8 0.0 collective-permute-done.17.refs_3_
  49.8 0.1 collective-permute-start.7
  49.9 0.0 copy-done.4
  49.9 9.3 %copy-done.1 = bf16[3584,4096]{1,0:T(8,128)(2,1)S(1)} copy-done((bf16[3584,4096]{1,0:T(8,128)(2,1)S(1)}, bf16[3584,4096]{1,0:T(8,128)(2,1)}, u32[]{:S(2)}) %copy-start.1) | copy-done | bytes 29360152
  59.2 10.1 %project.7 = (f32[32,4096]{1,0:T(8,128)}, bf16[32,4096]{1,0:T(8,128)(2,1)S(1)}) custom-call(f32[4]{0:T(128)S(1)} %subtract_convert_fusion.coef_ref, s32[1]{0:T(128)} %bitcast.core_ref, bf16[64,3584]{1,0:T(8,128)(2,1)S(1)} %get-tuple-element.39.refs_0_, bf16[64,3584]{1,0:T(8,128)(2,1)S(1)} %copy-done.4, bf16[64,3584]{1,0:T(8,128)(2,1)} %collective-permute-done.16.refs_2_, ...), custom_call_target="tpu_custom_call" | custom-call | flops 2701131776 | bytes 1835008 | tf_op jit(solution)/shard_map/project/pallas_call | solution.py:122
  69.4 0.0 collective-permute-done.10.refs_1_
  69.4 0.4 collective-permute-start
  69.8 0.0 collective-permute-done.1.refs_2_
  69.8 0.1 collective-permute-start.2
  69.9 0.0 collective-permute-done.12.refs_3_
  69.9 0.4 collective-permute-start.18
  70.3 10.2 %project.6 = (f32[32,4096]{1,0:T(8,128)}, bf16[32,4096]{1,0:T(8,128)(2,1)S(1)}) custom-call(f32[4]{0:T(128)S(1)} %subtract_convert_fusion.coef_ref, s32[1]{0:T(128)} %bitcast.core_ref, bf16[64,3584]{1,0:T(8,128)(2,1)S(1)} %get-tuple-element.38.refs_0_, bf16[64,3584]{1,0:T(8,128)(2,1)} %collective-permute-done.10.refs_1_, ...), custom_call_target="tpu_custom_call" | custom-call | flops 2701131776 | bytes 1835008 | tf_op jit(solution)/shard_map/project/pallas_call | solution.py:122
  80.5 0.0 collective-permute-done.5.refs_1_
  80.5 0.1 collective-permute-start.13
  80.6 0.0 collective-permute-done.7.refs_3_
  80.6 0.8 copy-done.10
  81.4 10.0 %project.5 = (f32[32,4096]{1,0:T(8,128)}, bf16[32,4096]{1,0:T(8,128)(2,1)S(1)}) custom-call(f32[4]{0:T(128)S(1)} %subtract_convert_fusion.coef_ref, s32[1]{0:T(128)} %bitcast.core_ref, bf16[64,3584]{1,0:T(8,128)(2,1)S(1)} %get-tuple-element.37.refs_0_, bf16[64,3584]{1,0:T(8,128)(2,1)S(1)} %collective-permute-done.5.refs_1_, ...), custom_call_target="tpu_custom_call" | custom-call | flops 2701131776 | bytes 1835008 | tf_op jit(solution)/shard_map/project/pallas_call | solution.py:122
  91.4 0.4 collective-permute-start.8
  91.8 0.0 collective-permute-done.refs_1_
  91.8 0.0 collective-permute-done.2.refs_3_
  91.8 0.8 copy-done.11
  92.6 9.9 %project.4 = (f32[32,4096]{1,0:T(8,128)}, bf16[32,4096]{1,0:T(8,128)(2,1)S(1)}) custom-call(f32[4]{0:T(128)S(1)} %subtract_convert_fusion.coef_ref, s32[1]{0:T(128)} %bitcast.core_ref, bf16[64,3584]{1,0:T(8,128)(2,1)S(1)} %get-tuple-element.36.refs_0_, bf16[64,3584]{1,0:T(8,128)(2,1)S(1)} %collective-permute-done.refs_1_, ...), custom_call_target="tpu_custom_call" | custom-call | flops 2701131776 | bytes 1835008 | tf_op jit(solution)/shard_map/project/pallas_call | solution.py:122
  102.5 0.1 collective-permute-start.3
  102.6 0.0 collective-permute-done.18
  102.6 0.1 convert_add_fusion
  102.7 0.0 copy-start.9
  102.7 2.1 %collective-permute-start.19 = (bf16[16,4096]{1,0:T(8,128)(2,1)S(1)}, bf16[16,4096]{1,0:T(8,128)(2,1)S(1)}, u32[]{:S(2)}, u32[]{:S(2)}) collective-permute-start(bf16[16,4096]{1,0:T(8,128)(2,1)S(1)} %select_convert_fusion), channel_id=1, source_target_pairs={{0,2},{1,3},{2,0},{3,1},{4,6},{5,7},{6,4},{7,5},{8,10},{9,11},{10,... | collective-permute-start | bytes 393224 | tf_op jit(solution)/shard_map/ppermute | solution.py:154
  104.8 0.0 collective-permute-done.13
  104.8 0.1 convert_add_fusion.1
  104.9 0.0 copy-start.5
  104.9 0.8 collective-permute-start.14
  105.8 0.0 collective-permute-done.8
  105.9 1.3 %collective-permute-start.9 = (bf16[16,4096]{1,0:T(8,128)(2,1)S(1)}, bf16[16,4096]{1,0:T(8,128)(2,1)S(1)}, u32[]{:S(2)}, u32[]{:S(2)}) collective-permute-start(bf16[16,4096]{1,0:T(8,128)(2,1)S(1)} %select_convert_fusion.2), channel_id=1, source_target_pairs={{0,2},{1,3},{2,0},{3,1},{4,6},{5,7},{6,4},{7,5},{8,10},{9,11},{10,... | collective-permute-start | bytes 393224 | tf_op jit(solution)/shard_map/ppermute | solution.py:154
  107.2 0.0 collective-permute-done.3
  107.3 0.8 collective-permute-start.4
  108.1 1.1 collective-permute-done.19
  109.2 2.8 %collective-permute-done.14 = bf16[16,4096]{1,0:T(8,128)(2,1)S(1)} collective-permute-done((bf16[16,4096]{1,0:T(8,128)(2,1)S(1)}, bf16[16,4096]{1,0:T(8,128)(2,1)S(1)}, u32[]{:S(2)}, u32[]{:S(2)}) %collective-permute-start.14) | collective-permute-done | bytes 131104 | tf_op jit(solution)/shard_map/ppermute | solution.py:154
  112.0 2.8 %collective-permute-done.9 = bf16[16,4096]{1,0:T(8,128)(2,1)S(1)} collective-permute-done((bf16[16,4096]{1,0:T(8,128)(2,1)S(1)}, bf16[16,4096]{1,0:T(8,128)(2,1)S(1)}, u32[]{:S(2)}, u32[]{:S(2)}) %collective-permute-start.9) | collective-permute-done | bytes 131104 | tf_op jit(solution)/shard_map/ppermute | solution.py:154
  114.8 2.5 %collective-permute-done.4 = bf16[16,4096]{1,0:T(8,128)(2,1)S(1)} collective-permute-done((bf16[16,4096]{1,0:T(8,128)(2,1)S(1)}, bf16[16,4096]{1,0:T(8,128)(2,1)S(1)}, u32[]{:S(2)}, u32[]{:S(2)}) %collective-permute-start.4) | collective-permute-done | bytes 131104 | tf_op jit(solution)/shard_map/ppermute | solution.py:154
  117.3 0.4 fusion
  117.8 0.1 fusion.1
  117.9 0.8 pad_maximum_fusion
  118.7 0.1 fusion.5
  118.8 0.8 pad_maximum_fusion.1
  (32 shorter events, 0.4 us)
Async XLA Ops:
  2.2 0.7 copy-start.12
  2.9 24.6 %copy-start.2 = (s32[28,4096]{1,0:T(8,128)S(1)}, s32[28,4096]{1,0:T(8,128)}, u32[]{:S(2)}) copy-start(s32[28,4096]{1,0:T(8,128)} %scales_ref.1) | copy-start | bytes 1376260
  3.2 14.5 %collective-permute-start.16 = (bf16[64,3584]{1,0:T(8,128)(2,1)S(1)}, bf16[64,3584]{1,0:T(8,128)(2,1)}, u32[]{:S(2)}, u32[]{:S(2)}) collective-permute-start(bf16[64,3584]{1,0:T(8,128)(2,1)S(1)} %get-tuple-element.39.refs_0_), channel_id=1, source_target_pairs={{0,2},{1,3},{2,0},{3,1},{4,6},{5,7},{6,4},{7,5},{8,10},{9,11},{10,... | collective-permute-start | bytes 1376264 | tf_op jit(solution)/shard_map/ppermute | solution.py:154
  6.2 12.0 %collective-permute-start.15 = (bf16[64,3584]{1,0:T(8,128)(2,1)S(1)}, bf16[64,3584]{1,0:T(8,128)(2,1)S(1)}, u32[]{:S(2)}, u32[]{:S(2)}) collective-permute-start(bf16[64,3584]{1,0:T(8,128)(2,1)S(1)} %get-tuple-element.39.refs_0_), channel_id=1, source_target_pairs={{0,1},{1,0},{2,3},{3,2},{4,5},{5,4},{6,7},{7,6},{8,9},{9,8},{10,11... | collective-permute-start | bytes 1376264 | tf_op jit(solution)/shard_map/ppermute | solution.py:154
  6.3 21.3 %collective-permute-start.11 = (bf16[64,3584]{1,0:T(8,128)(2,1)S(1)}, bf16[64,3584]{1,0:T(8,128)(2,1)}, u32[]{:S(2)}, u32[]{:S(2)}) collective-permute-start(bf16[64,3584]{1,0:T(8,128)(2,1)S(1)} %get-tuple-element.38.refs_0_), channel_id=1, source_target_pairs={{0,2},{1,3},{2,0},{3,1},{4,6},{5,7},{6,4},{7,5},{8,10},{9,11},{10,... | collective-permute-start | bytes 1376264 | tf_op jit(solution)/shard_map/ppermute | solution.py:154
  6.4 42.8 %collective-permute-start.6 = (bf16[64,3584]{1,0:T(8,128)(2,1)S(1)}, bf16[64,3584]{1,0:T(8,128)(2,1)S(1)}, u32[]{:S(2)}, u32[]{:S(2)}) collective-permute-start(bf16[64,3584]{1,0:T(8,128)(2,1)S(1)} %get-tuple-element.37.refs_0_), channel_id=1, source_target_pairs={{0,2},{1,3},{2,0},{3,1},{4,6},{5,7},{6,4},{7,5},{8,10},{9,11},{10,... | collective-permute-start | bytes 1376264 | tf_op jit(solution)/shard_map/ppermute | solution.py:154
  17.7 32.1 %collective-permute-start.17 = (bf16[64,3584]{1,0:T(8,128)(2,1)}, bf16[64,3584]{1,0:T(8,128)(2,1)}, u32[]{:S(2)}, u32[]{:S(2)}) collective-permute-start(bf16[64,3584]{1,0:T(8,128)(2,1)} %collective-permute-done.16.refs_2_), channel_id=1, source_target_pairs={{0,1},{1,0},{2,3},{3,2},{4,5},{5,4},{6,7},{7,6},{8,9},{9,8},{10,11... | collective-permute-start | bytes 1376264 | tf_op jit(solution)/shard_map/ppermute | solution.py:154
  17.7 51.6 %collective-permute-start.10 = (bf16[64,3584]{1,0:T(8,128)(2,1)S(1)}, bf16[64,3584]{1,0:T(8,128)(2,1)}, u32[]{:S(2)}, u32[]{:S(2)}) collective-permute-start(bf16[64,3584]{1,0:T(8,128)(2,1)S(1)} %get-tuple-element.38.refs_0_), channel_id=1, source_target_pairs={{0,1},{1,0},{2,3},{3,2},{4,5},{5,4},{6,7},{7,6},{8,9},{9,8},{10,11... | collective-permute-start | bytes 1376264 | tf_op jit(solution)/shard_map/ppermute | solution.py:154
  18.2 0.8 copy-start.3
  19.0 50.8 %collective-permute-start.1 = (bf16[64,3584]{1,0:T(8,128)(2,1)S(1)}, bf16[64,3584]{1,0:T(8,128)(2,1)S(1)}, u32[]{:S(2)}, u32[]{:S(2)}) collective-permute-start(bf16[64,3584]{1,0:T(8,128)(2,1)S(1)} %get-tuple-element.36.refs_0_), channel_id=1, source_target_pairs={{0,2},{1,3},{2,0},{3,1},{4,6},{5,7},{6,4},{7,5},{8,10},{9,11},{10,... | collective-permute-start | bytes 1376264 | tf_op jit(solution)/shard_map/ppermute | solution.py:154
  27.6 42.3 %collective-permute-start.12 = (bf16[64,3584]{1,0:T(8,128)(2,1)}, bf16[64,3584]{1,0:T(8,128)(2,1)}, u32[]{:S(2)}, u32[]{:S(2)}) collective-permute-start(bf16[64,3584]{1,0:T(8,128)(2,1)} %collective-permute-done.11.refs_2_), channel_id=1, source_target_pairs={{0,1},{1,0},{2,3},{3,2},{4,5},{5,4},{6,7},{7,6},{8,9},{9,8},{10,11... | collective-permute-start | bytes 1376264 | tf_op jit(solution)/shard_map/ppermute | solution.py:154
  27.6 22.3 %copy-start.4 = (bf16[64,3584]{1,0:T(8,128)(2,1)S(1)}, bf16[64,3584]{1,0:T(8,128)(2,1)}, u32[]{:S(2)}) copy-start(bf16[64,3584]{1,0:T(8,128)(2,1)} %copy-done.3) | copy-start | bytes 1376260
  39.5 9.7 %copy-start = (bf16[3584,4096]{1,0:T(8,128)(2,1)}, bf16[3584,4096]{1,0:T(8,128)(2,1)S(1)}, u32[]{:S(2)}) copy-start(bf16[3584,4096]{1,0:T(8,128)(2,1)S(1)} %dequantize.1.refs_5_) | copy-start | bytes 88080384
  49.2 31.3 %collective-permute-start.5 = (bf16[64,3584]{1,0:T(8,128)(2,1)S(1)}, bf16[64,3584]{1,0:T(8,128)(2,1)S(1)}, u32[]{:S(2)}, u32[]{:S(2)}) collective-permute-start(bf16[64,3584]{1,0:T(8,128)(2,1)S(1)} %get-tuple-element.37.refs_0_), channel_id=1, source_target_pairs={{0,1},{1,0},{2,3},{3,2},{4,5},{5,4},{6,7},{7,6},{8,9},{9,8},{10,11... | collective-permute-start | bytes 1376264 | tf_op jit(solution)/shard_map/ppermute | solution.py:154
  49.8 30.8 %collective-permute-start.7 = (bf16[64,3584]{1,0:T(8,128)(2,1)S(1)}, bf16[64,3584]{1,0:T(8,128)(2,1)S(1)}, u32[]{:S(2)}, u32[]{:S(2)}) collective-permute-start(bf16[64,3584]{1,0:T(8,128)(2,1)S(1)} %collective-permute-done.6.refs_2_), channel_id=1, source_target_pairs={{0,1},{1,0},{2,3},{3,2},{4,5},{5,4},{6,7},{7,6},{8,9},{9,8},{10,11... | collective-permute-start | bytes 1376264 | tf_op jit(solution)/shard_map/ppermute | solution.py:154
  49.9 9.4 %copy-start.1 = (bf16[3584,4096]{1,0:T(8,128)(2,1)S(1)}, bf16[3584,4096]{1,0:T(8,128)(2,1)}, u32[]{:S(2)}) copy-start(bf16[3584,4096]{1,0:T(8,128)(2,1)} %copy-done) | copy-start | bytes 88080384
  69.4 22.4 %collective-permute-start = (bf16[64,3584]{1,0:T(8,128)(2,1)S(1)}, bf16[64,3584]{1,0:T(8,128)(2,1)S(1)}, u32[]{:S(2)}, u32[]{:S(2)}) collective-permute-start(bf16[64,3584]{1,0:T(8,128)(2,1)S(1)} %get-tuple-element.36.refs_0_), channel_id=1, source_target_pairs={{0,1},{1,0},{2,3},{3,2},{4,5},{5,4},{6,7},{7,6},{8,9},{9,8},{10,11... | collective-permute-start | bytes 1376264 | tf_op jit(solution)/shard_map/ppermute | solution.py:154
  69.8 22.0 %collective-permute-start.2 = (bf16[64,3584]{1,0:T(8,128)(2,1)S(1)}, bf16[64,3584]{1,0:T(8,128)(2,1)S(1)}, u32[]{:S(2)}, u32[]{:S(2)}) collective-permute-start(bf16[64,3584]{1,0:T(8,128)(2,1)S(1)} %collective-permute-done.1.refs_2_), channel_id=1, source_target_pairs={{0,1},{1,0},{2,3},{3,2},{4,5},{5,4},{6,7},{7,6},{8,9},{9,8},{10,11... | collective-permute-start | bytes 1376264 | tf_op jit(solution)/shard_map/ppermute | solution.py:154
  69.9 32.7 %collective-permute-start.18 = (bf16[32,4096]{1,0:T(8,128)(2,1)S(1)}, bf16[32,4096]{1,0:T(8,128)(2,1)S(1)}, u32[]{:S(2)}, u32[]{:S(2)}) collective-permute-start(bf16[32,4096]{1,0:T(8,128)(2,1)S(1)} %get-tuple-element.17), channel_id=1, source_target_pairs={{0,1},{1,0},{2,3},{3,2},{4,5},{5,4},{6,7},{7,6},{8,9},{9,8},{10,11... | collective-permute-start | bytes 786440 | tf_op jit(solution)/shard_map/ppermute | solution.py:154
  80.5 24.3 %collective-permute-start.13 = (bf16[32,4096]{1,0:T(8,128)(2,1)S(1)}, bf16[32,4096]{1,0:T(8,128)(2,1)S(1)}, u32[]{:S(2)}, u32[]{:S(2)}) collective-permute-start(bf16[32,4096]{1,0:T(8,128)(2,1)S(1)} %get-tuple-element.15), channel_id=1, source_target_pairs={{0,1},{1,0},{2,3},{3,2},{4,5},{5,4},{6,7},{7,6},{8,9},{9,8},{10,11... | collective-permute-start | bytes 786440 | tf_op jit(solution)/shard_map/ppermute | solution.py:154
  80.6 0.8 copy-start.10
  91.4 11.3 %copy-start.6 = (f32[32,4096]{1,0:T(8,128)S(1)}, f32[32,4096]{1,0:T(8,128)}, u32[]{:S(2)}) copy-start(f32[32,4096]{1,0:T(8,128)} %get-tuple-element.16) | copy-start | bytes 1572868
  91.4 14.4 %collective-permute-start.8 = (bf16[32,4096]{1,0:T(8,128)(2,1)S(1)}, bf16[32,4096]{1,0:T(8,128)(2,1)S(1)}, u32[]{:S(2)}, u32[]{:S(2)}) collective-permute-start(bf16[32,4096]{1,0:T(8,128)(2,1)S(1)} %get-tuple-element.13), channel_id=1, source_target_pairs={{0,1},{1,0},{2,3},{3,2},{4,5},{5,4},{6,7},{7,6},{8,9},{9,8},{10,11... | collective-permute-start | bytes 786440 | tf_op jit(solution)/shard_map/ppermute | solution.py:154
  91.8 0.8 copy-start.11
  102.5 2.3 %copy-start.7 = (f32[32,4096]{1,0:T(8,128)S(1)}, f32[32,4096]{1,0:T(8,128)}, u32[]{:S(2)}) copy-start(f32[32,4096]{1,0:T(8,128)} %get-tuple-element.14) | copy-start | bytes 1572868
  102.5 3.3 %copy-start.8 = (f32[32,4096]{1,0:T(8,128)S(1)}, f32[32,4096]{1,0:T(8,128)}, u32[]{:S(2)}) copy-start(f32[32,4096]{1,0:T(8,128)} %get-tuple-element.12) | copy-start | bytes 1572868
  102.5 4.7 %collective-permute-start.3 = (bf16[32,4096]{1,0:T(8,128)(2,1)S(1)}, bf16[32,4096]{1,0:T(8,128)(2,1)S(1)}, u32[]{:S(2)}, u32[]{:S(2)}) collective-permute-start(bf16[32,4096]{1,0:T(8,128)(2,1)S(1)} %get-tuple-element.11), channel_id=1, source_target_pairs={{0,1},{1,0},{2,3},{3,2},{4,5},{5,4},{6,7},{7,6},{8,9},{9,8},{10,11... | collective-permute-start | bytes 786440 | tf_op jit(solution)/shard_map/ppermute | solution.py:154
  102.7 4.5 %copy-start.9 = (f32[32,4096]{1,0:T(8,128)S(1)}, f32[32,4096]{1,0:T(8,128)}, u32[]{:S(2)}) copy-start(f32[32,4096]{1,0:T(8,128)} %get-tuple-element.10) | copy-start | bytes 1572868
  102.7 6.4 %collective-permute-start.19 = (bf16[16,4096]{1,0:T(8,128)(2,1)S(1)}, bf16[16,4096]{1,0:T(8,128)(2,1)S(1)}, u32[]{:S(2)}, u32[]{:S(2)}) collective-permute-start(bf16[16,4096]{1,0:T(8,128)(2,1)S(1)} %select_convert_fusion), channel_id=1, source_target_pairs={{0,2},{1,3},{2,0},{3,1},{4,6},{5,7},{6,4},{7,5},{8,10},{9,11},{10,... | collective-permute-start | bytes 393224 | tf_op jit(solution)/shard_map/ppermute | solution.py:154
  104.9 12.4 %copy-start.5 = (bf16[64,4096]{1,0:T(8,128)(2,1)S(1)}, bf16[64,4096]{1,0:T(8,128)(2,1)}, u32[]{:S(2)}) copy-start(bf16[64,4096]{1,0:T(8,128)(2,1)} %param.10) | copy-start | bytes 1572868
  104.9 7.0 %collective-permute-start.14 = (bf16[16,4096]{1,0:T(8,128)(2,1)S(1)}, bf16[16,4096]{1,0:T(8,128)(2,1)S(1)}, u32[]{:S(2)}, u32[]{:S(2)}) collective-permute-start(bf16[16,4096]{1,0:T(8,128)(2,1)S(1)} %select_convert_fusion.1), channel_id=1, source_target_pairs={{0,2},{1,3},{2,0},{3,1},{4,6},{5,7},{6,4},{7,5},{8,10},{9,11},{10,... | collective-permute-start | bytes 393224 | tf_op jit(solution)/shard_map/ppermute | solution.py:154
  105.9 8.9 %collective-permute-start.9 = (bf16[16,4096]{1,0:T(8,128)(2,1)S(1)}, bf16[16,4096]{1,0:T(8,128)(2,1)S(1)}, u32[]{:S(2)}, u32[]{:S(2)}) collective-permute-start(bf16[16,4096]{1,0:T(8,128)(2,1)S(1)} %select_convert_fusion.2), channel_id=1, source_target_pairs={{0,2},{1,3},{2,0},{3,1},{4,6},{5,7},{6,4},{7,5},{8,10},{9,11},{10,... | collective-permute-start | bytes 393224 | tf_op jit(solution)/shard_map/ppermute | solution.py:154
  107.3 10.1 %collective-permute-start.4 = (bf16[16,4096]{1,0:T(8,128)(2,1)S(1)}, bf16[16,4096]{1,0:T(8,128)(2,1)S(1)}, u32[]{:S(2)}, u32[]{:S(2)}) collective-permute-start(bf16[16,4096]{1,0:T(8,128)(2,1)S(1)} %select_convert_fusion.3), channel_id=1, source_target_pairs={{0,2},{1,3},{2,0},{3,1},{4,6},{5,7},{6,4},{7,5},{8,10},{9,11},{10,... | collective-permute-start | bytes 393224 | tf_op jit(solution)/shard_map/ppermute | solution.py:154

commit v2 on v0

v2 whole, which is shorter than its diff:
```python
import functools
import math

import jax
import jax.numpy as jnp
import numpy as np
from jax import lax
from jax.experimental import pallas as pl
from jax.experimental.pallas import tpu as pltpu
from jax.sharding import PartitionSpec as P


ORDER = 28
DENSE = 896
TILE_ROWS = 16
VMEM = pl.BlockSpec(memory_space=pltpu.VMEM)
SMEM = pl.BlockSpec(memory_space=pltpu.SMEM)
HBM = pl.BlockSpec(memory_space=pltpu.HBM)
NIBBLES = 8


def chunk_rows(token_rows):
    quarter = token_rows // 4
    if quarter % TILE_ROWS:
        return [token_rows]
    return [quarter, 2 * quarter, quarter]


def paley_table():
    offsets = (np.arange(13)[None, :] - np.arange(13)[:, None]) % 13
    residues = np.zeros(13)
    residues[np.arange(1, 13) ** 2 % 13] = 1.0
    quadratic = np.where(offsets == 0, 0.0, np.where(residues[offsets] > 0, 1.0, -1.0))
    conference = np.zeros((14, 14))
    conference[0, 1:] = 1.0
    conference[1:, 0] = 1.0
    conference[1:, 1:] = quadratic
    upper = np.array([[1.0, 1.0], [1.0, -1.0]])
    lower = np.array([[1.0, -1.0], [-1.0, -1.0]])
    return np.kron(conference, upper) + np.kron(np.eye(14), lower)


def sylvester(order):
    table = np.ones((1, 1))
    while table.shape[0] < order:
        table = np.kron(np.array([[1.0, 1.0], [1.0, -1.0]]), table)
    return table


def cost(flops):
    return pl.CostEstimate(flops=flops, bytes_accessed=0, transcendentals=0)


def dense_table():
    return np.kron(sylvester(DENSE // ORDER), paley_table().T)


def bit_reversed(groups):
    bits = groups.bit_length() - 1
    return [sum(((d >> b) & 1) << (bits - 1 - b) for b in range(bits)) for d in range(groups)]


def sign_of(bit):
    return (1 - 2 * bit).astype(jnp.float32)


def prepare_kernel(groups, sizes, hidden_ref, signs_ref, first_ref, *rest_ref):
    token_rows = sum(sizes)
    flips = (2 * signs_ref[...] - 1).astype(jnp.float32)
    at, start = 0, 0
    for chunk, size in enumerate(sizes):
        for owner in bit_reversed(groups):
            rows = hidden_ref[pl.ds(owner * token_rows + start, size), :]
            value = (rows.astype(jnp.float32) * flips).astype(jnp.bfloat16)
            if chunk == 0:
                first_ref[pl.ds(at, size), :] = value
            else:
                rest_ref[0][pl.ds(at - groups * sizes[0], size), :] = value
            at += size
        start += size


def prepare(hidden, signs, groups, sizes):
    rows, width = hidden.shape
    size = groups * sizes[0]
    shapes = [jax.ShapeDtypeStruct((size, width), jnp.bfloat16)]
    if len(sizes) > 1:
        shapes.append(jax.ShapeDtypeStruct((rows - size, width), jnp.bfloat16))
    return pl.pallas_call(
        functools.partial(prepare_kernel, groups, sizes),
        out_shape=shapes,
        in_specs=[VMEM, VMEM],
        out_specs=[VMEM] * len(shapes),
        compiler_params=pltpu.CompilerParams(vmem_limit_bytes=12 * 2**20),
        cost_estimate=cost(rows * width),
        name="prepare",
    )(hidden, signs.reshape(1, width))


def rotate_blocks(mixed, table_ref):
    rows = mixed[0].shape[0]
    blocks = len(mixed)
    span = 1
    while span < blocks:
        for first in range(blocks):
            if not first & span:
                a, b = mixed[first], mixed[first + span]
                mixed[first], mixed[first + span] = a + b, a - b
        span *= 2
    out = []
    for block in range(blocks):
        high = mixed[block].astype(jnp.bfloat16)
        low = (mixed[block] - high.astype(jnp.float32)).astype(jnp.bfloat16)
        both = jnp.dot(
            jnp.concatenate([high, low], axis=0), table_ref[...], preferred_element_type=jnp.float32
        )
        out.append(both[:rows] + both[rows:])
    return out


def rotate_kernel(sizes, me_ref, own_ref, other_ref, table_ref, *out_refs):
    blocks = own_ref.shape[1] // DENSE
    sign = sign_of(me_ref[0] & 1)
    start = 0
    for chunk, size in enumerate(sizes):
        at = pl.ds(start, size)
        start += size
        mixed = []
        for block in range(blocks):
            columns = pl.ds(block * DENSE, DENSE)
            mixed.append(
                sign * own_ref[at, columns].astype(jnp.float32)
                + other_ref[at, columns].astype(jnp.float32)
            )
        for block, value in enumerate(rotate_blocks(mixed, table_ref)):
            columns = pl.ds(block * DENSE, DENSE)
            out_refs[2 * chunk][:, columns] = value
            out_refs[2 * chunk + 1][:, columns] = value.astype(jnp.bfloat16)


def rotate(own, other, me, table, sizes):
    rows, width = own.shape
    shapes = []
    for size in sizes:
        shapes.append(jax.ShapeDtypeStruct((size, width), jnp.float32))
        shapes.append(jax.ShapeDtypeStruct((size, width), jnp.bfloat16))
    return pl.pallas_call(
        functools.partial(rotate_kernel, sizes),
        out_shape=shapes,
        in_specs=[SMEM, VMEM, VMEM, VMEM],
        out_specs=[VMEM] * len(shapes),
        compiler_params=pltpu.CompilerParams(vmem_limit_bytes=20 * 2**20),
        cost_estimate=cost(4 * rows * width * DENSE),
        name="rotate",
    )(me, own, other, table)


def dequantize_kernel(group_size, packed_ref, scales_ref, weights_ref):
    words = packed_ref.shape[1]
    share = packed_ref.shape[0] // group_size
    for part in range(share):
        group = pl.program_id(0) * share + part
        rows = pl.ds(part * group_size, group_size)
        word = packed_ref[rows, :] ^ np.int32(-2004318072)
        for nibble in range(NIBBLES):
            codes = jnp.right_shift(jnp.left_shift(word, 28 - 4 * nibble), 28)
            scale = scales_ref[pl.ds(group, 1), pl.ds(nibble * words, words)]
            weights_ref[nibble, rows, :] = (codes * scale).astype(jnp.int8)


def dequantize(packed, group_scales):
    width, words = packed.shape
    group_count = group_scales.shape[0]
    group_size = width // group_count
    rows = group_size * (2 - group_count % 2)
    return pl.pallas_call(
        functools.partial(dequantize_kernel, group_size),
        grid=(width // rows,),
        out_shape=pltpu.HBM((NIBBLES, width, words), jnp.int8),
        in_specs=[
            pl.BlockSpec((rows, words), lambda i: (i, 0)),
            pl.BlockSpec(group_scales.shape, lambda i: (0, 0)),
        ],
        out_specs=pl.BlockSpec((NIBBLES, rows, words), lambda i: (0, i, 0)),
        compiler_params=pltpu.CompilerParams(vmem_limit_bytes=12 * 2**20),
        cost_estimate=cost(width * words * 8 * 1024),
        name="dequantize",
    )(packed, group_scales)


def project_kernel(count, unit, rotate_first, me_ref, *refs):
    parts = refs[:count]
    refs = refs[count:]
    if rotate_first:
        table_ref, refs = refs[0], refs[1:]
    weights_ref, keep_ref, send_ref, rotated_ref, buffer, sems = refs
    fetches = [
        pltpu.make_async_copy(weights_ref.at[n], buffer.at[n], sems.at[n]) for n in range(NIBBLES)
    ]
    for fetch in fetches:
        fetch.start()
    rows, width = parts[0].shape
    words = weights_ref.shape[2]
    blocks = width // DENSE
    me = me_ref[0]
    signs = []
    for r in range(count):
        bits = me & (me ^ r) if rotate_first else jnp.right_shift(me, 1) & (1 - r)
        parity = bits & 1
        for shift in range(1, max(count.bit_length() - 1, 1)):
            parity = parity ^ (jnp.right_shift(bits, shift) & 1)
        signs.append(sign_of(parity))
    mixed = []
    for block in range(blocks):
        columns = pl.ds(block * DENSE, DENSE)
        total = signs[0] * parts[0][:, columns].astype(jnp.float32)
        for r in range(1, count):
            total = total + signs[r] * parts[r][:, columns].astype(jnp.float32)
        mixed.append(total)
    if rotate_first:
        mixed = rotate_blocks(mixed, table_ref)
    for block in range(blocks):
        rotated_ref[:, pl.ds(block * DENSE, DENSE)] = (mixed[block] * unit).astype(jnp.bfloat16)
    half = rows // 2
    upper = me & 1 == 1

    @pl.loop(0, NIBBLES)
    def _(nibble):
        pltpu.make_async_copy(weights_ref.at[nibble], buffer.at[nibble], sems.at[nibble]).wait()
        product = jnp.dot(
            rotated_ref[...],
            buffer[nibble].astype(jnp.bfloat16),
            preferred_element_type=jnp.float32,
        )
        first, second = product[:half], product[half:]
        columns = pl.ds(pl.multiple_of(nibble * words, words), words)
        keep_ref[:, columns] = jnp.where(upper, second, first)
        send_ref[:, columns] = jnp.where(upper, first, second).astype(jnp.bfloat16)


def project(parts, me, table, weights, unit):
    count = len(parts)
    rows, width = parts[0].shape
    words = weights.shape[2]
    features = NIBBLES * words
    tables = [] if table is None else [table]
    return pl.pallas_call(
        functools.partial(project_kernel, count, unit, table is not None),
        out_shape=(
            jax.ShapeDtypeStruct((rows // 2, features), jnp.float32),
            jax.ShapeDtypeStruct((rows // 2, features), jnp.bfloat16),
        ),
        in_specs=[SMEM] + [VMEM] * (count + len(tables)) + [HBM],
        out_specs=(VMEM, VMEM),
        scratch_shapes=[
            pltpu.VMEM((rows, width), jnp.bfloat16),
            pltpu.VMEM(weights.shape, jnp.int8),
            pltpu.SemaphoreType.DMA((NIBBLES,)),
        ],
        compiler_params=pltpu.CompilerParams(vmem_limit_bytes=28 * 2**20),
        cost_estimate=cost(2 * 128 * width * features),
        name="project",
    )(me, *parts, *tables, pltpu.with_memory_space_constraint(weights, pltpu.HBM))


def finish_kernel(sizes, scale, *refs):
    chunks = len(sizes)
    keeps, gots = refs[:chunks], refs[chunks : 2 * chunks]
    residual_ref, new_ref, normed_ref = refs[2 * chunks :]
    start = 0
    for chunk, size in enumerate(sizes):
        rows = pl.ds(start, size)
        start += size
        branch = (keeps[chunk][...] + gots[chunk][...].astype(jnp.float32)) * scale
        fresh = (residual_ref[rows, :].astype(jnp.float32) + branch).astype(jnp.bfloat16)
        new_ref[rows, :] = fresh
        values = fresh.astype(jnp.float32)
        inverse = lax.rsqrt(jnp.mean(values * values, axis=1, keepdims=True) + 1e-05)
        normed_ref[rows, :] = (values * inverse).astype(jnp.bfloat16)


def finish(keeps, gots, residual, scale):
    chunks = len(keeps)
    shape = jax.ShapeDtypeStruct(residual.shape, jnp.bfloat16)
    return pl.pallas_call(
        functools.partial(finish_kernel, [keep.shape[0] for keep in keeps], scale),
        out_shape=(shape, shape),
        in_specs=[VMEM] * (2 * chunks + 1),
        out_specs=(VMEM, VMEM),
        compiler_params=pltpu.CompilerParams(vmem_limit_bytes=12 * 2**20),
        cost_estimate=cost(residual.size * 1024),
        name="finish",
    )(*keeps, *gots, residual)


def local(hidden, signs, packed, group_scales, residual):
    groups = lax.axis_size("tensor")
    bits = groups.bit_length() - 1
    me = lax.axis_index("tensor")
    where = me.reshape(1)
    total_width = hidden.shape[1] * groups
    sizes = chunk_rows(residual.shape[0])
    chunks = len(sizes)
    unit = 1.0 / math.sqrt(total_width)
    table = jnp.asarray(dense_table(), jnp.bfloat16)

    def swap(value, bit):
        return lax.ppermute(value, "tensor", [(i, i ^ (1 << bit)) for i in range(groups)])

    def bit_of(bit):
        return jnp.right_shift(me, bit) & 1

    own = prepare(hidden, signs, groups, sizes)
    have = {0: own[0]}
    for bit in reversed(range(bits)):
        have.update({r ^ (1 << bit): swap(value, bit) for r, value in list(have.items())})
    stages = [([have[r] for r in range(groups)], table)]
    if chunks > 1:
        other = swap(own[1], 0)
        pairs = rotate(own[1], other, where, table, [groups * size for size in sizes[1:]])
        for chunk in range(1, chunks):
            keep, send = pairs[2 * chunk - 2], pairs[2 * chunk - 1]
            for bit in range(1, bits):
                got = swap(send, bit)
                if bit < bits - 1:
                    keep = sign_of(bit_of(bit)) * keep + got.astype(jnp.float32)
                    send = keep.astype(jnp.bfloat16)
            stages.append(([keep, got], None))
    weights = dequantize(packed, group_scales)
    keeps, gots = [], []
    for parts, maybe_table in stages:
        value, send = project(parts, where, maybe_table, weights, unit)
        got = swap(send, 0)
        for bit in range(1, bits):
            value = value + got.astype(jnp.float32)
            half = value.shape[0] // 2
            upper = bit_of(bit) == 1
            send = jnp.where(upper, value[:half], value[half:]).astype(jnp.bfloat16)
            value = jnp.where(upper, value[half:], value[:half])
            got = swap(send, bit)
        keeps.append(value)
        gots.append(got)
    return finish(keeps, gots, residual, 1.0 / (45.0 * math.sqrt(total_width)))


def solution(mesh):
    return jax.shard_map(
        local,
        mesh=mesh,
        in_specs=(
            P("dp", "tensor"),
            P("tensor"),
            P("tensor", None),
            P("tensor", None),
            P(("dp", "tensor"), None),
        ),
        out_specs=(P(("dp", "tensor"), None), P(("dp", "tensor"), None)),
        check_vma=False,
    )
```

time: 433 us -> 116 us (0.27)
  local copies, waits for them, and re-layouts: 235 us -> 7.1 us
  other arithmetic: 54.8 us -> 0.4 us
  Pallas kernels: 0 us -> 43.2 us
  matrix products: 40.9 us -> 0 us
  waiting for transfers between devices: 78.3 us -> 52.9 us
  between operations: 14.1 us -> 0.79 us
    convert_element_type x2 -> x0, local copies, waits for them, and re-layouts: 216 us -> none  [the longest x1 215 us: local(): table = (outer[:, None, :, None] * inner[None, :, None, :]).reshape(local...]
    convert_element_type x5 -> x3, other arithmetic: 53.2 us -> 0.1 us  [local(): send = jnp.where(upper, value[:half], value[half:]).astype(jnp.bfloat16)]
    ppermute x0 -> x12, waiting for transfers between devices: none -> 52.9 us  [swap(): lax.ppermute(value, 'tensor', [(i, i ^ 1 << bit) for i in range(groups)])]
    reduce_scatter x1 -> x0, waiting for transfers between devices: 45.6 us -> none  [local(): lax.psum_scatter(jnp.dot(rotated, weights, preferred_element_type=jnp.flo...]
    pallas_call x0 -> x7, Pallas kernels: none -> 43.2 us  [the longest x3 24.1 us: project(): pl.pallas_call(functools.partial(project_kernel, count, unit, table is no...]
    dot_general x3 -> x0, matrix products: 40.9 us -> none  [the longest x1 15.6 us: local(): jnp.dot(rotated, weights, preferred_element_type=jnp.float32)]
    all_to_all x2 -> x0, waiting for transfers between devices: 32.6 us -> none  [the longest x1 18.6 us: local(): lax.all_to_all(partial_rot, 'tensor', split_axis=0, concat_axis=1, tiled=...]
    ppermute x0 -> x12, starting transfers between devices: none -> 11.7 us  [swap(): lax.ppermute(value, 'tensor', [(i, i ^ 1 << bit) for i in range(groups)])]
  transfers between devices with their start and end apart: 3 -> 12, of which waited for: 3 -> 6; matrix products, arithmetic and copies ran while one was open for 8% -> 0% of each run, Pallas kernels for 0% -> 24%
where the time goes in v2:
time: 116 us
  waiting for transfers between devices  52.9 us (46%)
  Pallas kernels  43.2 us (37%)
  starting transfers between devices  11.7 us (10%)
  local copies, waits for them, and re-layouts  7.1 us (6%)
    ppermute x12, waiting for transfers between devices, swap(): lax.ppermute(value, 'tensor', [(i, i ^ 1 << bit) for i in range(groups)])  52.9 us
    pallas_call x3, Pallas kernels, project(): pl.pallas_call(functools.partial(project_kernel, count, unit, table is no...  24.1 us
    ppermute x12, starting transfers between devices, swap(): lax.ppermute(value, 'tensor', [(i, i ^ 1 << bit) for i in range(groups)])  11.7 us
    pallas_call x1, Pallas kernels, dequantize(): pl.pallas_call(functools.partial(dequantize_kernel, group_size), grid=(wi...  11.2 us
    unnamed x14, local copies, waits for them, and re-layouts  6.37 us
    pallas_call x1, Pallas kernels, rotate(): pl.pallas_call(functools.partial(rotate_kernel, sizes), out_shape=shapes,...  5.29 us
  transfers between devices with their start and end apart: 12, of which 6 were waited for; matrix products, arithmetic and copies ran while one was open for 0% of the time, Pallas kernels for 24%

profile of v2, /device:TPU:0, one launch (start us, length us, event | category | flops | bytes accessed | tf_op | source)
XLA Modules:
  0.0 116.1 jit_solution(10011392727574747813)
XLA Ops:
  0.6 0.7 reshape.11.signs_ref
  1.4 0.0 copy-start
  1.4 1.5 %copy-done = bf16[256,3584]{1,0:T(8,128)(2,1)S(1)} copy-done((bf16[256,3584]{1,0:T(8,128)(2,1)S(1)}, bf16[256,3584]{1,0:T(8,128)(2,1)}, u32[]{:S(2)}) %copy-start) | copy-done | bytes 1835032
  2.9 0.0 copy-start.6
  2.9 1.3 %prepare.1 = (bf16[64,3584]{1,0:T(8,128)(2,1)S(1)}, bf16[192,3584]{1,0:T(8,128)(2,1)}) custom-call(bf16[256,3584]{1,0:T(8,128)(2,1)S(1)} %copy-done, s32[1,3584]{1,0:T(1,128)S(1)} %reshape.11.signs_ref), custom_call_target="tpu_custom_call" | custom-call | flops 917504 | tf_op jit(solution)/shard_map/prepare/pallas_call | solution.py:89
  4.2 3.0 %collective-permute-start.1 = (bf16[64,3584]{1,0:T(8,128)(2,1)S(1)}, bf16[64,3584]{1,0:T(8,128)(2,1)S(1)}, u32[]{:S(2)}, u32[]{:S(2)}) collective-permute-start(bf16[64,3584]{1,0:T(8,128)(2,1)S(1)} %get-tuple-element.14.refs_0_), channel_id=1, source_target_pairs={{0,2},{1,3},{2,0},{3,1},{4,6},{5,7},{6,4},{7,5},{8,10},{9,11},{10,... | collective-permute-start | bytes 1376264 | tf_op jit(solution)/shard_map/ppermute | solution.py:308
  7.2 0.0 collective-permute-start
  7.2 0.0 copy-start.1
  7.2 0.5 collective-permute-start.4
  7.7 10.0 %collective-permute-done.1.refs_2_ = bf16[64,3584]{1,0:T(8,128)(2,1)S(1)} collective-permute-done((bf16[64,3584]{1,0:T(8,128)(2,1)S(1)}, bf16[64,3584]{1,0:T(8,128)(2,1)S(1)}, u32[]{:S(2)}, u32[]{:S(2)}) %collective-permute-start.1) | collective-permute-done | bytes 458784 | tf_op jit(solution)/shard_map/ppermute | solution.py:308
  17.7 0.0 collective-permute-start.2
  17.7 0.0 copy-done.6
  17.7 0.0 copy-start.5
  17.7 3.1 %copy-done.5 = s32[3584,512]{1,0:T(8,128)S(1)} copy-done((s32[3584,512]{1,0:T(8,128)S(1)}, s32[3584,512]{1,0:T(8,128)}, u32[]{:S(2)}) %copy-start.5) | copy-done | bytes 7340056
  20.8 11.2 %dequantize.1.refs_5_.refs_2_ = s8[8,3584,512]{2,1,0:T(32,128)(4,1)} custom-call(s32[3584,512]{1,0:T(8,128)S(1)} %copy-done.5, s32[28,4096]{1,0:T(8,128)S(1)} %copy-done.6), custom_call_target="tpu_custom_call" | custom-call | flops 15032385536 | tf_op jit(solution)/shard_map/dequantize/pallas_call | solution.py:176
  32.0 0.0 collective-permute-done.refs_1_
  32.0 0.0 collective-permute-done.2.refs_3_
  32.0 0.0 copy-start.3
  32.0 0.8 copy-done.3
  32.8 0.0 copy-done.1
  32.8 0.0 copy-start.4
  32.8 1.0 copy-done.4
  33.8 9.7 %project.3 = (f32[32,4096]{1,0:T(8,128)S(1)}, bf16[32,4096]{1,0:T(8,128)(2,1)}) custom-call(s32[1]{0:T(128)} %bitcast.me_ref, bf16[64,3584]{1,0:T(8,128)(2,1)S(1)} %get-tuple-element.14.refs_0_, bf16[64,3584]{1,0:T(8,128)(2,1)S(1)} %collective-permute-done.refs_1_, bf16[64,3584]{1,0:T(8,128)(2,1)S(1)} %collective-permute-done.1.refs_2_, ...), custom_call_target="tpu_custom_call" | custom-call | flops 3758096384 | tf_op jit(solution)/shard_map/project/pallas_call | solution.py:247
  43.5 0.6 collective-permute-start.3
  44.1 1.4 %collective-permute-done.3 = bf16[32,4096]{1,0:T(8,128)(2,1)S(1)} collective-permute-done((bf16[32,4096]{1,0:T(8,128)(2,1)}, bf16[32,4096]{1,0:T(8,128)(2,1)S(1)}, u32[]{:S(2)}, u32[]{:S(2)}) %collective-permute-start.3) | collective-permute-done | bytes 262176 | tf_op jit(solution)/shard_map/ppermute | solution.py:308
  45.5 0.0 collective-permute-done.4.other_ref
  45.5 5.3 %rotate.1 = (f32[128,3584]{1,0:T(8,128)S(1)}, bf16[128,3584]{1,0:T(8,128)(2,1)S(1)}, f32[64,3584]{1,0:T(8,128)S(1)}, bf16[64,3584]{1,0:T(8,128)(2,1)S(1)}) custom-call(s32[1]{0:T(128)} %bitcast.me_ref, bf16[192,3584]{1,0:T(8,128)(2,1)} %get-tuple-element.17.own_ref, bf16[192,3584]{1,0:T(8,128)(2,1)} %collective-permute-done.4.other_ref, ...), custom_call_target="tpu_custom_call" | custom-call | flops 2466250752 | tf_op jit(solution)/shard_map/rotate/pallas_call | solution.py:147
  50.8 1.8 %collective-permute-start.7 = (bf16[64,3584]{1,0:T(8,128)(2,1)S(1)}, bf16[64,3584]{1,0:T(8,128)(2,1)S(1)}, u32[]{:S(2)}, u32[]{:S(2)}) collective-permute-start(bf16[64,3584]{1,0:T(8,128)(2,1)S(1)} %get-tuple-element.23), channel_id=1, source_target_pairs={{0,2},{1,3},{2,0},{3,1},{4,6},{5,7},{6,4},{7,5},{8,10},{9,11},{10,... | collective-permute-start | bytes 1376264 | tf_op jit(solution)/shard_map/ppermute | solution.py:308
  52.7 11.0 %collective-permute-done.7.refs_1_ = bf16[64,3584]{1,0:T(8,128)(2,1)S(1)} collective-permute-done((bf16[64,3584]{1,0:T(8,128)(2,1)S(1)}, bf16[64,3584]{1,0:T(8,128)(2,1)S(1)}, u32[]{:S(2)}, u32[]{:S(2)}) %collective-permute-start.7) | collective-permute-done | bytes 458784 | tf_op jit(solution)/shard_map/ppermute | solution.py:308
  63.7 7.6 %project.5 = (f32[32,4096]{1,0:T(8,128)S(1)}, bf16[32,4096]{1,0:T(8,128)(2,1)S(1)}) custom-call(s32[1]{0:T(128)} %bitcast.me_ref, f32[64,3584]{1,0:T(8,128)S(1)} %get-tuple-element.22.refs_0_, bf16[64,3584]{1,0:T(8,128)(2,1)S(1)} %collective-permute-done.7.refs_1_, s8[8,3584,512]{2,1,0:T(32,128)(4,1)} %dequantize.1.refs_5_.refs_2_), custom_call_target="tpu_custom_call" | custom-call | flops 3758096384 | tf_op jit(solution)/shard_map/project/pallas_call | solution.py:247
  71.3 0.1 collective-permute-start.8
  71.4 1.8 %collective-permute-start.9 = (bf16[16,4096]{1,0:T(8,128)(2,1)S(1)}, bf16[16,4096]{1,0:T(8,128)(2,1)S(1)}, u32[]{:S(2)}, u32[]{:S(2)}) collective-permute-start(bf16[16,4096]{1,0:T(8,128)(2,1)S(1)} %select_convert_fusion.2), channel_id=1, source_target_pairs={{0,2},{1,3},{2,0},{3,1},{4,6},{5,7},{6,4},{7,5},{8,10},{9,11},{10,... | collective-permute-start | bytes 393224 | tf_op jit(solution)/shard_map/ppermute | solution.py:308
  73.2 0.3 collective-permute-start.5
  73.5 0.0 collective-permute-done.8
  73.6 1.8 %collective-permute-start.11 = (bf16[16,4096]{1,0:T(8,128)(2,1)S(1)}, bf16[16,4096]{1,0:T(8,128)(2,1)S(1)}, u32[]{:S(2)}, u32[]{:S(2)}) collective-permute-start(bf16[16,4096]{1,0:T(8,128)(2,1)S(1)} %select_convert_fusion.1), channel_id=1, source_target_pairs={{0,2},{1,3},{2,0},{3,1},{4,6},{5,7},{6,4},{7,5},{8,10},{9,11},{10,... | collective-permute-start | bytes 393224 | tf_op jit(solution)/shard_map/ppermute | solution.py:308
  75.4 22.1 %collective-permute-done.5.refs_1_ = bf16[128,3584]{1,0:T(8,128)(2,1)S(1)} collective-permute-done((bf16[128,3584]{1,0:T(8,128)(2,1)S(1)}, bf16[128,3584]{1,0:T(8,128)(2,1)S(1)}, u32[]{:S(2)}, u32[]{:S(2)}) %collective-permute-start.5) | collective-permute-done | bytes 917536 | tf_op jit(solution)/shard_map/ppermute | solution.py:308
  97.5 6.8 %project.4 = (f32[64,4096]{1,0:T(8,128)S(1)}, bf16[64,4096]{1,0:T(8,128)(2,1)S(1)}) custom-call(s32[1]{0:T(128)} %bitcast.me_ref, f32[128,3584]{1,0:T(8,128)S(1)} %get-tuple-element.18.refs_0_, bf16[128,3584]{1,0:T(8,128)(2,1)S(1)} %collective-permute-done.5.refs_1_, s8[8,3584,512]{2,1,0:T(32,128)(4,1)} %dequantize.1.refs_5_.refs_2_), custom_call_target="tpu_custom_call" | custom-call | flops 3758096384 | tf_op jit(solution)/shard_map/project/pallas_call | solution.py:247
  104.4 0.1 collective-permute-start.6
  104.5 1.9 %collective-permute-done.6 = bf16[64,4096]{1,0:T(8,128)(2,1)S(1)} collective-permute-done((bf16[64,4096]{1,0:T(8,128)(2,1)S(1)}, bf16[64,4096]{1,0:T(8,128)(2,1)S(1)}, u32[]{:S(2)}, u32[]{:S(2)}) %collective-permute-start.6) | collective-permute-done | bytes 524320 | tf_op jit(solution)/shard_map/ppermute | solution.py:308
  106.3 0.1 convert_add_fusion
  106.4 0.0 copy-start.2
  106.4 0.1 select_convert_fusion
  106.5 1.8 %collective-permute-start.10 = (bf16[32,4096]{1,0:T(8,128)(2,1)S(1)}, bf16[32,4096]{1,0:T(8,128)(2,1)S(1)}, u32[]{:S(2)}, u32[]{:S(2)}) collective-permute-start(bf16[32,4096]{1,0:T(8,128)(2,1)S(1)} %select_convert_fusion), channel_id=1, source_target_pairs={{0,2},{1,3},{2,0},{3,1},{4,6},{5,7},{6,4},{7,5},{8,10},{9,11},{10,... | collective-permute-start | bytes 786440 | tf_op jit(solution)/shard_map/ppermute | solution.py:308
  108.3 0.1 slice_select_fusion.refs_1_
  108.4 0.0 collective-permute-done.9.refs_3_
  108.4 0.0 collective-permute-done.11.refs_5_
  108.4 6.5 %collective-permute-done.10.refs_4_ = bf16[32,4096]{1,0:T(8,128)(2,1)S(1)} collective-permute-done((bf16[32,4096]{1,0:T(8,128)(2,1)S(1)}, bf16[32,4096]{1,0:T(8,128)(2,1)S(1)}, u32[]{:S(2)}, u32[]{:S(2)}) %collective-permute-start.10) | collective-permute-done | bytes 262176 | tf_op jit(solution)/shard_map/ppermute | solution.py:308
  114.9 0.0 copy-done.2
  114.9 1.2 %finish.1 = (bf16[64,4096]{1,0:T(8,128)(2,1)}, bf16[64,4096]{1,0:T(8,128)(2,1)}) custom-call(f32[16,4096]{1,0:T(8,128)S(1)} %slice_select_fusion.2.refs_0_, f32[32,4096]{1,0:T(8,128)S(1)} %slice_select_fusion.refs_1_, f32[16,4096]{1,0:T(8,128)S(1)} %slice_select_fusion.1.refs_2_, bf16[16,4096]{1,0:T(8,128)(2,1)S(1)} %collective-permute-done.9.refs_3_, ...), custom_call_target="tpu_custom_call" | custom-call | flops 268435456 | tf_op jit(solution)/shard_map/finish/pallas_call | solution.py:285
  (6 shorter events, 0.2 us)
Async XLA Ops:
  1.4 1.5 %copy-start = (bf16[256,3584]{1,0:T(8,128)(2,1)S(1)}, bf16[256,3584]{1,0:T(8,128)(2,1)}, u32[]{:S(2)}) copy-start(bf16[256,3584]{1,0:T(8,128)(2,1)} %hidden_ref.1) | copy-start | bytes 5505028
  2.9 14.9 %copy-start.6 = (s32[28,4096]{1,0:T(8,128)S(1)}, s32[28,4096]{1,0:T(8,128)}, u32[]{:S(2)}) copy-start(s32[28,4096]{1,0:T(8,128)} %scales_ref.1) | copy-start | bytes 1376260
  4.2 13.5 %collective-permute-start.1 = (bf16[64,3584]{1,0:T(8,128)(2,1)S(1)}, bf16[64,3584]{1,0:T(8,128)(2,1)S(1)}, u32[]{:S(2)}, u32[]{:S(2)}) collective-permute-start(bf16[64,3584]{1,0:T(8,128)(2,1)S(1)} %get-tuple-element.14.refs_0_), channel_id=1, source_target_pairs={{0,2},{1,3},{2,0},{3,1},{4,6},{5,7},{6,4},{7,5},{8,10},{9,11},{10,... | collective-permute-start | bytes 1376264 | tf_op jit(solution)/shard_map/ppermute | solution.py:308
  7.2 24.8 %collective-permute-start = (bf16[64,3584]{1,0:T(8,128)(2,1)S(1)}, bf16[64,3584]{1,0:T(8,128)(2,1)S(1)}, u32[]{:S(2)}, u32[]{:S(2)}) collective-permute-start(bf16[64,3584]{1,0:T(8,128)(2,1)S(1)} %get-tuple-element.14.refs_0_), channel_id=1, source_target_pairs={{0,1},{1,0},{2,3},{3,2},{4,5},{5,4},{6,7},{7,6},{8,9},{9,8},{10,11... | collective-permute-start | bytes 1376264 | tf_op jit(solution)/shard_map/ppermute | solution.py:308
  7.2 25.6 %copy-start.1 = (bf16[896,896]{1,0:T(8,128)(2,1)S(1)}, bf16[896,896]{1,0:T(8,128)(2,1)}, u32[]{:S(2)}) copy-start(bf16[896,896]{1,0:T(8,128)(2,1)} %constant.8.clone.refs_4_.table_ref) | copy-start | bytes 4816900
  7.2 38.3 %collective-permute-start.4 = (bf16[192,3584]{1,0:T(8,128)(2,1)}, bf16[192,3584]{1,0:T(8,128)(2,1)}, u32[]{:S(2)}, u32[]{:S(2)}) collective-permute-start(bf16[192,3584]{1,0:T(8,128)(2,1)} %get-tuple-element.17.own_ref), channel_id=1, source_target_pairs={{0,1},{1,0},{2,3},{3,2},{4,5},{5,4},{6,7},{7,6},{8,9},{9,8},{10,11... | collective-permute-start | bytes 4128776 | tf_op jit(solution)/shard_map/ppermute | solution.py:308
  17.7 14.3 %collective-permute-start.2 = (bf16[64,3584]{1,0:T(8,128)(2,1)S(1)}, bf16[64,3584]{1,0:T(8,128)(2,1)S(1)}, u32[]{:S(2)}, u32[]{:S(2)}) collective-permute-start(bf16[64,3584]{1,0:T(8,128)(2,1)S(1)} %collective-permute-done.1.refs_2_), channel_id=1, source_target_pairs={{0,1},{1,0},{2,3},{3,2},{4,5},{5,4},{6,7},{7,6},{8,9},{9,8},{10,11... | collective-permute-start | bytes 1376264 | tf_op jit(solution)/shard_map/ppermute | solution.py:308
  17.7 3.1 %copy-start.5 = (s32[3584,512]{1,0:T(8,128)S(1)}, s32[3584,512]{1,0:T(8,128)}, u32[]{:S(2)}) copy-start(s32[3584,512]{1,0:T(8,128)} %packed_ref.1) | copy-start | bytes 22020100
  32.0 0.8 copy-start.3
  32.8 1.0 copy-start.4
  43.5 1.9 %collective-permute-start.3 = (bf16[32,4096]{1,0:T(8,128)(2,1)}, bf16[32,4096]{1,0:T(8,128)(2,1)S(1)}, u32[]{:S(2)}, u32[]{:S(2)}) collective-permute-start(bf16[32,4096]{1,0:T(8,128)(2,1)} %get-tuple-element.16), channel_id=1, source_target_pairs={{0,1},{1,0},{2,3},{3,2},{4,5},{5,4},{6,7},{7,6},{8,9},{9,8},{10,11... | collective-permute-start | bytes 786440 | tf_op jit(solution)/shard_map/ppermute | solution.py:308
  50.8 12.9 %collective-permute-start.7 = (bf16[64,3584]{1,0:T(8,128)(2,1)S(1)}, bf16[64,3584]{1,0:T(8,128)(2,1)S(1)}, u32[]{:S(2)}, u32[]{:S(2)}) collective-permute-start(bf16[64,3584]{1,0:T(8,128)(2,1)S(1)} %get-tuple-element.23), channel_id=1, source_target_pairs={{0,2},{1,3},{2,0},{3,1},{4,6},{5,7},{6,4},{7,5},{8,10},{9,11},{10,... | collective-permute-start | bytes 1376264 | tf_op jit(solution)/shard_map/ppermute | solution.py:308
  71.3 2.2 %collective-permute-start.8 = (bf16[32,4096]{1,0:T(8,128)(2,1)S(1)}, bf16[32,4096]{1,0:T(8,128)(2,1)S(1)}, u32[]{:S(2)}, u32[]{:S(2)}) collective-permute-start(bf16[32,4096]{1,0:T(8,128)(2,1)S(1)} %get-tuple-element.25), channel_id=1, source_target_pairs={{0,1},{1,0},{2,3},{3,2},{4,5},{5,4},{6,7},{7,6},{8,9},{9,8},{10,11... | collective-permute-start | bytes 786440 | tf_op jit(solution)/shard_map/ppermute | solution.py:308
  71.4 36.9 %collective-permute-start.9 = (bf16[16,4096]{1,0:T(8,128)(2,1)S(1)}, bf16[16,4096]{1,0:T(8,128)(2,1)S(1)}, u32[]{:S(2)}, u32[]{:S(2)}) collective-permute-start(bf16[16,4096]{1,0:T(8,128)(2,1)S(1)} %select_convert_fusion.2), channel_id=1, source_target_pairs={{0,2},{1,3},{2,0},{3,1},{4,6},{5,7},{6,4},{7,5},{8,10},{9,11},{10,... | collective-permute-start | bytes 393224 | tf_op jit(solution)/shard_map/ppermute | solution.py:308
  73.2 24.3 %collective-permute-start.5 = (bf16[128,3584]{1,0:T(8,128)(2,1)S(1)}, bf16[128,3584]{1,0:T(8,128)(2,1)S(1)}, u32[]{:S(2)}, u32[]{:S(2)}) collective-permute-start(bf16[128,3584]{1,0:T(8,128)(2,1)S(1)} %get-tuple-element.19), channel_id=1, source_target_pairs={{0,2},{1,3},{2,0},{3,1},{4,6},{5,7},{6,4},{7,5},{8,10},{9,11},{10,... | collective-permute-start | bytes 2752520 | tf_op jit(solution)/shard_map/ppermute | solution.py:308
  73.6 34.8 %collective-permute-start.11 = (bf16[16,4096]{1,0:T(8,128)(2,1)S(1)}, bf16[16,4096]{1,0:T(8,128)(2,1)S(1)}, u32[]{:S(2)}, u32[]{:S(2)}) collective-permute-start(bf16[16,4096]{1,0:T(8,128)(2,1)S(1)} %select_convert_fusion.1), channel_id=1, source_target_pairs={{0,2},{1,3},{2,0},{3,1},{4,6},{5,7},{6,4},{7,5},{8,10},{9,11},{10,... | collective-permute-start | bytes 393224 | tf_op jit(solution)/shard_map/ppermute | solution.py:308
  104.4 2.0 %collective-permute-start.6 = (bf16[64,4096]{1,0:T(8,128)(2,1)S(1)}, bf16[64,4096]{1,0:T(8,128)(2,1)S(1)}, u32[]{:S(2)}, u32[]{:S(2)}) collective-permute-start(bf16[64,4096]{1,0:T(8,128)(2,1)S(1)} %get-tuple-element.21), channel_id=1, source_target_pairs={{0,1},{1,0},{2,3},{3,2},{4,5},{5,4},{6,7},{7,6},{8,9},{9,8},{10,11... | collective-permute-start | bytes 1572872 | tf_op jit(solution)/shard_map/ppermute | solution.py:308
  106.4 8.5 %copy-start.2 = (bf16[64,4096]{1,0:T(8,128)(2,1)S(1)}, bf16[64,4096]{1,0:T(8,128)(2,1)}, u32[]{:S(2)}) copy-start(bf16[64,4096]{1,0:T(8,128)(2,1)} %refs_6_.1) | copy-start | bytes 1572868
  106.5 8.4 %collective-permute-start.10 = (bf16[32,4096]{1,0:T(8,128)(2,1)S(1)}, bf16[32,4096]{1,0:T(8,128)(2,1)S(1)}, u32[]{:S(2)}, u32[]{:S(2)}) collective-permute-start(bf16[32,4096]{1,0:T(8,128)(2,1)S(1)} %select_convert_fusion), channel_id=1, source_target_pairs={{0,2},{1,3},{2,0},{3,1},{4,6},{5,7},{6,4},{7,5},{8,10},{9,11},{10,... | collective-permute-start | bytes 786440 | tf_op jit(solution)/shard_map/ppermute | solution.py:308

commit v3 on v2

--- a/solution.py
+++ b/solution.py
@@ -16,6 +16,7 @@
 VMEM = pl.BlockSpec(memory_space=pltpu.VMEM)
 SMEM = pl.BlockSpec(memory_space=pltpu.SMEM)
 HBM = pl.BlockSpec(memory_space=pltpu.HBM)
+ANY = pl.BlockSpec(memory_space=pl.ANY)
 NIBBLES = 8
 
 
@@ -64,40 +65,54 @@
     return (1 - 2 * bit).astype(jnp.float32)
 
 
-def prepare_kernel(groups, sizes, hidden_ref, signs_ref, first_ref, *rest_ref):
-    token_rows = sum(sizes)
-    flips = (2 * signs_ref[...] - 1).astype(jnp.float32)
-    at, start = 0, 0
-    for chunk, size in enumerate(sizes):
+def prepare_kernel(groups, token_rows, places, hidden_ref, signs_ref, *refs):
+    out_refs, (staged, sems) = refs[:-2], refs[-2:]
+    width = hidden_ref.shape[1]
+    copies, at = [], 0
+    for start, size in places:
         for owner in bit_reversed(groups):
-            rows = hidden_ref[pl.ds(owner * token_rows + start, size), :]
-            value = (rows.astype(jnp.float32) * flips).astype(jnp.bfloat16)
-            if chunk == 0:
-                first_ref[pl.ds(at, size), :] = value
-            else:
-                rest_ref[0][pl.ds(at - groups * sizes[0], size), :] = value
+            copies.append(
+                pltpu.make_async_copy(
+                    hidden_ref.at[pl.ds(owner * token_rows + start, size), :],
+                    staged.at[pl.ds(at, size), :],
+                    sems.at[len(copies)],
+                )
+            )
+            copies[-1].start()
             at += size
-        start += size
-
-
-def prepare(hidden, signs, groups, sizes):
-    rows, width = hidden.shape
-    size = groups * sizes[0]
-    shapes = [jax.ShapeDtypeStruct((size, width), jnp.bfloat16)]
-    if len(sizes) > 1:
-        shapes.append(jax.ShapeDtypeStruct((rows - size, width), jnp.bfloat16))
+    flips = (2 * signs_ref[...] - 1).astype(jnp.float32).reshape(1, width)
+    at = 0
+    for index, copy in enumerate(copies):
+        size = places[index // groups][1]
+        copy.wait()
+        rows = pl.ds(at, size)
+        value = (staged[rows, :].astype(jnp.float32) * flips).astype(jnp.bfloat16)
+        for out_ref in out_refs:
+            out_ref[rows, :] = value
+        at += size
+
+
+def prepare(hidden, signs, groups, places, outputs):
+    width = hidden.shape[1]
+    rows = groups * sum(size for _, size in places)
+    count = groups * len(places)
     return pl.pallas_call(
-        functools.partial(prepare_kernel, groups, sizes),
-        out_shape=shapes,
-        in_specs=[VMEM, VMEM],
-        out_specs=[VMEM] * len(shapes),
+        functools.partial(prepare_kernel, groups, hidden.shape[0] // groups, places),
+        out_shape=[jax.ShapeDtypeStruct((rows, width), jnp.bfloat16)]
+        + [pltpu.HBM((rows, width), jnp.bfloat16)] * (outputs - 1),
+        in_specs=[HBM, VMEM],
+        out_specs=[VMEM] * outputs,
+        scratch_shapes=[
+            pltpu.VMEM((rows, width), jnp.bfloat16),
+            pltpu.SemaphoreType.DMA((count,)),
+        ],
         compiler_params=pltpu.CompilerParams(vmem_limit_bytes=12 * 2**20),
         cost_estimate=cost(rows * width),
         name="prepare",
-    )(hidden, signs.reshape(1, width))
-
-
-def rotate_blocks(mixed, table_ref):
+    )(pltpu.with_memory_space_constraint(hidden, pltpu.HBM), signs)
+
+
+def rotate_blocks(mixed, table_ref, stacked_ref):
     rows = mixed[0].shape[0]
     blocks = len(mixed)
     span = 1
@@ -107,35 +122,41 @@
                 a, b = mixed[first], mixed[first + span]
                 mixed[first], mixed[first + span] = a + b, a - b
         span *= 2
-    out = []
     for block in range(blocks):
-        high = mixed[block].astype(jnp.bfloat16)
-        low = (mixed[block] - high.astype(jnp.float32)).astype(jnp.bfloat16)
-        both = jnp.dot(
-            jnp.concatenate([high, low], axis=0), table_ref[...], preferred_element_type=jnp.float32
-        )
-        out.append(both[:rows] + both[rows:])
-    return out
-
-
-def rotate_kernel(sizes, me_ref, own_ref, other_ref, table_ref, *out_refs):
+        stacked_ref[pl.ds(block * rows, rows), :] = mixed[block].astype(jnp.bfloat16)
+    turned = jnp.dot(stacked_ref[...], table_ref[...], preferred_element_type=jnp.float32)
+    return [turned[block * rows : (block + 1) * rows] for block in range(blocks)]
+
+
+def rotate_kernel(sizes, me_ref, own_in, other_in, table_in, *refs):
+    out_refs, stacked_ref = refs[:-5], refs[-5]
+    own_ref, other_ref, table_ref, sems = refs[-4:]
+    moves = [
+        pltpu.make_async_copy(own_in, own_ref, sems.at[0]),
+        pltpu.make_async_copy(other_in, other_ref, sems.at[1]),
+        pltpu.make_async_copy(table_in, table_ref, sems.at[2]),
+    ]
+    for move in moves:
+        move.start()
+    for move in moves:
+        move.wait()
     blocks = own_ref.shape[1] // DENSE
     sign = sign_of(me_ref[0] & 1)
-    start = 0
-    for chunk, size in enumerate(sizes):
-        at = pl.ds(start, size)
-        start += size
-        mixed = []
-        for block in range(blocks):
-            columns = pl.ds(block * DENSE, DENSE)
-            mixed.append(
-                sign * own_ref[at, columns].astype(jnp.float32)
-                + other_ref[at, columns].astype(jnp.float32)
-            )
-        for block, value in enumerate(rotate_blocks(mixed, table_ref)):
-            columns = pl.ds(block * DENSE, DENSE)
-            out_refs[2 * chunk][:, columns] = value
-            out_refs[2 * chunk + 1][:, columns] = value.astype(jnp.bfloat16)
+    mixed = []
+    for block in range(blocks):
+        columns = pl.ds(block * DENSE, DENSE)
+        mixed.append(
+            sign * own_ref[:, columns].astype(jnp.float32)
+            + other_ref[:, columns].astype(jnp.float32)
+        )
+    for block, value in enumerate(rotate_blocks(mixed, table_ref, stacked_ref)):
+        columns = pl.ds(block * DENSE, DENSE)
+        start = 0
+        for chunk, size in enumerate(sizes):
+            piece = value[start : start + size]
+            start += size
+            out_refs[2 * chunk][:, columns] = piece
+            out_refs[2 * chunk + 1][:, columns] = piece.astype(jnp.bfloat16)
 
 
 def rotate(own, other, me, table, sizes):
@@ -147,12 +168,19 @@
     return pl.pallas_call(
         functools.partial(rotate_kernel, sizes),
         out_shape=shapes,
-        in_specs=[SMEM, VMEM, VMEM, VMEM],
+        in_specs=[SMEM, ANY, ANY, ANY],
         out_specs=[VMEM] * len(shapes),
+        scratch_shapes=[
+            pltpu.VMEM((rows * width // DENSE, DENSE), jnp.bfloat16),
+            pltpu.VMEM(own.shape, own.dtype),
+            pltpu.VMEM(other.shape, other.dtype),
+            pltpu.VMEM(table.shape, table.dtype),
+            pltpu.SemaphoreType.DMA((3,)),
+        ],
         compiler_params=pltpu.CompilerParams(vmem_limit_bytes=20 * 2**20),
-        cost_estimate=cost(4 * rows * width * DENSE),
+        cost_estimate=cost(2 * rows * width * DENSE),
         name="rotate",
-    )(me, own, other, table)
+    )(me, *[pltpu.with_memory_space_constraint(value, pltpu.HBM) for value in (own, other, table)])
 
 
 def dequantize_kernel(group_size, packed_ref, scales_ref, weights_ref):
@@ -185,20 +213,28 @@
         compiler_params=pltpu.CompilerParams(vmem_limit_bytes=12 * 2**20),
         cost_estimate=cost(width * words * 8 * 1024),
         name="dequantize",
-    )(packed, group_scales)
+    )(
+        pltpu.with_memory_space_constraint(packed, pltpu.HBM),
+        pltpu.with_memory_space_constraint(group_scales, pltpu.HBM),
+    )
 
 
 def project_kernel(count, unit, rotate_first, me_ref, *refs):
-    parts = refs[:count]
-    refs = refs[count:]
-    if rotate_first:
-        table_ref, refs = refs[0], refs[1:]
-    weights_ref, keep_ref, send_ref, rotated_ref, buffer, sems = refs
-    fetches = [
-        pltpu.make_async_copy(weights_ref.at[n], buffer.at[n], sems.at[n]) for n in range(NIBBLES)
+    total = count + rotate_first
+    parts, refs = refs[:total], refs[total:]
+    weights_ref, keep_ref, send_ref, rotated_ref, buffer, sems = refs[:6]
+    staged, staged_sems = refs[6 : 6 + total], refs[6 + total]
+    stacked_ref = refs[-1]
+    moves = [
+        pltpu.make_async_copy(parts[r], staged[r], staged_sems.at[r]) for r in range(total)
     ]
-    for fetch in fetches:
-        fetch.start()
+    for move in moves:
+        move.start()
+    for n in range(NIBBLES):
+        pltpu.make_async_copy(weights_ref.at[n], buffer.at[n], sems.at[n]).start()
+    for move in moves:
+        move.wait()
+    parts, table_ref = staged[:count], staged[-1]
     rows, width = parts[0].shape
     words = weights_ref.shape[2]
     blocks = width // DENSE
@@ -218,7 +254,7 @@
             total = total + signs[r] * parts[r][:, columns].astype(jnp.float32)
         mixed.append(total)
     if rotate_first:
-        mixed = rotate_blocks(mixed, table_ref)
+        mixed = rotate_blocks(mixed, table_ref, stacked_ref)
     for block in range(blocks):
         rotated_ref[:, pl.ds(block * DENSE, DENSE)] = (mixed[block] * unit).astype(jnp.bfloat16)
     half = rows // 2
@@ -243,24 +279,33 @@
     rows, width = parts[0].shape
     words = weights.shape[2]
     features = NIBBLES * words
-    tables = [] if table is None else [table]
+    operands = list(parts)
+    if table is not None:
+        operands.append(pltpu.with_memory_space_constraint(table, pltpu.HBM))
     return pl.pallas_call(
         functools.partial(project_kernel, count, unit, table is not None),
         out_shape=(
             jax.ShapeDtypeStruct((rows // 2, features), jnp.float32),
             jax.ShapeDtypeStruct((rows // 2, features), jnp.bfloat16),
         ),
-        in_specs=[SMEM] + [VMEM] * (count + len(tables)) + [HBM],
+        in_specs=[SMEM] + [ANY] * len(operands) + [HBM],
         out_specs=(VMEM, VMEM),
         scratch_shapes=[
             pltpu.VMEM((rows, width), jnp.bfloat16),
             pltpu.VMEM(weights.shape, jnp.int8),
             pltpu.SemaphoreType.DMA((NIBBLES,)),
+            *[pltpu.VMEM(operand.shape, operand.dtype) for operand in operands],
+            pltpu.SemaphoreType.DMA((len(operands),)),
+            pltpu.VMEM((rows * width // DENSE, DENSE), jnp.bfloat16),
         ],
         compiler_params=pltpu.CompilerParams(vmem_limit_bytes=28 * 2**20),
         cost_estimate=cost(2 * 128 * width * features),
         name="project",
-    )(me, *parts, *tables, pltpu.with_memory_space_constraint(weights, pltpu.HBM))
+    )(
+        me,
+        *operands,
+        pltpu.with_memory_space_constraint(weights, pltpu.HBM),
+    )
 
 
 def finish_kernel(sizes, scale, *refs):
@@ -310,14 +355,16 @@
     def bit_of(bit):
         return jnp.right_shift(me, bit) & 1
 
-    own = prepare(hidden, signs, groups, sizes)
-    have = {0: own[0]}
+    (first,) = prepare(hidden, signs, groups, [(0, sizes[0])], 1)
+    have = {0: first}
     for bit in reversed(range(bits)):
         have.update({r ^ (1 << bit): swap(value, bit) for r, value in list(have.items())})
     stages = [([have[r] for r in range(groups)], table)]
     if chunks > 1:
-        other = swap(own[1], 0)
-        pairs = rotate(own[1], other, where, table, [groups * size for size in sizes[1:]])
+        places = [(sum(sizes[:chunk]), sizes[chunk]) for chunk in range(1, chunks)]
+        sent, own = prepare(hidden, signs, groups, places, 2)
+        other = swap(sent, 0)
+        pairs = rotate(own, other, where, table, [groups * size for size in sizes[1:]])
         for chunk in range(1, chunks):
             keep, send = pairs[2 * chunk - 2], pairs[2 * chunk - 1]
             for bit in range(1, bits):

time: 116 us -> 117 us (level)
  Pallas kernels: 43.2 us -> 53.4 us
  local copies, waits for them, and re-layouts: 7.1 us -> 0.72 us
  waiting for transfers between devices: 52.9 us -> 49.6 us
    unnamed x14 -> x4, local copies, waits for them, and re-layouts: 6.37 us -> 0.72 us
    pallas_call x3, Pallas kernels: 24.1 us -> 28.7 us  [project(): pl.pallas_call(functools.partial(project_kernel, count, unit, table is no...]
    pallas_call x1, Pallas kernels: 11.2 us -> 15.2 us  [dequantize(): pl.pallas_call(functools.partial(dequantize_kernel, group_size), grid=(wi...]
    ppermute x12, waiting for transfers between devices: 52.9 us -> 49.6 us  [swap(): lax.ppermute(value, 'tensor', [(i, i ^ 1 << bit) for i in range(groups)])]
    pallas_call x1 -> x2, Pallas kernels: 1.34 us -> 4.11 us  [prepare(): pl.pallas_call(functools.partial(prepare_kernel, groups, hidden.shape[0]...]
  transfers between devices with their start and end apart: 12 -> 12, of which waited for: 6 -> 6; matrix products, arithmetic and copies ran while one was open for 0% -> 0% of each run, Pallas kernels for 24% -> 33%
where the time goes in v3:
time: 117 us
  Pallas kernels  53.4 us (46%)
  waiting for transfers between devices  49.6 us (42%)
  starting transfers between devices  11.9 us (10%)
    ppermute x12, waiting for transfers between devices, swap(): lax.ppermute(value, 'tensor', [(i, i ^ 1 << bit) for i in range(groups)])  49.6 us
    pallas_call x3, Pallas kernels, project(): pl.pallas_call(functools.partial(project_kernel, count, unit, table is no...  28.7 us
    pallas_call x1, Pallas kernels, dequantize(): pl.pallas_call(functools.partial(dequantize_kernel, group_size), grid=(wi...  15.2 us
    ppermute x12, starting transfers between devices, swap(): lax.ppermute(value, 'tensor', [(i, i ^ 1 << bit) for i in range(groups)])  11.9 us
    pallas_call x1, Pallas kernels, rotate(): pl.pallas_call(functools.partial(rotate_kernel, sizes), out_shape=shapes,...  4.2 us
    pallas_call x2, Pallas kernels, prepare(): pl.pallas_call(functools.partial(prepare_kernel, groups, hidden.shape[0]...  4.11 us
  transfers between devices with their start and end apart: 12, of which 6 were waited for; matrix products, arithmetic and copies ran while one was open for 0% of the time, Pallas kernels for 33%

profile of v3, /device:TPU:0, one launch (start us, length us, event | category | flops | bytes accessed | tf_op | source)
XLA Modules:
  0.0 116.8 jit_solution(6691450812292808356)
XLA Ops:
  0.6 0.0 copy-start.1
  0.6 0.7 copy-done.1
  1.3 1.1 prepare.2.refs_0_
  2.5 3.1 %collective-permute-start.1 = (bf16[64,3584]{1,0:T(8,128)(2,1)S(1)}, bf16[64,3584]{1,0:T(8,128)(2,1)S(1)}, u32[]{:S(2)}, u32[]{:S(2)}) collective-permute-start(bf16[64,3584]{1,0:T(8,128)(2,1)S(1)} %prepare.2.refs_0_), channel_id=1, source_target_pairs={{0,2},{1,3},{2,0},{3,1},{4,6},{5,7},{6,4},{7,5},{8,10},{9,11},{10,... | collective-permute-start | bytes 1376264 | tf_op jit(solution)/shard_map/ppermute | solution.py:353
  5.5 0.0 collective-permute-start
  5.5 3.0 %prepare.3 = (bf16[192,3584]{1,0:T(8,128)(2,1)}, bf16[192,3584]{1,0:T(8,128)(2,1)}) custom-call(bf16[256,3584]{1,0:T(8,128)(2,1)} %hidden_ref.3, s32[3584]{0:T(1024)S(1)} %copy-done.1), custom_call_target="tpu_custom_call" | custom-call | flops 688128 | tf_op jit(solution)/shard_map/prepare/pallas_call | solution.py:99
  8.5 0.6 collective-permute-start.4
  9.1 6.9 %collective-permute-done.1.refs_2_ = bf16[64,3584]{1,0:T(8,128)(2,1)S(1)} collective-permute-done((bf16[64,3584]{1,0:T(8,128)(2,1)S(1)}, bf16[64,3584]{1,0:T(8,128)(2,1)S(1)}, u32[]{:S(2)}, u32[]{:S(2)}) %collective-permute-start.1) | collective-permute-done | bytes 458784 | tf_op jit(solution)/shard_map/ppermute | solution.py:353
  16.1 0.0 collective-permute-start.2
  16.1 15.2 %dequantize.1.refs_5_.refs_2_ = s8[8,3584,512]{2,1,0:T(32,128)(4,1)} custom-call(s32[3584,512]{1,0:T(8,128)} %packed_ref.1, s32[28,4096]{1,0:T(8,128)} %scales_ref.1), custom_call_target="tpu_custom_call" | custom-call | flops 15032385536 | tf_op jit(solution)/shard_map/dequantize/pallas_call | solution.py:204
  31.3 0.0 collective-permute-done.refs_1_
  31.3 0.0 collective-permute-done.2.refs_3_
  31.3 13.4 %project.3 = (f32[32,4096]{1,0:T(8,128)S(1)}, bf16[32,4096]{1,0:T(8,128)(2,1)S(1)}) custom-call(s32[1]{0:T(128)} %bitcast.me_ref, bf16[64,3584]{1,0:T(8,128)(2,1)S(1)} %prepare.2.refs_0_, bf16[64,3584]{1,0:T(8,128)(2,1)S(1)} %collective-permute-done.refs_1_, bf16[64,3584]{1,0:T(8,128)(2,1)S(1)} %collective-permute-done.1.refs_2_, ...), custom_call_target="tpu_custom_call" | custom-call | flops 3758096384 | tf_op jit(solution)/shard_map/project/pallas_call | solution.py:285
  44.7 0.6 collective-permute-start.3
  45.2 1.2 collective-permute-done.3
  46.5 0.0 collective-permute-done.4.other_in
  46.5 4.2 %rotate.1 = (f32[128,3584]{1,0:T(8,128)S(1)}, bf16[128,3584]{1,0:T(8,128)(2,1)S(1)}, f32[64,3584]{1,0:T(8,128)S(1)}, bf16[64,3584]{1,0:T(8,128)(2,1)S(1)}) custom-call(s32[1]{0:T(128)} %bitcast.me_ref, bf16[192,3584]{1,0:T(8,128)(2,1)} %get-tuple-element.16.own_in, bf16[192,3584]{1,0:T(8,128)(2,1)} %collective-permute-done.4.other_in, ...), custom_call_target="tpu_custom_call" | custom-call | flops 1233125376 | tf_op jit(solution)/shard_map/rotate/pallas_call | solution.py:168
  50.7 1.8 %collective-permute-start.7 = (bf16[64,3584]{1,0:T(8,128)(2,1)S(1)}, bf16[64,3584]{1,0:T(8,128)(2,1)S(1)}, u32[]{:S(2)}, u32[]{:S(2)}) collective-permute-start(bf16[64,3584]{1,0:T(8,128)(2,1)S(1)} %get-tuple-element.23), channel_id=1, source_target_pairs={{0,2},{1,3},{2,0},{3,1},{4,6},{5,7},{6,4},{7,5},{8,10},{9,11},{10,... | collective-permute-start | bytes 1376264 | tf_op jit(solution)/shard_map/ppermute | solution.py:353
  52.5 11.0 %collective-permute-done.7.refs_1_ = bf16[64,3584]{1,0:T(8,128)(2,1)S(1)} collective-permute-done((bf16[64,3584]{1,0:T(8,128)(2,1)S(1)}, bf16[64,3584]{1,0:T(8,128)(2,1)S(1)}, u32[]{:S(2)}, u32[]{:S(2)}) %collective-permute-start.7) | collective-permute-done | bytes 458784 | tf_op jit(solution)/shard_map/ppermute | solution.py:353
  63.5 8.1 %project.5 = (f32[32,4096]{1,0:T(8,128)S(1)}, bf16[32,4096]{1,0:T(8,128)(2,1)S(1)}) custom-call(s32[1]{0:T(128)} %bitcast.me_ref, f32[64,3584]{1,0:T(8,128)S(1)} %get-tuple-element.22.refs_0_, bf16[64,3584]{1,0:T(8,128)(2,1)S(1)} %collective-permute-done.7.refs_1_, s8[8,3584,512]{2,1,0:T(32,128)(4,1)} %dequantize.1.refs_5_.refs_2_), custom_call_target="tpu_custom_call" | custom-call | flops 3758096384 | tf_op jit(solution)/shard_map/project/pallas_call | solution.py:285
  71.7 0.1 collective-permute-start.8
  71.8 1.8 %collective-permute-start.9 = (bf16[16,4096]{1,0:T(8,128)(2,1)S(1)}, bf16[16,4096]{1,0:T(8,128)(2,1)S(1)}, u32[]{:S(2)}, u32[]{:S(2)}) collective-permute-start(bf16[16,4096]{1,0:T(8,128)(2,1)S(1)} %select_convert_fusion.2), channel_id=1, source_target_pairs={{0,2},{1,3},{2,0},{3,1},{4,6},{5,7},{6,4},{7,5},{8,10},{9,11},{10,... | collective-permute-start | bytes 393224 | tf_op jit(solution)/shard_map/ppermute | solution.py:353
  73.6 0.3 collective-permute-start.5
  73.9 0.0 collective-permute-done.8
  74.0 1.8 %collective-permute-start.11 = (bf16[16,4096]{1,0:T(8,128)(2,1)S(1)}, bf16[16,4096]{1,0:T(8,128)(2,1)S(1)}, u32[]{:S(2)}, u32[]{:S(2)}) collective-permute-start(bf16[16,4096]{1,0:T(8,128)(2,1)S(1)} %select_convert_fusion.1), channel_id=1, source_target_pairs={{0,2},{1,3},{2,0},{3,1},{4,6},{5,7},{6,4},{7,5},{8,10},{9,11},{10,... | collective-permute-start | bytes 393224 | tf_op jit(solution)/shard_map/ppermute | solution.py:353
  75.8 22.1 %collective-permute-done.5.refs_1_ = bf16[128,3584]{1,0:T(8,128)(2,1)S(1)} collective-permute-done((bf16[128,3584]{1,0:T(8,128)(2,1)S(1)}, bf16[128,3584]{1,0:T(8,128)(2,1)S(1)}, u32[]{:S(2)}, u32[]{:S(2)}) %collective-permute-start.5) | collective-permute-done | bytes 917536 | tf_op jit(solution)/shard_map/ppermute | solution.py:353
  97.9 7.2 %project.4 = (f32[64,4096]{1,0:T(8,128)S(1)}, bf16[64,4096]{1,0:T(8,128)(2,1)S(1)}) custom-call(s32[1]{0:T(128)} %bitcast.me_ref, f32[128,3584]{1,0:T(8,128)S(1)} %get-tuple-element.18.refs_0_, bf16[128,3584]{1,0:T(8,128)(2,1)S(1)} %collective-permute-done.5.refs_1_, s8[8,3584,512]{2,1,0:T(32,128)(4,1)} %dequantize.1.refs_5_.refs_2_), custom_call_target="tpu_custom_call" | custom-call | flops 3758096384 | tf_op jit(solution)/shard_map/project/pallas_call | solution.py:285
  105.1 0.1 collective-permute-start.6
  105.2 1.9 %collective-permute-done.6 = bf16[64,4096]{1,0:T(8,128)(2,1)S(1)} collective-permute-done((bf16[64,4096]{1,0:T(8,128)(2,1)S(1)}, bf16[64,4096]{1,0:T(8,128)(2,1)S(1)}, u32[]{:S(2)}, u32[]{:S(2)}) %collective-permute-start.6) | collective-permute-done | bytes 524320 | tf_op jit(solution)/shard_map/ppermute | solution.py:353
  107.0 0.1 convert_add_fusion
  107.1 0.0 copy-start
  107.1 0.1 select_convert_fusion
  107.2 1.8 %collective-permute-start.10 = (bf16[32,4096]{1,0:T(8,128)(2,1)S(1)}, bf16[32,4096]{1,0:T(8,128)(2,1)S(1)}, u32[]{:S(2)}, u32[]{:S(2)}) collective-permute-start(bf16[32,4096]{1,0:T(8,128)(2,1)S(1)} %select_convert_fusion), channel_id=1, source_target_pairs={{0,2},{1,3},{2,0},{3,1},{4,6},{5,7},{6,4},{7,5},{8,10},{9,11},{10,... | collective-permute-start | bytes 786440 | tf_op jit(solution)/shard_map/ppermute | solution.py:353
  109.0 0.1 slice_select_fusion.refs_1_
  109.1 0.0 collective-permute-done.9.refs_3_
  109.1 0.0 collective-permute-done.11.refs_5_
  109.1 6.5 %collective-permute-done.10.refs_4_ = bf16[32,4096]{1,0:T(8,128)(2,1)S(1)} collective-permute-done((bf16[32,4096]{1,0:T(8,128)(2,1)S(1)}, bf16[32,4096]{1,0:T(8,128)(2,1)S(1)}, u32[]{:S(2)}, u32[]{:S(2)}) %collective-permute-start.10) | collective-permute-done | bytes 262176 | tf_op jit(solution)/shard_map/ppermute | solution.py:353
  115.6 0.0 copy-done
  115.6 1.2 %finish.1 = (bf16[64,4096]{1,0:T(8,128)(2,1)}, bf16[64,4096]{1,0:T(8,128)(2,1)}) custom-call(f32[16,4096]{1,0:T(8,128)S(1)} %slice_select_fusion.2.refs_0_, f32[32,4096]{1,0:T(8,128)S(1)} %slice_select_fusion.refs_1_, f32[16,4096]{1,0:T(8,128)S(1)} %slice_select_fusion.1.refs_2_, bf16[16,4096]{1,0:T(8,128)(2,1)S(1)} %collective-permute-done.9.refs_3_, ...), custom_call_target="tpu_custom_call" | custom-call | flops 268435456 | tf_op jit(solution)/shard_map/finish/pallas_call | solution.py:330
  (6 shorter events, 0.2 us)
Async XLA Ops:
  0.6 0.7 copy-start.1
  2.5 13.6 %collective-permute-start.1 = (bf16[64,3584]{1,0:T(8,128)(2,1)S(1)}, bf16[64,3584]{1,0:T(8,128)(2,1)S(1)}, u32[]{:S(2)}, u32[]{:S(2)}) collective-permute-start(bf16[64,3584]{1,0:T(8,128)(2,1)S(1)} %prepare.2.refs_0_), channel_id=1, source_target_pairs={{0,2},{1,3},{2,0},{3,1},{4,6},{5,7},{6,4},{7,5},{8,10},{9,11},{10,... | collective-permute-start | bytes 1376264 | tf_op jit(solution)/shard_map/ppermute | solution.py:353
  5.5 25.7 %collective-permute-start = (bf16[64,3584]{1,0:T(8,128)(2,1)S(1)}, bf16[64,3584]{1,0:T(8,128)(2,1)S(1)}, u32[]{:S(2)}, u32[]{:S(2)}) collective-permute-start(bf16[64,3584]{1,0:T(8,128)(2,1)S(1)} %prepare.2.refs_0_), channel_id=1, source_target_pairs={{0,1},{1,0},{2,3},{3,2},{4,5},{5,4},{6,7},{7,6},{8,9},{9,8},{10,11... | collective-permute-start | bytes 1376264 | tf_op jit(solution)/shard_map/ppermute | solution.py:353
  8.5 37.9 %collective-permute-start.4 = (bf16[192,3584]{1,0:T(8,128)(2,1)}, bf16[192,3584]{1,0:T(8,128)(2,1)}, u32[]{:S(2)}, u32[]{:S(2)}) collective-permute-start(bf16[192,3584]{1,0:T(8,128)(2,1)} %get-tuple-element.17), channel_id=1, source_target_pairs={{0,1},{1,0},{2,3},{3,2},{4,5},{5,4},{6,7},{7,6},{8,9},{9,8},{10,11... | collective-permute-start | bytes 4128776 | tf_op jit(solution)/shard_map/ppermute | solution.py:353
  16.1 15.2 %collective-permute-start.2 = (bf16[64,3584]{1,0:T(8,128)(2,1)S(1)}, bf16[64,3584]{1,0:T(8,128)(2,1)S(1)}, u32[]{:S(2)}, u32[]{:S(2)}) collective-permute-start(bf16[64,3584]{1,0:T(8,128)(2,1)S(1)} %collective-permute-done.1.refs_2_), channel_id=1, source_target_pairs={{0,1},{1,0},{2,3},{3,2},{4,5},{5,4},{6,7},{7,6},{8,9},{9,8},{10,11... | collective-permute-start | bytes 1376264 | tf_op jit(solution)/shard_map/ppermute | solution.py:353
  44.7 1.7 %collective-permute-start.3 = (bf16[32,4096]{1,0:T(8,128)(2,1)S(1)}, bf16[32,4096]{1,0:T(8,128)(2,1)S(1)}, u32[]{:S(2)}, u32[]{:S(2)}) collective-permute-start(bf16[32,4096]{1,0:T(8,128)(2,1)S(1)} %get-tuple-element.15), channel_id=1, source_target_pairs={{0,1},{1,0},{2,3},{3,2},{4,5},{5,4},{6,7},{7,6},{8,9},{9,8},{10,11... | collective-permute-start | bytes 786440 | tf_op jit(solution)/shard_map/ppermute | solution.py:353
  50.7 12.9 %collective-permute-start.7 = (bf16[64,3584]{1,0:T(8,128)(2,1)S(1)}, bf16[64,3584]{1,0:T(8,128)(2,1)S(1)}, u32[]{:S(2)}, u32[]{:S(2)}) collective-permute-start(bf16[64,3584]{1,0:T(8,128)(2,1)S(1)} %get-tuple-element.23), channel_id=1, source_target_pairs={{0,2},{1,3},{2,0},{3,1},{4,6},{5,7},{6,4},{7,5},{8,10},{9,11},{10,... | collective-permute-start | bytes 1376264 | tf_op jit(solution)/shard_map/ppermute | solution.py:353
  71.7 2.2 %collective-permute-start.8 = (bf16[32,4096]{1,0:T(8,128)(2,1)S(1)}, bf16[32,4096]{1,0:T(8,128)(2,1)S(1)}, u32[]{:S(2)}, u32[]{:S(2)}) collective-permute-start(bf16[32,4096]{1,0:T(8,128)(2,1)S(1)} %get-tuple-element.25), channel_id=1, source_target_pairs={{0,1},{1,0},{2,3},{3,2},{4,5},{5,4},{6,7},{7,6},{8,9},{9,8},{10,11... | collective-permute-start | bytes 786440 | tf_op jit(solution)/shard_map/ppermute | solution.py:353
  71.8 37.3 %collective-permute-start.9 = (bf16[16,4096]{1,0:T(8,128)(2,1)S(1)}, bf16[16,4096]{1,0:T(8,128)(2,1)S(1)}, u32[]{:S(2)}, u32[]{:S(2)}) collective-permute-start(bf16[16,4096]{1,0:T(8,128)(2,1)S(1)} %select_convert_fusion.2), channel_id=1, source_target_pairs={{0,2},{1,3},{2,0},{3,1},{4,6},{5,7},{6,4},{7,5},{8,10},{9,11},{10,... | collective-permute-start | bytes 393224 | tf_op jit(solution)/shard_map/ppermute | solution.py:353
  73.6 24.3 %collective-permute-start.5 = (bf16[128,3584]{1,0:T(8,128)(2,1)S(1)}, bf16[128,3584]{1,0:T(8,128)(2,1)S(1)}, u32[]{:S(2)}, u32[]{:S(2)}) collective-permute-start(bf16[128,3584]{1,0:T(8,128)(2,1)S(1)} %get-tuple-element.19), channel_id=1, source_target_pairs={{0,2},{1,3},{2,0},{3,1},{4,6},{5,7},{6,4},{7,5},{8,10},{9,11},{10,... | collective-permute-start | bytes 2752520 | tf_op jit(solution)/shard_map/ppermute | solution.py:353
  74.0 35.1 %collective-permute-start.11 = (bf16[16,4096]{1,0:T(8,128)(2,1)S(1)}, bf16[16,4096]{1,0:T(8,128)(2,1)S(1)}, u32[]{:S(2)}, u32[]{:S(2)}) collective-permute-start(bf16[16,4096]{1,0:T(8,128)(2,1)S(1)} %select_convert_fusion.1), channel_id=1, source_target_pairs={{0,2},{1,3},{2,0},{3,1},{4,6},{5,7},{6,4},{7,5},{8,10},{9,11},{10,... | collective-permute-start | bytes 393224 | tf_op jit(solution)/shard_map/ppermute | solution.py:353
  105.1 2.0 %collective-permute-start.6 = (bf16[64,4096]{1,0:T(8,128)(2,1)S(1)}, bf16[64,4096]{1,0:T(8,128)(2,1)S(1)}, u32[]{:S(2)}, u32[]{:S(2)}) collective-permute-start(bf16[64,4096]{1,0:T(8,128)(2,1)S(1)} %get-tuple-element.21), channel_id=1, source_target_pairs={{0,1},{1,0},{2,3},{3,2},{4,5},{5,4},{6,7},{7,6},{8,9},{9,8},{10,11... | collective-permute-start | bytes 1572872 | tf_op jit(solution)/shard_map/ppermute | solution.py:353
  107.1 8.5 %copy-start = (bf16[64,4096]{1,0:T(8,128)(2,1)S(1)}, bf16[64,4096]{1,0:T(8,128)(2,1)}, u32[]{:S(2)}) copy-start(bf16[64,4096]{1,0:T(8,128)(2,1)} %refs_6_.1) | copy-start | bytes 1572868
  107.2 8.4 %collective-permute-start.10 = (bf16[32,4096]{1,0:T(8,128)(2,1)S(1)}, bf16[32,4096]{1,0:T(8,128)(2,1)S(1)}, u32[]{:S(2)}, u32[]{:S(2)}) collective-permute-start(bf16[32,4096]{1,0:T(8,128)(2,1)S(1)} %select_convert_fusion), channel_id=1, source_target_pairs={{0,2},{1,3},{2,0},{3,1},{4,6},{5,7},{6,4},{7,5},{8,10},{9,11},{10,... | collective-permute-start | bytes 786440 | tf_op jit(solution)/shard_map/ppermute | solution.py:353

commit v4 on v3

v4 whole, which is shorter than its diff:
```python
import functools
import math

import jax
import jax.numpy as jnp
import numpy as np
from jax import lax
from jax.experimental import pallas as pl
from jax.experimental.pallas import tpu as pltpu
from jax.sharding import PartitionSpec as P


ORDER = 28
DENSE = 896
TILE_ROWS = 16
VMEM = pl.BlockSpec(memory_space=pltpu.VMEM)
SMEM = pl.BlockSpec(memory_space=pltpu.SMEM)
HBM = pl.BlockSpec(memory_space=pltpu.HBM)
BYTES = 4
GRANT = 16


def chunk_rows(token_rows):
    quarter = token_rows // 4
    if quarter % TILE_ROWS:
        return [token_rows]
    return [quarter, 2 * quarter, quarter]


def paley_table():
    offsets = (np.arange(13)[None, :] - np.arange(13)[:, None]) % 13
    residues = np.zeros(13)
    residues[np.arange(1, 13) ** 2 % 13] = 1.0
    quadratic = np.where(offsets == 0, 0.0, np.where(residues[offsets] > 0, 1.0, -1.0))
    conference = np.zeros((14, 14))
    conference[0, 1:] = 1.0
    conference[1:, 0] = 1.0
    conference[1:, 1:] = quadratic
    upper = np.array([[1.0, 1.0], [1.0, -1.0]])
    lower = np.array([[1.0, -1.0], [-1.0, -1.0]])
    return np.kron(conference, upper) + np.kron(np.eye(14), lower)


def sylvester(order):
    table = np.ones((1, 1))
    while table.shape[0] < order:
        table = np.kron(np.array([[1.0, 1.0], [1.0, -1.0]]), table)
    return table


def cost(flops):
    return pl.CostEstimate(flops=flops, bytes_accessed=0, transcendentals=0)


def dense_table():
    return np.kron(sylvester(DENSE // ORDER), paley_table().T)


def bit_reversed(groups):
    bits = groups.bit_length() - 1
    return [sum(((d >> b) & 1) << (bits - 1 - b) for b in range(bits)) for d in range(groups)]


def sign_of(bit):
    return (1 - 2 * bit).astype(jnp.float32)


def prepare_kernel(groups, token_rows, places, hidden_ref, signs_ref, out_ref, staged, sems):
    width = hidden_ref.shape[1]
    copies, at = [], 0
    for start, size in places:
        for owner in bit_reversed(groups):
            copies.append(
                pltpu.make_async_copy(
                    hidden_ref.at[pl.ds(owner * token_rows + start, size), :],
                    staged.at[pl.ds(at, size), :],
                    sems.at[len(copies)],
                )
            )
            copies[-1].start()
            at += size
    flips = (2 * signs_ref[...] - 1).astype(jnp.float32).reshape(1, width)
    at = 0
    for index, copy in enumerate(copies):
        size = places[index // groups][1]
        copy.wait()
        rows = pl.ds(at, size)
        out_ref[rows, :] = (staged[rows, :].astype(jnp.float32) * flips).astype(jnp.bfloat16)
        at += size


def prepare(hidden, signs, groups, places):
    width = hidden.shape[1]
    rows = groups * sum(size for _, size in places)
    count = groups * len(places)
    return pl.pallas_call(
        functools.partial(prepare_kernel, groups, hidden.shape[0] // groups, places),
        out_shape=jax.ShapeDtypeStruct((rows, width), jnp.bfloat16),
        in_specs=[HBM, VMEM],
        out_specs=VMEM,
        scratch_shapes=[
            pltpu.VMEM((rows, width), jnp.bfloat16),
            pltpu.SemaphoreType.DMA((count,)),
        ],
        compiler_params=pltpu.CompilerParams(vmem_limit_bytes=12 * 2**20),
        cost_estimate=cost(rows * width),
        name="prepare",
    )(pltpu.with_memory_space_constraint(hidden, pltpu.HBM), signs)


def rotate_blocks(mixed, table_ref, stacked_ref):
    rows = mixed[0].shape[0]
    blocks = len(mixed)
    span = 1
    while span < blocks:
        for first in range(blocks):
            if not first & span:
                a, b = mixed[first], mixed[first + span]
                mixed[first], mixed[first + span] = a + b, a - b
        span *= 2
    for block in range(blocks):
        stacked_ref[pl.ds(block * rows, rows), :] = mixed[block].astype(jnp.bfloat16)
    turned = jnp.dot(stacked_ref[...], table_ref[...], preferred_element_type=jnp.float32)
    return [turned[block * rows : (block + 1) * rows] for block in range(blocks)]


def rotate_kernel(groups, places, me_ref, hidden_ref, signs_ref, other_ref, table_ref, *refs):
    out_refs, stacked_ref = refs[:-1], refs[-1]
    width = hidden_ref.shape[1]
    token_rows = hidden_ref.shape[0] // groups
    flips = (2 * signs_ref[...] - 1).astype(jnp.float32).reshape(1, width)
    flips = flips * sign_of(me_ref[0] & 1)
    mixed = []
    for block in range(width // DENSE):
        columns = pl.ds(block * DENSE, DENSE)
        own = [
            hidden_ref[pl.ds(owner * token_rows + start, size), columns]
            for start, size in places
            for owner in bit_reversed(groups)
        ]
        own = jnp.concatenate(own, axis=0).astype(jnp.float32)
        turned = own * flips[:, block * DENSE : (block + 1) * DENSE]
        mixed.append(turned + other_ref[:, columns].astype(jnp.float32))
    for block, value in enumerate(rotate_blocks(mixed, table_ref, stacked_ref)):
        columns = pl.ds(block * DENSE, DENSE)
        start = 0
        for chunk, (_, size) in enumerate(places):
            piece = value[start : start + groups * size]
            start += groups * size
            out_refs[2 * chunk][:, columns] = piece
            out_refs[2 * chunk + 1][:, columns] = piece.astype(jnp.bfloat16)


def rotate(hidden, signs, other, me, table, groups, places):
    rows, width = other.shape
    shapes = []
    for _, size in places:
        shapes.append(jax.ShapeDtypeStruct((groups * size, width), jnp.float32))
        shapes.append(jax.ShapeDtypeStruct((groups * size, width), jnp.bfloat16))
    return pl.pallas_call(
        functools.partial(rotate_kernel, groups, places),
        out_shape=shapes,
        in_specs=[SMEM, VMEM, VMEM, VMEM, VMEM],
        out_specs=[VMEM] * len(shapes),
        scratch_shapes=[pltpu.VMEM((rows * width // DENSE, DENSE), jnp.bfloat16)],
        compiler_params=pltpu.CompilerParams(vmem_limit_bytes=20 * 2**20),
        cost_estimate=cost(2 * rows * width * DENSE),
        name="rotate",
    )(me, hidden, signs, other, table)


def dequantize_kernel(packed_ref, bytes_ref):
    word = packed_ref[...] ^ np.int32(-2139062144)
    for place in range(BYTES):
        moved = jnp.right_shift(jnp.left_shift(word, 24 - 8 * place), 24)
        bytes_ref[place, :, :] = moved.astype(jnp.int8)


def dequantize(packed, group_count):
    width, words = packed.shape
    rows = width // group_count * 7 if group_count % 7 == 0 else width // group_count
    return pl.pallas_call(
        dequantize_kernel,
        grid=(width // rows,),
        out_shape=jax.ShapeDtypeStruct((BYTES, width, words), jnp.int8),
        in_specs=[pl.BlockSpec((rows, words), lambda i: (i, 0))],
        out_specs=pl.BlockSpec((BYTES, rows, words), lambda i: (0, i, 0)),
        compiler_params=pltpu.CompilerParams(vmem_limit_bytes=16 * 2**20),
        cost_estimate=cost(width * words * 8 * 512),
        name="dequantize",
    )(pltpu.with_memory_space_constraint(packed, pltpu.HBM))


def project_kernel(count, unit, rotate_first, me_ref, *refs):
    parts, refs = refs[:count], refs[count:]
    if rotate_first:
        table_ref, refs = refs[0], refs[1:]
    scales_ref, bytes_ref, keep_ref, send_ref, rotated_ref, stacked_ref = refs
    rows, width = parts[0].shape
    words = bytes_ref.shape[2]
    group_count = scales_ref.shape[0]
    group_size = width // group_count
    blocks = width // DENSE
    me = me_ref[0]
    signs = []
    for r in range(count):
        bits = me & (me ^ r) if rotate_first else jnp.right_shift(me, 1) & (1 - r)
        parity = bits & 1
        for shift in range(1, max(count.bit_length() - 1, 1)):
            parity = parity ^ (jnp.right_shift(bits, shift) & 1)
        signs.append(sign_of(parity))
    mixed = []
    for block in range(blocks):
        columns = pl.ds(block * DENSE, DENSE)
        total = signs[0] * parts[0][:, columns].astype(jnp.float32)
        for r in range(1, count):
            total = total + signs[r] * parts[r][:, columns].astype(jnp.float32)
        mixed.append(total)
    if rotate_first:
        mixed = rotate_blocks(mixed, table_ref, stacked_ref)
    for block in range(blocks):
        rotated_ref[:, pl.ds(block * DENSE, DENSE)] = (mixed[block] * unit).astype(jnp.bfloat16)
    half = rows // 2
    upper = me & 1 == 1

    @pl.loop(0, BYTES)
    def _(place):
        spans = [
            pl.ds(pl.multiple_of((2 * place + side) * words, words), words) for side in range(2)
        ]
        sides = [[], []]
        for group in range(group_count):
            both = bytes_ref[place, group * group_size : (group + 1) * group_size, :]
            high = (both & jnp.int8(-16)).astype(jnp.bfloat16)
            low = both.astype(jnp.bfloat16) - high - jnp.bfloat16(8)
            sides[0].append(low * scales_ref[group : group + 1, spans[0]])
            sides[1].append(high * scales_ref[group : group + 1, spans[1]])
        for columns, weights in zip(spans, sides):
            product = jnp.dot(
                rotated_ref[...],
                jnp.concatenate(weights, axis=0),
                preferred_element_type=jnp.float32,
            )
            first, second = product[:half], product[half:]
            keep_ref[:, columns] = jnp.where(upper, second, first)
            send_ref[:, columns] = jnp.where(upper, first, second).astype(jnp.bfloat16)


def project(parts, me, table, scales, weights, unit):
    count = len(parts)
    rows, width = parts[0].shape
    features = scales.shape[1]
    tables = [] if table is None else [table]
    return pl.pallas_call(
        functools.partial(project_kernel, count, unit, table is not None),
        out_shape=(
            jax.ShapeDtypeStruct((rows // 2, features), jnp.float32),
            jax.ShapeDtypeStruct((rows // 2, features), jnp.bfloat16),
        ),
        in_specs=[SMEM] + [VMEM] * (count + len(tables) + 2),
        out_specs=(VMEM, VMEM),
        scratch_shapes=[
            pltpu.VMEM((rows, width), jnp.bfloat16),
            pltpu.VMEM((rows * width // DENSE, DENSE), jnp.bfloat16),
        ],
        compiler_params=pltpu.CompilerParams(vmem_limit_bytes=GRANT * 2**20),
        cost_estimate=cost(2 * 128 * width * features),
        name="project",
    )(me, *parts, *tables, scales, weights)


def finish_kernel(sizes, scale, *refs):
    chunks = len(sizes)
    keeps, gots = refs[:chunks], refs[chunks : 2 * chunks]
    residual_ref, new_ref, normed_ref = refs[2 * chunks :]
    start = 0
    for chunk, size in enumerate(sizes):
        rows = pl.ds(start, size)
        start += size
        branch = (keeps[chunk][...] + gots[chunk][...].astype(jnp.float32)) * scale
        fresh = (residual_ref[rows, :].astype(jnp.float32) + branch).astype(jnp.bfloat16)
        new_ref[rows, :] = fresh
        values = fresh.astype(jnp.float32)
        inverse = lax.rsqrt(jnp.mean(values * values, axis=1, keepdims=True) + 1e-05)
        normed_ref[rows, :] = (values * inverse).astype(jnp.bfloat16)


def finish(keeps, gots, residual, scale):
    chunks = len(keeps)
    shape = jax.ShapeDtypeStruct(residual.shape, jnp.bfloat16)
    return pl.pallas_call(
        functools.partial(finish_kernel, [keep.shape[0] for keep in keeps], scale),
        out_shape=(shape, shape),
        in_specs=[VMEM] * (2 * chunks + 1),
        out_specs=(VMEM, VMEM),
        compiler_params=pltpu.CompilerParams(vmem_limit_bytes=12 * 2**20),
        cost_estimate=cost(residual.size * 1024),
        name="finish",
    )(*keeps, *gots, residual)


def local(hidden, signs, packed, group_scales, residual):
    groups = lax.axis_size("tensor")
    bits = groups.bit_length() - 1
    me = lax.axis_index("tensor")
    where = me.reshape(1)
    total_width = hidden.shape[1] * groups
    sizes = chunk_rows(residual.shape[0])
    chunks = len(sizes)
    unit = 1.0 / math.sqrt(total_width)
    table = jnp.asarray(dense_table(), jnp.bfloat16)

    def swap(value, bit):
        return lax.ppermute(value, "tensor", [(i, i ^ (1 << bit)) for i in range(groups)])

    def bit_of(bit):
        return jnp.right_shift(me, bit) & 1

    first = prepare(hidden, signs, groups, [(0, sizes[0])])
    have = {0: first}
    for bit in reversed(range(bits)):
        have.update({r ^ (1 << bit): swap(value, bit) for r, value in list(have.items())})
    stages = [([have[r] for r in range(groups)], table)]
    if chunks > 1:
        places = [(sum(sizes[:chunk]), sizes[chunk]) for chunk in range(1, chunks)]
        sent = prepare(hidden, signs, groups, places)
        other = swap(sent, 0)
        pairs = rotate(hidden, signs, other, where, table, groups, places)
        for chunk in range(1, chunks):
            keep, send = pairs[2 * chunk - 2], pairs[2 * chunk - 1]
            for bit in range(1, bits):
                got = swap(send, bit)
                if bit < bits - 1:
                    keep = sign_of(bit_of(bit)) * keep + got.astype(jnp.float32)
                    send = keep.astype(jnp.bfloat16)
            stages.append(([keep, got], None))
    weights = dequantize(packed, group_scales.shape[0])
    words = packed.shape[1]
    side = jnp.arange(group_scales.shape[1]) // words % 2
    scales = group_scales.astype(jnp.float32) * jnp.where(side == 1, 0.0625, 1.0)[None, :]
    scales = scales.astype(jnp.bfloat16)
    keeps, gots = [], []
    for parts, maybe_table in stages:
        value, send = project(parts, where, maybe_table, scales, weights, unit)
        got = swap(send, 0)
        for bit in range(1, bits):
            value = value + got.astype(jnp.float32)
            half = value.shape[0] // 2
            upper = bit_of(bit) == 1
            send = jnp.where(upper, value[:half], value[half:]).astype(jnp.bfloat16)
            value = jnp.where(upper, value[half:], value[:half])
            got = swap(send, bit)
        keeps.append(value)
        gots.append(got)
    return finish(keeps, gots, residual, 1.0 / (45.0 * math.sqrt(total_width)))


def solution(mesh):
    return jax.shard_map(
        local,
        mesh=mesh,
        in_specs=(
            P("dp", "tensor"),
            P("tensor"),
            P("tensor", None),
            P("tensor", None),
            P(("dp", "tensor"), None),
        ),
        out_specs=(P(("dp", "tensor"), None), P(("dp", "tensor"), None)),
        check_vma=False,
    )
```

time: 117 us -> 111 us (0.949)
  Pallas kernels: 53.4 us -> 35.7 us
  local copies, waits for them, and re-layouts: 0.72 us -> 10.4 us
  other arithmetic: 0.4 us -> 1.57 us
    pallas_call x2, Pallas kernels: 19.4 us -> 9.05 us  [the longest x1 5.74 us: dequantize(): pl.pallas_call(dequantize_kernel, grid=(width // rows,), out_shape=jax.Sh...]
    unnamed x4 -> x36, local copies, waits for them, and re-layouts: 0.72 us -> 10.4 us
    pallas_call x3, Pallas kernels: 28.7 us -> 21.6 us  [project(): pl.pallas_call(functools.partial(project_kernel, count, unit, table is no...]
  transfers between devices with their start and end apart: 12 -> 12, of which waited for: 6 -> 6; matrix products, arithmetic and copies ran while one was open for 0% -> 1% of each run, Pallas kernels for 33% -> 21%
where the time goes in v4:
time: 111 us; the launch traced here: 110 us
  waiting for transfers between devices  50.2 us (45%)
  Pallas kernels  35.7 us (32%)
  starting transfers between devices  11.6 us (10%)
  local copies, waits for them, and re-layouts  10.4 us (9%)
  other arithmetic  1.57 us (1%)
    ppermute x12, waiting for transfers between devices, swap(): lax.ppermute(value, 'tensor', [(i, i ^ 1 << bit) for i in range(groups)])  50.2 us
    pallas_call x3, Pallas kernels, project(): pl.pallas_call(functools.partial(project_kernel, count, unit, table is no...  21.6 us
    ppermute x12, starting transfers between devices, swap(): lax.ppermute(value, 'tensor', [(i, i ^ 1 << bit) for i in range(groups)])  11.6 us
    unnamed x36, local copies, waits for them, and re-layouts  10.4 us
    pallas_call x1, Pallas kernels, dequantize(): pl.pallas_call(dequantize_kernel, grid=(width // rows,), out_shape=jax.Sh...  5.74 us
    pallas_call x2, Pallas kernels, prepare(): pl.pallas_call(functools.partial(prepare_kernel, groups, hidden.shape[0]...  3.8 us
    pallas_call x1, Pallas kernels, rotate(): pl.pallas_call(functools.partial(rotate_kernel, groups, places), out_shap...  3.3 us
  transfers between devices with their start and end apart: 12, of which 6 were waited for; matrix products, arithmetic and copies ran while one was open for 1% of the time, Pallas kernels for 21%

profile of v4, /device:TPU:0, one launch (start us, length us, event | category | flops | bytes accessed | tf_op | source)
XLA Modules:
  0.0 110.3 jit_solution(11552882756314448294)
XLA Ops:
  0.6 0.0 copy-start.8
  0.6 0.7 copy-done.8
  1.4 1.1 %prepare.2.refs_0_ = bf16[64,3584]{1,0:T(8,128)(2,1)S(1)} custom-call(bf16[256,3584]{1,0:T(8,128)(2,1)} %hidden_ref.5, s32[3584]{0:T(1024)S(1)} %copy-done.8), custom_call_target="tpu_custom_call" | custom-call | flops 229376 | tf_op jit(solution)/shard_map/prepare/pallas_call | solution.py:96
  2.5 0.0 copy-start.4
  2.5 0.0 copy-start.17
  2.5 3.1 %collective-permute-start.1 = (bf16[64,3584]{1,0:T(8,128)(2,1)S(1)}, bf16[64,3584]{1,0:T(8,128)(2,1)S(1)}, u32[]{:S(2)}, u32[]{:S(2)}) collective-permute-start(bf16[64,3584]{1,0:T(8,128)(2,1)S(1)} %prepare.2.refs_0_), channel_id=1, source_target_pairs={{0,2},{1,3},{2,0},{3,1},{4,6},{5,7},{6,4},{7,5},{8,10},{9,11},{10,... | collective-permute-start | bytes 1376264 | tf_op jit(solution)/shard_map/ppermute | solution.py:314
  5.6 0.0 collective-permute-start
  5.6 0.0 copy-done.9
  5.6 2.7 %prepare.3 = bf16[192,3584]{1,0:T(8,128)(2,1)} custom-call(bf16[256,3584]{1,0:T(8,128)(2,1)} %hidden_ref.5, s32[3584]{0:T(1024)S(1)} %copy-done.9), custom_call_target="tpu_custom_call" | custom-call | flops 688128 | tf_op jit(solution)/shard_map/prepare/pallas_call | solution.py:96
  8.3 0.6 collective-permute-start.4
  8.8 0.0 copy-done.17
  8.9 0.0 copy-done.4
  8.9 0.0 copy-start.6
  8.9 0.0 copy-start.1
  8.9 7.2 %collective-permute-done.1.refs_2_ = bf16[64,3584]{1,0:T(8,128)(2,1)S(1)} collective-permute-done((bf16[64,3584]{1,0:T(8,128)(2,1)S(1)}, bf16[64,3584]{1,0:T(8,128)(2,1)S(1)}, u32[]{:S(2)}, u32[]{:S(2)}) %collective-permute-start.1) | collective-permute-done | bytes 458784 | tf_op jit(solution)/shard_map/ppermute | solution.py:314
  16.1 0.0 collective-permute-start.2
  16.1 5.7 %dequantize.1.refs_6_.refs_3_ = s8[4,3584,512]{2,1,0:T(32,128)(4,1)S(1)} custom-call(s32[3584,512]{1,0:T(8,128)} %packed_ref.1), custom_call_target="tpu_custom_call" | custom-call | flops 7516192768 | tf_op jit(solution)/shard_map/dequantize/pallas_call | solution.py:182
  21.9 0.0 copy-done.10
  21.9 0.0 collective-permute-done.refs_1_
  21.9 0.0 copy-start.12
  21.9 0.8 copy-done.12
  22.6 0.0 collective-permute-done.2.refs_3_
  22.6 0.0 copy-done.6
  22.6 0.0 copy-done.1
  22.7 0.0 copy-done.5
  22.7 0.0 copy-start.11
  22.7 1.0 copy-done.11
  23.7 1.0 copy-done.13
  24.7 8.2 %project.3 = (f32[32,4096]{1,0:T(8,128)S(1)}, bf16[32,4096]{1,0:T(8,128)(2,1)}) custom-call(s32[1]{0:T(128)} %bitcast.me_ref, bf16[64,3584]{1,0:T(8,128)(2,1)S(1)} %copy-done.5, bf16[64,3584]{1,0:T(8,128)(2,1)S(1)} %copy-done.13, bf16[64,3584]{1,0:T(8,128)(2,1)S(1)} %copy-done.11, bf16[64,3584]{1,0:T(8,128)(2,1)S(1)} %collective-permute-done.2.refs_3_, ...), custom_call_target="tpu_custom_call" | custom-call | flops 3758096384 | tf_op jit(solution)/shard_map/project/pallas_call | solution.py:254
  32.9 0.8 copy-done.2
  33.7 2.9 %copy-done.14 = s8[4,3584,512]{2,1,0:T(32,128)(4,1)} copy-done((s8[4,3584,512]{2,1,0:T(32,128)(4,1)}, s8[4,3584,512]{2,1,0:T(32,128)(4,1)S(1)}, u32[]{:S(2)}) %copy-start.14) | copy-done | bytes 7340056
  36.6 0.3 collective-permute-start.3
  37.0 1.6 %collective-permute-done.3 = bf16[32,4096]{1,0:T(8,128)(2,1)} collective-permute-done((bf16[32,4096]{1,0:T(8,128)(2,1)}, bf16[32,4096]{1,0:T(8,128)(2,1)}, u32[]{:S(2)}, u32[]{:S(2)}) %collective-permute-start.3) | collective-permute-done | bytes 262176 | tf_op jit(solution)/shard_map/ppermute | solution.py:314
  38.5 1.2 %convert_add_fusion.2 = f32[32,4096]{1,0:T(8,128)S(1)} fusion(f32[32,4096]{1,0:T(8,128)} %copy-done.2, bf16[32,4096]{1,0:T(8,128)(2,1)} %collective-permute-done.3), kind=kLoop, calls=%fused_computation.3 | loop fusion | flops 262144 | bytes 1310720 | tf_op jit(solution)/shard_map/add | solution.py:347
  39.7 0.0 copy-start.7
  39.7 0.0 collective-permute-done.4.other_ref
  39.7 0.0 copy-done
  39.7 3.3 %rotate.1 = (f32[128,3584]{1,0:T(8,128)S(1)}, bf16[128,3584]{1,0:T(8,128)(2,1)S(1)}, f32[64,3584]{1,0:T(8,128)S(1)}, bf16[64,3584]{1,0:T(8,128)(2,1)S(1)}) custom-call(s32[1]{0:T(128)} %bitcast.me_ref, bf16[256,3584]{1,0:T(8,128)(2,1)S(1)} %copy-done, s32[3584]{0:T(1024)S(1)} %copy-done.9, bf16[192,3584]{1,0:T(8,128)(2,1)} %collective-permute-done.4.other_ref, ...), custom_call_target="tpu_custom_call" | custom-call | flops 1233125376 | tf_op jit(solution)/shard_map/rotate/pallas_call | solution.py:160
  43.0 1.8 %collective-permute-start.7 = (bf16[64,3584]{1,0:T(8,128)(2,1)S(1)}, bf16[64,3584]{1,0:T(8,128)(2,1)S(1)}, u32[]{:S(2)}, u32[]{:S(2)}) collective-permute-start(bf16[64,3584]{1,0:T(8,128)(2,1)S(1)} %get-tuple-element.19), channel_id=1, source_target_pairs={{0,2},{1,3},{2,0},{3,1},{4,6},{5,7},{6,4},{7,5},{8,10},{9,11},{10,... | collective-permute-start | bytes 1376264 | tf_op jit(solution)/shard_map/ppermute | solution.py:314
  44.8 11.0 %collective-permute-done.7.refs_1_ = bf16[64,3584]{1,0:T(8,128)(2,1)S(1)} collective-permute-done((bf16[64,3584]{1,0:T(8,128)(2,1)S(1)}, bf16[64,3584]{1,0:T(8,128)(2,1)S(1)}, u32[]{:S(2)}, u32[]{:S(2)}) %collective-permute-start.7) | collective-permute-done | bytes 458784 | tf_op jit(solution)/shard_map/ppermute | solution.py:314
  55.8 0.0 copy-done.7
  55.8 3.1 %copy-done.15 = s8[4,3584,512]{2,1,0:T(32,128)(4,1)S(1)} copy-done((s8[4,3584,512]{2,1,0:T(32,128)(4,1)S(1)}, s8[4,3584,512]{2,1,0:T(32,128)(4,1)}, u32[]{:S(2)}) %copy-start.15) | copy-done | bytes 7340056
  58.9 6.7 %project.5 = (f32[32,4096]{1,0:T(8,128)S(1)}, bf16[32,4096]{1,0:T(8,128)(2,1)S(1)}) custom-call(s32[1]{0:T(128)} %bitcast.me_ref, f32[64,3584]{1,0:T(8,128)S(1)} %get-tuple-element.18.refs_0_, bf16[64,3584]{1,0:T(8,128)(2,1)S(1)} %collective-permute-done.7.refs_1_, bf16[28,4096]{1,0:T(8,128)(2,1)S(1)} %copy-done.7, s8[4,3584,512]{2,1,0:T(32,128)(4,1)S(1)} %copy-done.15), custom_call_target="tpu_custom_call" | custom-call | flops 3758096384 | tf_op jit(solution)/shard_map/project/pallas_call | solution.py:254
  65.6 0.1 collective-permute-start.8
  65.7 1.8 %collective-permute-start.9 = (bf16[16,4096]{1,0:T(8,128)(2,1)S(1)}, bf16[16,4096]{1,0:T(8,128)(2,1)S(1)}, u32[]{:S(2)}, u32[]{:S(2)}) collective-permute-start(bf16[16,4096]{1,0:T(8,128)(2,1)S(1)} %select_convert_fusion.2), channel_id=1, source_target_pairs={{0,2},{1,3},{2,0},{3,1},{4,6},{5,7},{6,4},{7,5},{8,10},{9,11},{10,... | collective-permute-start | bytes 393224 | tf_op jit(solution)/shard_map/ppermute | solution.py:314
  67.5 0.3 collective-permute-start.5
  67.8 0.0 collective-permute-done.8
  67.8 0.1 convert_add_fusion.1
  67.9 1.8 %collective-permute-start.11 = (bf16[16,4096]{1,0:T(8,128)(2,1)S(1)}, bf16[16,4096]{1,0:T(8,128)(2,1)S(1)}, u32[]{:S(2)}, u32[]{:S(2)}) collective-permute-start(bf16[16,4096]{1,0:T(8,128)(2,1)S(1)} %select_convert_fusion.1), channel_id=1, source_target_pairs={{0,2},{1,3},{2,0},{3,1},{4,6},{5,7},{6,4},{7,5},{8,10},{9,11},{10,... | collective-permute-start | bytes 393224 | tf_op jit(solution)/shard_map/ppermute | solution.py:314
  69.7 22.1 %collective-permute-done.5.refs_1_ = bf16[128,3584]{1,0:T(8,128)(2,1)S(1)} collective-permute-done((bf16[128,3584]{1,0:T(8,128)(2,1)S(1)}, bf16[128,3584]{1,0:T(8,128)(2,1)S(1)}, u32[]{:S(2)}, u32[]{:S(2)}) %collective-permute-start.5) | collective-permute-done | bytes 917536 | tf_op jit(solution)/shard_map/ppermute | solution.py:314
  91.8 0.0 copy-done.16
  91.8 6.7 %project.4 = (f32[64,4096]{1,0:T(8,128)S(1)}, bf16[64,4096]{1,0:T(8,128)(2,1)S(1)}) custom-call(s32[1]{0:T(128)} %bitcast.me_ref, f32[128,3584]{1,0:T(8,128)S(1)} %get-tuple-element.14.refs_0_, bf16[128,3584]{1,0:T(8,128)(2,1)S(1)} %collective-permute-done.5.refs_1_, bf16[28,4096]{1,0:T(8,128)(2,1)S(1)} %copy-done.7, s8[4,3584,512]{2,1,0:T(32,128)(4,1)S(1)} %copy-done.16), custom_call_target="tpu_custom_call" | custom-call | flops 3758096384 | tf_op jit(solution)/shard_map/project/pallas_call | solution.py:254
  98.5 0.1 collective-permute-start.6
  98.6 1.9 %collective-permute-done.6 = bf16[64,4096]{1,0:T(8,128)(2,1)S(1)} collective-permute-done((bf16[64,4096]{1,0:T(8,128)(2,1)S(1)}, bf16[64,4096]{1,0:T(8,128)(2,1)S(1)}, u32[]{:S(2)}, u32[]{:S(2)}) %collective-permute-start.6) | collective-permute-done | bytes 524320 | tf_op jit(solution)/shard_map/ppermute | solution.py:314
  100.5 0.1 convert_add_fusion
  100.6 0.0 copy-start.3
  100.6 0.1 select_convert_fusion
  100.7 1.8 %collective-permute-start.10 = (bf16[32,4096]{1,0:T(8,128)(2,1)S(1)}, bf16[32,4096]{1,0:T(8,128)(2,1)S(1)}, u32[]{:S(2)}, u32[]{:S(2)}) collective-permute-start(bf16[32,4096]{1,0:T(8,128)(2,1)S(1)} %select_convert_fusion), channel_id=1, source_target_pairs={{0,2},{1,3},{2,0},{3,1},{4,6},{5,7},{6,4},{7,5},{8,10},{9,11},{10,... | collective-permute-start | bytes 786440 | tf_op jit(solution)/shard_map/ppermute | solution.py:314
  102.5 0.1 slice_select_fusion.refs_1_
  102.5 0.0 collective-permute-done.9.refs_3_
  102.5 0.0 collective-permute-done.11.refs_5_
  102.5 6.5 %collective-permute-done.10.refs_4_ = bf16[32,4096]{1,0:T(8,128)(2,1)S(1)} collective-permute-done((bf16[32,4096]{1,0:T(8,128)(2,1)S(1)}, bf16[32,4096]{1,0:T(8,128)(2,1)S(1)}, u32[]{:S(2)}, u32[]{:S(2)}) %collective-permute-start.10) | collective-permute-done | bytes 262176 | tf_op jit(solution)/shard_map/ppermute | solution.py:314
  109.1 0.0 copy-done.3
  109.1 1.2 %finish.1 = (bf16[64,4096]{1,0:T(8,128)(2,1)}, bf16[64,4096]{1,0:T(8,128)(2,1)}) custom-call(f32[16,4096]{1,0:T(8,128)S(1)} %slice_select_fusion.2.refs_0_, f32[32,4096]{1,0:T(8,128)S(1)} %slice_select_fusion.refs_1_, f32[16,4096]{1,0:T(8,128)S(1)} %slice_select_fusion.1.refs_2_, bf16[16,4096]{1,0:T(8,128)(2,1)S(1)} %collective-permute-done.9.refs_3_, ...), custom_call_target="tpu_custom_call" | custom-call | flops 268435456 | tf_op jit(solution)/shard_map/finish/pallas_call | solution.py:291
  (15 shorter events, 0.2 us)
Async XLA Ops:
  0.6 0.7 copy-start.8
  1.3 4.2 %copy-start.9 = (s32[3584]{0:T(1024)S(1)}, s32[3584]{0:T(1024)}, u32[]{:S(2)}) copy-start(s32[3584]{0:T(1024)} %signs_ref.5) | copy-start | bytes 43012
  2.5 6.4 %copy-start.4 = (bf16[64,3584]{1,0:T(8,128)(2,1)}, bf16[64,3584]{1,0:T(8,128)(2,1)S(1)}, u32[]{:S(2)}) copy-start(bf16[64,3584]{1,0:T(8,128)(2,1)S(1)} %prepare.2.refs_0_) | copy-start | bytes 1376260
  2.5 6.3 %copy-start.17 = (s32[28,4096]{1,0:T(8,128)S(1)}, s32[28,4096]{1,0:T(8,128)}, u32[]{:S(2)}) copy-start(s32[28,4096]{1,0:T(8,128)} %param.9) | copy-start | bytes 1376260
  2.5 13.6 %collective-permute-start.1 = (bf16[64,3584]{1,0:T(8,128)(2,1)S(1)}, bf16[64,3584]{1,0:T(8,128)(2,1)S(1)}, u32[]{:S(2)}, u32[]{:S(2)}) collective-permute-start(bf16[64,3584]{1,0:T(8,128)(2,1)S(1)} %prepare.2.refs_0_), channel_id=1, source_target_pairs={{0,2},{1,3},{2,0},{3,1},{4,6},{5,7},{6,4},{7,5},{8,10},{9,11},{10,... | collective-permute-start | bytes 1376264 | tf_op jit(solution)/shard_map/ppermute | solution.py:314
  5.6 16.3 %collective-permute-start = (bf16[64,3584]{1,0:T(8,128)(2,1)S(1)}, bf16[64,3584]{1,0:T(8,128)(2,1)S(1)}, u32[]{:S(2)}, u32[]{:S(2)}) collective-permute-start(bf16[64,3584]{1,0:T(8,128)(2,1)S(1)} %prepare.2.refs_0_), channel_id=1, source_target_pairs={{0,1},{1,0},{2,3},{3,2},{4,5},{5,4},{6,7},{7,6},{8,9},{9,8},{10,11... | collective-permute-start | bytes 1376264 | tf_op jit(solution)/shard_map/ppermute | solution.py:314
  8.3 31.4 %collective-permute-start.4 = (bf16[192,3584]{1,0:T(8,128)(2,1)}, bf16[192,3584]{1,0:T(8,128)(2,1)}, u32[]{:S(2)}, u32[]{:S(2)}) collective-permute-start(bf16[192,3584]{1,0:T(8,128)(2,1)} %prepare.3), channel_id=1, source_target_pairs={{0,1},{1,0},{2,3},{3,2},{4,5},{5,4},{6,7},{7,6},{8,9},{9,8},{10,11... | collective-permute-start | bytes 4128776 | tf_op jit(solution)/shard_map/ppermute | solution.py:314
  8.9 13.7 %copy-start.6 = (bf16[28,4096]{1,0:T(8,128)(2,1)}, bf16[28,4096]{1,0:T(8,128)(2,1)S(1)}, u32[]{:S(2)}) copy-start(bf16[28,4096]{1,0:T(8,128)(2,1)S(1)} %multiply_convert_fusion.refs_5_.refs_2_) | copy-start | bytes 688132
  8.9 13.7 %copy-start.1 = (bf16[896,896]{1,0:T(8,128)(2,1)S(1)}, bf16[896,896]{1,0:T(8,128)(2,1)}, u32[]{:S(2)}) copy-start(bf16[896,896]{1,0:T(8,128)(2,1)} %constant.43.clone.refs_4_.table_ref) | copy-start | bytes 4816900
  16.1 5.8 %copy-start.10 = (bf16[64,3584]{1,0:T(8,128)(2,1)}, bf16[64,3584]{1,0:T(8,128)(2,1)S(1)}, u32[]{:S(2)}) copy-start(bf16[64,3584]{1,0:T(8,128)(2,1)S(1)} %collective-permute-done.1.refs_2_) | copy-start | bytes 1376260
  16.1 6.6 %copy-start.5 = (bf16[64,3584]{1,0:T(8,128)(2,1)S(1)}, bf16[64,3584]{1,0:T(8,128)(2,1)}, u32[]{:S(2)}) copy-start(bf16[64,3584]{1,0:T(8,128)(2,1)} %copy-done.4) | copy-start | bytes 1376260
  16.1 6.5 %collective-permute-start.2 = (bf16[64,3584]{1,0:T(8,128)(2,1)S(1)}, bf16[64,3584]{1,0:T(8,128)(2,1)S(1)}, u32[]{:S(2)}, u32[]{:S(2)}) collective-permute-start(bf16[64,3584]{1,0:T(8,128)(2,1)S(1)} %collective-permute-done.1.refs_2_), channel_id=1, source_target_pairs={{0,1},{1,0},{2,3},{3,2},{4,5},{5,4},{6,7},{7,6},{8,9},{9,8},{10,11... | collective-permute-start | bytes 1376264 | tf_op jit(solution)/shard_map/ppermute | solution.py:314
  21.9 0.8 copy-start.12
  22.7 1.0 copy-start.11
  23.7 1.0 copy-start.13
  24.7 15.0 %copy-start = (bf16[256,3584]{1,0:T(8,128)(2,1)S(1)}, bf16[256,3584]{1,0:T(8,128)(2,1)}, u32[]{:S(2)}) copy-start(bf16[256,3584]{1,0:T(8,128)(2,1)} %hidden_ref.5) | copy-start | bytes 5505028
  32.9 0.8 copy-start.2
  33.7 2.9 %copy-start.14 = (s8[4,3584,512]{2,1,0:T(32,128)(4,1)}, s8[4,3584,512]{2,1,0:T(32,128)(4,1)S(1)}, u32[]{:S(2)}) copy-start(s8[4,3584,512]{2,1,0:T(32,128)(4,1)S(1)} %dequantize.1.refs_6_.refs_3_) | copy-start | bytes 22020100
  36.6 1.9 %collective-permute-start.3 = (bf16[32,4096]{1,0:T(8,128)(2,1)}, bf16[32,4096]{1,0:T(8,128)(2,1)}, u32[]{:S(2)}, u32[]{:S(2)}) collective-permute-start(bf16[32,4096]{1,0:T(8,128)(2,1)} %get-tuple-element.13), channel_id=1, source_target_pairs={{0,1},{1,0},{2,3},{3,2},{4,5},{5,4},{6,7},{7,6},{8,9},{9,8},{10,11... | collective-permute-start | bytes 786440 | tf_op jit(solution)/shard_map/ppermute | solution.py:314
  39.7 16.2 %copy-start.7 = (bf16[28,4096]{1,0:T(8,128)(2,1)S(1)}, bf16[28,4096]{1,0:T(8,128)(2,1)}, u32[]{:S(2)}) copy-start(bf16[28,4096]{1,0:T(8,128)(2,1)} %copy-done.6) | copy-start | bytes 688132
  43.0 12.8 %collective-permute-start.7 = (bf16[64,3584]{1,0:T(8,128)(2,1)S(1)}, bf16[64,3584]{1,0:T(8,128)(2,1)S(1)}, u32[]{:S(2)}, u32[]{:S(2)}) collective-permute-start(bf16[64,3584]{1,0:T(8,128)(2,1)S(1)} %get-tuple-element.19), channel_id=1, source_target_pairs={{0,2},{1,3},{2,0},{3,1},{4,6},{5,7},{6,4},{7,5},{8,10},{9,11},{10,... | collective-permute-start | bytes 1376264 | tf_op jit(solution)/shard_map/ppermute | solution.py:314
  55.8 3.1 %copy-start.15 = (s8[4,3584,512]{2,1,0:T(32,128)(4,1)S(1)}, s8[4,3584,512]{2,1,0:T(32,128)(4,1)}, u32[]{:S(2)}) copy-start(s8[4,3584,512]{2,1,0:T(32,128)(4,1)} %copy-done.14) | copy-start | bytes 22020100
  58.9 32.9 %copy-start.16 = (s8[4,3584,512]{2,1,0:T(32,128)(4,1)S(1)}, s8[4,3584,512]{2,1,0:T(32,128)(4,1)}, u32[]{:S(2)}) copy-start(s8[4,3584,512]{2,1,0:T(32,128)(4,1)} %copy-done.14) | copy-start | bytes 22020100
  65.6 2.2 %collective-permute-start.8 = (bf16[32,4096]{1,0:T(8,128)(2,1)S(1)}, bf16[32,4096]{1,0:T(8,128)(2,1)S(1)}, u32[]{:S(2)}, u32[]{:S(2)}) collective-permute-start(bf16[32,4096]{1,0:T(8,128)(2,1)S(1)} %get-tuple-element.21), channel_id=1, source_target_pairs={{0,1},{1,0},{2,3},{3,2},{4,5},{5,4},{6,7},{7,6},{8,9},{9,8},{10,11... | collective-permute-start | bytes 786440 | tf_op jit(solution)/shard_map/ppermute | solution.py:314
  65.7 36.8 %collective-permute-start.9 = (bf16[16,4096]{1,0:T(8,128)(2,1)S(1)}, bf16[16,4096]{1,0:T(8,128)(2,1)S(1)}, u32[]{:S(2)}, u32[]{:S(2)}) collective-permute-start(bf16[16,4096]{1,0:T(8,128)(2,1)S(1)} %select_convert_fusion.2), channel_id=1, source_target_pairs={{0,2},{1,3},{2,0},{3,1},{4,6},{5,7},{6,4},{7,5},{8,10},{9,11},{10,... | collective-permute-start | bytes 393224 | tf_op jit(solution)/shard_map/ppermute | solution.py:314
  67.5 24.3 %collective-permute-start.5 = (bf16[128,3584]{1,0:T(8,128)(2,1)S(1)}, bf16[128,3584]{1,0:T(8,128)(2,1)S(1)}, u32[]{:S(2)}, u32[]{:S(2)}) collective-permute-start(bf16[128,3584]{1,0:T(8,128)(2,1)S(1)} %get-tuple-element.15), channel_id=1, source_target_pairs={{0,2},{1,3},{2,0},{3,1},{4,6},{5,7},{6,4},{7,5},{8,10},{9,11},{10,... | collective-permute-start | bytes 2752520 | tf_op jit(solution)/shard_map/ppermute | solution.py:314
  67.9 34.7 %collective-permute-start.11 = (bf16[16,4096]{1,0:T(8,128)(2,1)S(1)}, bf16[16,4096]{1,0:T(8,128)(2,1)S(1)}, u32[]{:S(2)}, u32[]{:S(2)}) collective-permute-start(bf16[16,4096]{1,0:T(8,128)(2,1)S(1)} %select_convert_fusion.1), channel_id=1, source_target_pairs={{0,2},{1,3},{2,0},{3,1},{4,6},{5,7},{6,4},{7,5},{8,10},{9,11},{10,... | collective-permute-start | bytes 393224 | tf_op jit(solution)/shard_map/ppermute | solution.py:314
  98.5 2.0 %collective-permute-start.6 = (bf16[64,4096]{1,0:T(8,128)(2,1)S(1)}, bf16[64,4096]{1,0:T(8,128)(2,1)S(1)}, u32[]{:S(2)}, u32[]{:S(2)}) collective-permute-start(bf16[64,4096]{1,0:T(8,128)(2,1)S(1)} %get-tuple-element.17), channel_id=1, source_target_pairs={{0,1},{1,0},{2,3},{3,2},{4,5},{5,4},{6,7},{7,6},{8,9},{9,8},{10,11... | collective-permute-start | bytes 1572872 | tf_op jit(solution)/shard_map/ppermute | solution.py:314
  100.6 8.5 %copy-start.3 = (bf16[64,4096]{1,0:T(8,128)(2,1)S(1)}, bf16[64,4096]{1,0:T(8,128)(2,1)}, u32[]{:S(2)}) copy-start(bf16[64,4096]{1,0:T(8,128)(2,1)} %refs_6_.1) | copy-start | bytes 1572868
  100.7 8.4 %collective-permute-start.10 = (bf16[32,4096]{1,0:T(8,128)(2,1)S(1)}, bf16[32,4096]{1,0:T(8,128)(2,1)S(1)}, u32[]{:S(2)}, u32[]{:S(2)}) collective-permute-start(bf16[32,4096]{1,0:T(8,128)(2,1)S(1)} %select_convert_fusion), channel_id=1, source_target_pairs={{0,2},{1,3},{2,0},{3,1},{4,6},{5,7},{6,4},{7,5},{8,10},{9,11},{10,... | collective-permute-start | bytes 786440 | tf_op jit(solution)/shard_map/ppermute | solution.py:314

commit v5 on v4

--- a/solution.py
+++ b/solution.py
@@ -65,8 +65,11 @@
     return (1 - 2 * bit).astype(jnp.float32)
 
 
-def prepare_kernel(groups, token_rows, places, hidden_ref, signs_ref, out_ref, staged, sems):
+def prepare_kernel(groups, token_rows, places, hidden_ref, signs_ref, *refs):
+    out_refs, (staged, flips, sems, flips_sem) = refs[:-4], refs[-4:]
     width = hidden_ref.shape[1]
+    flips_copy = pltpu.make_async_copy(signs_ref, flips, flips_sem)
+    flips_copy.start()
     copies, at = [], 0
     for start, size in places:
         for owner in bit_reversed(groups):
@@ -79,33 +82,42 @@
             )
             copies[-1].start()
             at += size
-    flips = (2 * signs_ref[...] - 1).astype(jnp.float32).reshape(1, width)
+    flips_copy.wait()
+    flip = (2 * flips[...] - 1).astype(jnp.float32).reshape(1, width)
+    first_rows = groups * places[0][1]
     at = 0
     for index, copy in enumerate(copies):
         size = places[index // groups][1]
         copy.wait()
-        rows = pl.ds(at, size)
-        out_ref[rows, :] = (staged[rows, :].astype(jnp.float32) * flips).astype(jnp.bfloat16)
+        value = (staged[pl.ds(at, size), :].astype(jnp.float32) * flip).astype(jnp.bfloat16)
+        if index < groups:
+            out_refs[0][pl.ds(at, size), :] = value
+        else:
+            out_refs[1][pl.ds(at - first_rows, size), :] = value
         at += size
 
 
 def prepare(hidden, signs, groups, places):
-    width = hidden.shape[1]
-    rows = groups * sum(size for _, size in places)
-    count = groups * len(places)
-    return pl.pallas_call(
-        functools.partial(prepare_kernel, groups, hidden.shape[0] // groups, places),
-        out_shape=jax.ShapeDtypeStruct((rows, width), jnp.bfloat16),
-        in_specs=[HBM, VMEM],
-        out_specs=VMEM,
+    rows, width = hidden.shape
+    first_rows = groups * places[0][1]
+    shapes = [pltpu.VMEM((first_rows, width), jnp.bfloat16)]
+    if len(places) > 1:
+        shapes.append(pltpu.VMEM((rows - first_rows, width), jnp.bfloat16))
+    return pl.pallas_call(
+        functools.partial(prepare_kernel, groups, rows // groups, places),
+        out_shape=shapes,
+        in_specs=[HBM, HBM],
+        out_specs=[VMEM] * len(shapes),
         scratch_shapes=[
             pltpu.VMEM((rows, width), jnp.bfloat16),
-            pltpu.SemaphoreType.DMA((count,)),
+            pltpu.VMEM((width,), jnp.int32),
+            pltpu.SemaphoreType.DMA((groups * len(places),)),
+            pltpu.SemaphoreType.DMA,
         ],
-        compiler_params=pltpu.CompilerParams(vmem_limit_bytes=12 * 2**20),
+        compiler_params=pltpu.CompilerParams(vmem_limit_bytes=8 * 2**20),
         cost_estimate=cost(rows * width),
         name="prepare",
-    )(pltpu.with_memory_space_constraint(hidden, pltpu.HBM), signs)
+    )(*[pltpu.with_memory_space_constraint(value, pltpu.HBM) for value in (hidden, signs)])
 
 
 def rotate_blocks(mixed, table_ref, stacked_ref):
@@ -316,16 +328,15 @@
     def bit_of(bit):
         return jnp.right_shift(me, bit) & 1
 
-    first = prepare(hidden, signs, groups, [(0, sizes[0])])
+    places = [(sum(sizes[:chunk]), sizes[chunk]) for chunk in range(chunks)]
+    first, *sent = prepare(hidden, signs, groups, places)
     have = {0: first}
     for bit in reversed(range(bits)):
         have.update({r ^ (1 << bit): swap(value, bit) for r, value in list(have.items())})
     stages = [([have[r] for r in range(groups)], table)]
     if chunks > 1:
-        places = [(sum(sizes[:chunk]), sizes[chunk]) for chunk in range(1, chunks)]
-        sent = prepare(hidden, signs, groups, places)
-        other = swap(sent, 0)
-        pairs = rotate(hidden, signs, other, where, table, groups, places)
+        other = swap(sent[0], 0)
+        pairs = rotate(hidden, signs, other, where, table, groups, places[1:])
         for chunk in range(1, chunks):
             keep, send = pairs[2 * chunk - 2], pairs[2 * chunk - 1]
             for bit in range(1, bits):

time: 111 us -> 113 us (1.018)
  waiting for transfers between devices: 50.2 us -> 53 us
    ppermute x12, waiting for transfers between devices: 50.2 us -> 53 us  [swap(): lax.ppermute(value, 'tensor', [(i, i ^ 1 << bit) for i in range(groups)])]
    pallas_call x2 -> x1, Pallas kernels: 3.8 us -> 3.05 us  [prepare(): pl.pallas_call(functools.partial(prepare_kernel, groups, rows // groups,...]
    unnamed x36 -> x34, local copies, waits for them, and re-layouts: 10.4 us -> 10.7 us
  transfers between devices with their start and end apart: 12 -> 12, of which waited for: 6 -> 6; matrix products, arithmetic and copies ran while one was open for 1% -> 1% of each run, Pallas kernels for 21% -> 18%
where the time goes in v5:
time: 113 us
  waiting for transfers between devices  53 us (47%)
  Pallas kernels  34.9 us (31%)
  starting transfers between devices  11.6 us (10%)
  local copies, waits for them, and re-layouts  10.7 us (9%)
  other arithmetic  1.57 us (1%)
    ppermute x12, waiting for transfers between devices, swap(): lax.ppermute(value, 'tensor', [(i, i ^ 1 << bit) for i in range(groups)])  53 us
    pallas_call x3, Pallas kernels, project(): pl.pallas_call(functools.partial(project_kernel, count, unit, table is no...  21.6 us
    ppermute x12, starting transfers between devices, swap(): lax.ppermute(value, 'tensor', [(i, i ^ 1 << bit) for i in range(groups)])  11.6 us
    unnamed x34, local copies, waits for them, and re-layouts  10.7 us
    pallas_call x1, Pallas kernels, dequantize(): pl.pallas_call(dequantize_kernel, grid=(width // rows,), out_shape=jax.Sh...  5.72 us
    pallas_call x1, Pallas kernels, rotate(): pl.pallas_call(functools.partial(rotate_kernel, groups, places), out_shap...  3.3 us
    pallas_call x1, Pallas kernels, prepare(): pl.pallas_call(functools.partial(prepare_kernel, groups, rows // groups,...  3.05 us
  transfers between devices with their start and end apart: 12, of which 6 were waited for; matrix products, arithmetic and copies ran while one was open for 1% of the time, Pallas kernels for 18%

profile of v5, /device:TPU:0, one launch (start us, length us, event | category | flops | bytes accessed | tf_op | source)
XLA Modules:
  0.0 112.5 jit_solution(14390982839758842101)
XLA Ops:
  0.6 0.0 copy-start.16
  0.6 3.0 %prepare.1 = (bf16[64,3584]{1,0:T(8,128)(2,1)S(1)}, bf16[192,3584]{1,0:T(8,128)(2,1)}) custom-call(bf16[256,3584]{1,0:T(8,128)(2,1)} %hidden_ref.3, s32[3584]{0:T(1024)} %signs_ref.3), custom_call_target="tpu_custom_call" | custom-call | flops 917504 | tf_op jit(solution)/shard_map/prepare/pallas_call | solution.py:106
  3.7 0.0 copy-start.7
  3.7 3.1 %collective-permute-start.1 = (bf16[64,3584]{1,0:T(8,128)(2,1)S(1)}, bf16[64,3584]{1,0:T(8,128)(2,1)S(1)}, u32[]{:S(2)}, u32[]{:S(2)}) collective-permute-start(bf16[64,3584]{1,0:T(8,128)(2,1)S(1)} %get-tuple-element.14.refs_0_), channel_id=1, source_target_pairs={{0,2},{1,3},{2,0},{3,1},{4,6},{5,7},{6,4},{7,5},{8,10},{9,11},{10,... | collective-permute-start | bytes 1376264 | tf_op jit(solution)/shard_map/ppermute | solution.py:326
  6.8 0.0 collective-permute-start
  6.8 0.5 collective-permute-start.4
  7.3 0.0 copy-done.16
  7.3 0.0 copy-start.4
  7.4 0.0 copy-start.1
  7.4 9.9 %collective-permute-done.1.refs_2_ = bf16[64,3584]{1,0:T(8,128)(2,1)S(1)} collective-permute-done((bf16[64,3584]{1,0:T(8,128)(2,1)S(1)}, bf16[64,3584]{1,0:T(8,128)(2,1)S(1)}, u32[]{:S(2)}, u32[]{:S(2)}) %collective-permute-start.1) | collective-permute-done | bytes 458784 | tf_op jit(solution)/shard_map/ppermute | solution.py:326
  17.3 0.0 copy-start.9
  17.3 0.0 collective-permute-start.2
  17.3 5.7 %dequantize.1.refs_6_.refs_3_ = s8[4,3584,512]{2,1,0:T(32,128)(4,1)S(1)} custom-call(s32[3584,512]{1,0:T(8,128)} %packed_ref.1), custom_call_target="tpu_custom_call" | custom-call | flops 7516192768 | tf_op jit(solution)/shard_map/dequantize/pallas_call | solution.py:194
  23.0 0.0 copy-done.7
  23.0 0.0 copy-done.9
  23.0 0.0 collective-permute-done.refs_1_
  23.0 0.0 copy-start.11
  23.1 0.8 copy-done.11
  23.8 0.0 collective-permute-done.2.refs_3_
  23.8 0.0 copy-done.4
  23.8 0.0 copy-done.1
  23.8 0.0 copy-start.8
  23.8 1.0 copy-done.8
  24.9 0.0 copy-start.10
  24.9 1.0 copy-done.10
  25.9 0.0 copy-start.12
  25.9 1.0 copy-done.12
  26.9 8.2 %project.3 = (f32[32,4096]{1,0:T(8,128)S(1)}, bf16[32,4096]{1,0:T(8,128)(2,1)}) custom-call(s32[1]{0:T(128)} %bitcast.me_ref, bf16[64,3584]{1,0:T(8,128)(2,1)S(1)} %copy-done.8, bf16[64,3584]{1,0:T(8,128)(2,1)S(1)} %copy-done.12, bf16[64,3584]{1,0:T(8,128)(2,1)S(1)} %copy-done.10, bf16[64,3584]{1,0:T(8,128)(2,1)S(1)} %collective-permute-done.2.refs_3_, ...), custom_call_target="tpu_custom_call" | custom-call | flops 3758096384 | tf_op jit(solution)/shard_map/project/pallas_call | solution.py:266
  35.1 0.8 copy-done.2
  35.9 2.9 %copy-done.13 = s8[4,3584,512]{2,1,0:T(32,128)(4,1)} copy-done((s8[4,3584,512]{2,1,0:T(32,128)(4,1)}, s8[4,3584,512]{2,1,0:T(32,128)(4,1)S(1)}, u32[]{:S(2)}) %copy-start.13) | copy-done | bytes 7340056
  38.8 0.3 collective-permute-start.3
  39.2 1.5 %collective-permute-done.3 = bf16[32,4096]{1,0:T(8,128)(2,1)} collective-permute-done((bf16[32,4096]{1,0:T(8,128)(2,1)}, bf16[32,4096]{1,0:T(8,128)(2,1)}, u32[]{:S(2)}, u32[]{:S(2)}) %collective-permute-start.3) | collective-permute-done | bytes 262176 | tf_op jit(solution)/shard_map/ppermute | solution.py:326
  40.7 1.2 %convert_add_fusion.2 = f32[32,4096]{1,0:T(8,128)S(1)} fusion(f32[32,4096]{1,0:T(8,128)} %copy-done.2, bf16[32,4096]{1,0:T(8,128)(2,1)} %collective-permute-done.3), kind=kLoop, calls=%fused_computation.3 | loop fusion | flops 262144 | bytes 1310720 | tf_op jit(solution)/shard_map/add | solution.py:358
  41.9 0.0 copy-start.5
  41.9 0.0 collective-permute-done.4.other_ref
  41.9 0.0 copy-done
  41.9 0.0 copy-done.6
  41.9 3.3 %rotate.1 = (f32[128,3584]{1,0:T(8,128)S(1)}, bf16[128,3584]{1,0:T(8,128)(2,1)S(1)}, f32[64,3584]{1,0:T(8,128)S(1)}, bf16[64,3584]{1,0:T(8,128)(2,1)S(1)}) custom-call(s32[1]{0:T(128)} %bitcast.me_ref, bf16[256,3584]{1,0:T(8,128)(2,1)S(1)} %copy-done, s32[3584]{0:T(1024)S(1)} %copy-done.6, bf16[192,3584]{1,0:T(8,128)(2,1)} %collective-permute-done.4.other_ref, ...), custom_call_target="tpu_custom_call" | custom-call | flops 1233125376 | tf_op jit(solution)/shard_map/rotate/pallas_call | solution.py:172
  45.2 1.8 %collective-permute-start.7 = (bf16[64,3584]{1,0:T(8,128)(2,1)S(1)}, bf16[64,3584]{1,0:T(8,128)(2,1)S(1)}, u32[]{:S(2)}, u32[]{:S(2)}) collective-permute-start(bf16[64,3584]{1,0:T(8,128)(2,1)S(1)} %get-tuple-element.23), channel_id=1, source_target_pairs={{0,2},{1,3},{2,0},{3,1},{4,6},{5,7},{6,4},{7,5},{8,10},{9,11},{10,... | collective-permute-start | bytes 1376264 | tf_op jit(solution)/shard_map/ppermute | solution.py:326
  47.0 11.0 %collective-permute-done.7.refs_1_ = bf16[64,3584]{1,0:T(8,128)(2,1)S(1)} collective-permute-done((bf16[64,3584]{1,0:T(8,128)(2,1)S(1)}, bf16[64,3584]{1,0:T(8,128)(2,1)S(1)}, u32[]{:S(2)}, u32[]{:S(2)}) %collective-permute-start.7) | collective-permute-done | bytes 458784 | tf_op jit(solution)/shard_map/ppermute | solution.py:326
  58.0 0.0 copy-done.5
  58.0 3.1 %copy-done.14 = s8[4,3584,512]{2,1,0:T(32,128)(4,1)S(1)} copy-done((s8[4,3584,512]{2,1,0:T(32,128)(4,1)S(1)}, s8[4,3584,512]{2,1,0:T(32,128)(4,1)}, u32[]{:S(2)}) %copy-start.14) | copy-done | bytes 7340056
  61.1 6.7 %project.5 = (f32[32,4096]{1,0:T(8,128)S(1)}, bf16[32,4096]{1,0:T(8,128)(2,1)S(1)}) custom-call(s32[1]{0:T(128)} %bitcast.me_ref, f32[64,3584]{1,0:T(8,128)S(1)} %get-tuple-element.22.refs_0_, bf16[64,3584]{1,0:T(8,128)(2,1)S(1)} %collective-permute-done.7.refs_1_, bf16[28,4096]{1,0:T(8,128)(2,1)S(1)} %copy-done.5, s8[4,3584,512]{2,1,0:T(32,128)(4,1)S(1)} %copy-done.14), custom_call_target="tpu_custom_call" | custom-call | flops 3758096384 | tf_op jit(solution)/shard_map/project/pallas_call | solution.py:266
  67.8 0.1 collective-permute-start.8
  67.9 1.8 %collective-permute-start.9 = (bf16[16,4096]{1,0:T(8,128)(2,1)S(1)}, bf16[16,4096]{1,0:T(8,128)(2,1)S(1)}, u32[]{:S(2)}, u32[]{:S(2)}) collective-permute-start(bf16[16,4096]{1,0:T(8,128)(2,1)S(1)} %select_convert_fusion.2), channel_id=1, source_target_pairs={{0,2},{1,3},{2,0},{3,1},{4,6},{5,7},{6,4},{7,5},{8,10},{9,11},{10,... | collective-permute-start | bytes 393224 | tf_op jit(solution)/shard_map/ppermute | solution.py:326
  69.7 0.3 collective-permute-start.5
  70.0 0.0 collective-permute-done.8
  70.0 0.1 convert_add_fusion.1
  70.1 1.8 %collective-permute-start.11 = (bf16[16,4096]{1,0:T(8,128)(2,1)S(1)}, bf16[16,4096]{1,0:T(8,128)(2,1)S(1)}, u32[]{:S(2)}, u32[]{:S(2)}) collective-permute-start(bf16[16,4096]{1,0:T(8,128)(2,1)S(1)} %select_convert_fusion.1), channel_id=1, source_target_pairs={{0,2},{1,3},{2,0},{3,1},{4,6},{5,7},{6,4},{7,5},{8,10},{9,11},{10,... | collective-permute-start | bytes 393224 | tf_op jit(solution)/shard_map/ppermute | solution.py:326
  71.9 22.1 %collective-permute-done.5.refs_1_ = bf16[128,3584]{1,0:T(8,128)(2,1)S(1)} collective-permute-done((bf16[128,3584]{1,0:T(8,128)(2,1)S(1)}, bf16[128,3584]{1,0:T(8,128)(2,1)S(1)}, u32[]{:S(2)}, u32[]{:S(2)}) %collective-permute-start.5) | collective-permute-done | bytes 917536 | tf_op jit(solution)/shard_map/ppermute | solution.py:326
  94.0 0.0 copy-done.15
  94.0 6.7 %project.4 = (f32[64,4096]{1,0:T(8,128)S(1)}, bf16[64,4096]{1,0:T(8,128)(2,1)S(1)}) custom-call(s32[1]{0:T(128)} %bitcast.me_ref, f32[128,3584]{1,0:T(8,128)S(1)} %get-tuple-element.18.refs_0_, bf16[128,3584]{1,0:T(8,128)(2,1)S(1)} %collective-permute-done.5.refs_1_, bf16[28,4096]{1,0:T(8,128)(2,1)S(1)} %copy-done.5, s8[4,3584,512]{2,1,0:T(32,128)(4,1)S(1)} %copy-done.15), custom_call_target="tpu_custom_call" | custom-call | flops 3758096384 | tf_op jit(solution)/shard_map/project/pallas_call | solution.py:266
  100.7 0.1 collective-permute-start.6
  100.9 1.9 %collective-permute-done.6 = bf16[64,4096]{1,0:T(8,128)(2,1)S(1)} collective-permute-done((bf16[64,4096]{1,0:T(8,128)(2,1)S(1)}, bf16[64,4096]{1,0:T(8,128)(2,1)S(1)}, u32[]{:S(2)}, u32[]{:S(2)}) %collective-permute-start.6) | collective-permute-done | bytes 524320 | tf_op jit(solution)/shard_map/ppermute | solution.py:326
  102.7 0.1 convert_add_fusion
  102.8 0.0 copy-start.3
  102.8 0.1 select_convert_fusion
  102.9 1.8 %collective-permute-start.10 = (bf16[32,4096]{1,0:T(8,128)(2,1)S(1)}, bf16[32,4096]{1,0:T(8,128)(2,1)S(1)}, u32[]{:S(2)}, u32[]{:S(2)}) collective-permute-start(bf16[32,4096]{1,0:T(8,128)(2,1)S(1)} %select_convert_fusion), channel_id=1, source_target_pairs={{0,2},{1,3},{2,0},{3,1},{4,6},{5,7},{6,4},{7,5},{8,10},{9,11},{10,... | collective-permute-start | bytes 786440 | tf_op jit(solution)/shard_map/ppermute | solution.py:326
  104.7 0.1 slice_select_fusion.refs_1_
  104.8 0.0 collective-permute-done.9.refs_3_
  104.8 0.0 collective-permute-done.11.refs_5_
  104.8 6.5 %collective-permute-done.10.refs_4_ = bf16[32,4096]{1,0:T(8,128)(2,1)S(1)} collective-permute-done((bf16[32,4096]{1,0:T(8,128)(2,1)S(1)}, bf16[32,4096]{1,0:T(8,128)(2,1)S(1)}, u32[]{:S(2)}, u32[]{:S(2)}) %collective-permute-start.10) | collective-permute-done | bytes 262176 | tf_op jit(solution)/shard_map/ppermute | solution.py:326
  111.3 0.0 copy-done.3
  111.3 1.2 %finish.1 = (bf16[64,4096]{1,0:T(8,128)(2,1)}, bf16[64,4096]{1,0:T(8,128)(2,1)}) custom-call(f32[16,4096]{1,0:T(8,128)S(1)} %slice_select_fusion.2.refs_0_, f32[32,4096]{1,0:T(8,128)S(1)} %slice_select_fusion.refs_1_, f32[16,4096]{1,0:T(8,128)S(1)} %slice_select_fusion.1.refs_2_, bf16[16,4096]{1,0:T(8,128)(2,1)S(1)} %collective-permute-done.9.refs_3_, ...), custom_call_target="tpu_custom_call" | custom-call | flops 268435456 | tf_op jit(solution)/shard_map/finish/pallas_call | solution.py:303
  (12 shorter events, 0.2 us)
Async XLA Ops:
  0.6 6.7 %copy-start.16 = (s32[28,4096]{1,0:T(8,128)S(1)}, s32[28,4096]{1,0:T(8,128)}, u32[]{:S(2)}) copy-start(s32[28,4096]{1,0:T(8,128)} %param.9) | copy-start | bytes 1376260
  3.7 19.3 %copy-start.7 = (bf16[64,3584]{1,0:T(8,128)(2,1)}, bf16[64,3584]{1,0:T(8,128)(2,1)S(1)}, u32[]{:S(2)}) copy-start(bf16[64,3584]{1,0:T(8,128)(2,1)S(1)} %get-tuple-element.14.refs_0_) | copy-start | bytes 1376260
  3.7 13.6 %collective-permute-start.1 = (bf16[64,3584]{1,0:T(8,128)(2,1)S(1)}, bf16[64,3584]{1,0:T(8,128)(2,1)S(1)}, u32[]{:S(2)}, u32[]{:S(2)}) collective-permute-start(bf16[64,3584]{1,0:T(8,128)(2,1)S(1)} %get-tuple-element.14.refs_0_), channel_id=1, source_target_pairs={{0,2},{1,3},{2,0},{3,1},{4,6},{5,7},{6,4},{7,5},{8,10},{9,11},{10,... | collective-permute-start | bytes 1376264 | tf_op jit(solution)/shard_map/ppermute | solution.py:326
  6.8 16.3 %collective-permute-start = (bf16[64,3584]{1,0:T(8,128)(2,1)S(1)}, bf16[64,3584]{1,0:T(8,128)(2,1)S(1)}, u32[]{:S(2)}, u32[]{:S(2)}) collective-permute-start(bf16[64,3584]{1,0:T(8,128)(2,1)S(1)} %get-tuple-element.14.refs_0_), channel_id=1, source_target_pairs={{0,1},{1,0},{2,3},{3,2},{4,5},{5,4},{6,7},{7,6},{8,9},{9,8},{10,11... | collective-permute-start | bytes 1376264 | tf_op jit(solution)/shard_map/ppermute | solution.py:326
  6.8 35.1 %collective-permute-start.4 = (bf16[192,3584]{1,0:T(8,128)(2,1)}, bf16[192,3584]{1,0:T(8,128)(2,1)}, u32[]{:S(2)}, u32[]{:S(2)}) collective-permute-start(bf16[192,3584]{1,0:T(8,128)(2,1)} %get-tuple-element.17), channel_id=1, source_target_pairs={{0,1},{1,0},{2,3},{3,2},{4,5},{5,4},{6,7},{7,6},{8,9},{9,8},{10,11... | collective-permute-start | bytes 4128776 | tf_op jit(solution)/shard_map/ppermute | solution.py:326
  7.3 16.5 %copy-start.4 = (bf16[28,4096]{1,0:T(8,128)(2,1)}, bf16[28,4096]{1,0:T(8,128)(2,1)S(1)}, u32[]{:S(2)}) copy-start(bf16[28,4096]{1,0:T(8,128)(2,1)S(1)} %multiply_convert_fusion.refs_5_.refs_2_) | copy-start | bytes 688132
  7.4 16.5 %copy-start.1 = (bf16[896,896]{1,0:T(8,128)(2,1)S(1)}, bf16[896,896]{1,0:T(8,128)(2,1)}, u32[]{:S(2)}) copy-start(bf16[896,896]{1,0:T(8,128)(2,1)} %constant.43.clone.refs_4_.table_ref) | copy-start | bytes 4816900
  17.3 5.7 %copy-start.9 = (bf16[64,3584]{1,0:T(8,128)(2,1)}, bf16[64,3584]{1,0:T(8,128)(2,1)S(1)}, u32[]{:S(2)}) copy-start(bf16[64,3584]{1,0:T(8,128)(2,1)S(1)} %collective-permute-done.1.refs_2_) | copy-start | bytes 1376260
  17.3 6.5 %collective-permute-start.2 = (bf16[64,3584]{1,0:T(8,128)(2,1)S(1)}, bf16[64,3584]{1,0:T(8,128)(2,1)S(1)}, u32[]{:S(2)}, u32[]{:S(2)}) collective-permute-start(bf16[64,3584]{1,0:T(8,128)(2,1)S(1)} %collective-permute-done.1.refs_2_), channel_id=1, source_target_pairs={{0,1},{1,0},{2,3},{3,2},{4,5},{5,4},{6,7},{7,6},{8,9},{9,8},{10,11... | collective-permute-start | bytes 1376264 | tf_op jit(solution)/shard_map/ppermute | solution.py:326
  23.0 0.8 copy-start.11
  23.8 1.0 copy-start.8
  24.9 1.0 copy-start.10
  25.9 1.0 copy-start.12
  26.9 15.0 %copy-start = (bf16[256,3584]{1,0:T(8,128)(2,1)S(1)}, bf16[256,3584]{1,0:T(8,128)(2,1)}, u32[]{:S(2)}) copy-start(bf16[256,3584]{1,0:T(8,128)(2,1)} %hidden_ref.3) | copy-start | bytes 5505028
  26.9 15.0 %copy-start.6 = (s32[3584]{0:T(1024)S(1)}, s32[3584]{0:T(1024)}, u32[]{:S(2)}) copy-start(s32[3584]{0:T(1024)} %signs_ref.3) | copy-start | bytes 43012
  35.1 0.8 copy-start.2
  35.9 2.9 %copy-start.13 = (s8[4,3584,512]{2,1,0:T(32,128)(4,1)}, s8[4,3584,512]{2,1,0:T(32,128)(4,1)S(1)}, u32[]{:S(2)}) copy-start(s8[4,3584,512]{2,1,0:T(32,128)(4,1)S(1)} %dequantize.1.refs_6_.refs_3_) | copy-start | bytes 22020100
  38.8 1.9 %collective-permute-start.3 = (bf16[32,4096]{1,0:T(8,128)(2,1)}, bf16[32,4096]{1,0:T(8,128)(2,1)}, u32[]{:S(2)}, u32[]{:S(2)}) collective-permute-start(bf16[32,4096]{1,0:T(8,128)(2,1)} %get-tuple-element.16), channel_id=1, source_target_pairs={{0,1},{1,0},{2,3},{3,2},{4,5},{5,4},{6,7},{7,6},{8,9},{9,8},{10,11... | collective-permute-start | bytes 786440 | tf_op jit(solution)/shard_map/ppermute | solution.py:326
  41.9 16.2 %copy-start.5 = (bf16[28,4096]{1,0:T(8,128)(2,1)S(1)}, bf16[28,4096]{1,0:T(8,128)(2,1)}, u32[]{:S(2)}) copy-start(bf16[28,4096]{1,0:T(8,128)(2,1)} %copy-done.4) | copy-start | bytes 688132
  45.2 12.8 %collective-permute-start.7 = (bf16[64,3584]{1,0:T(8,128)(2,1)S(1)}, bf16[64,3584]{1,0:T(8,128)(2,1)S(1)}, u32[]{:S(2)}, u32[]{:S(2)}) collective-permute-start(bf16[64,3584]{1,0:T(8,128)(2,1)S(1)} %get-tuple-element.23), channel_id=1, source_target_pairs={{0,2},{1,3},{2,0},{3,1},{4,6},{5,7},{6,4},{7,5},{8,10},{9,11},{10,... | collective-permute-start | bytes 1376264 | tf_op jit(solution)/shard_map/ppermute | solution.py:326
  58.0 3.1 %copy-start.14 = (s8[4,3584,512]{2,1,0:T(32,128)(4,1)S(1)}, s8[4,3584,512]{2,1,0:T(32,128)(4,1)}, u32[]{:S(2)}) copy-start(s8[4,3584,512]{2,1,0:T(32,128)(4,1)} %copy-done.13) | copy-start | bytes 22020100
  61.1 32.9 %copy-start.15 = (s8[4,3584,512]{2,1,0:T(32,128)(4,1)S(1)}, s8[4,3584,512]{2,1,0:T(32,128)(4,1)}, u32[]{:S(2)}) copy-start(s8[4,3584,512]{2,1,0:T(32,128)(4,1)} %copy-done.13) | copy-start | bytes 22020100
  67.8 2.2 %collective-permute-start.8 = (bf16[32,4096]{1,0:T(8,128)(2,1)S(1)}, bf16[32,4096]{1,0:T(8,128)(2,1)S(1)}, u32[]{:S(2)}, u32[]{:S(2)}) collective-permute-start(bf16[32,4096]{1,0:T(8,128)(2,1)S(1)} %get-tuple-element.25), channel_id=1, source_target_pairs={{0,1},{1,0},{2,3},{3,2},{4,5},{5,4},{6,7},{7,6},{8,9},{9,8},{10,11... | collective-permute-start | bytes 786440 | tf_op jit(solution)/shard_map/ppermute | solution.py:326
  67.9 36.9 %collective-permute-start.9 = (bf16[16,4096]{1,0:T(8,128)(2,1)S(1)}, bf16[16,4096]{1,0:T(8,128)(2,1)S(1)}, u32[]{:S(2)}, u32[]{:S(2)}) collective-permute-start(bf16[16,4096]{1,0:T(8,128)(2,1)S(1)} %select_convert_fusion.2), channel_id=1, source_target_pairs={{0,2},{1,3},{2,0},{3,1},{4,6},{5,7},{6,4},{7,5},{8,10},{9,11},{10,... | collective-permute-start | bytes 393224 | tf_op jit(solution)/shard_map/ppermute | solution.py:326
  69.7 24.3 %collective-permute-start.5 = (bf16[128,3584]{1,0:T(8,128)(2,1)S(1)}, bf16[128,3584]{1,0:T(8,128)(2,1)S(1)}, u32[]{:S(2)}, u32[]{:S(2)}) collective-permute-start(bf16[128,3584]{1,0:T(8,128)(2,1)S(1)} %get-tuple-element.19), channel_id=1, source_target_pairs={{0,2},{1,3},{2,0},{3,1},{4,6},{5,7},{6,4},{7,5},{8,10},{9,11},{10,... | collective-permute-start | bytes 2752520 | tf_op jit(solution)/shard_map/ppermute | solution.py:326
  70.1 34.7 %collective-permute-start.11 = (bf16[16,4096]{1,0:T(8,128)(2,1)S(1)}, bf16[16,4096]{1,0:T(8,128)(2,1)S(1)}, u32[]{:S(2)}, u32[]{:S(2)}) collective-permute-start(bf16[16,4096]{1,0:T(8,128)(2,1)S(1)} %select_convert_fusion.1), channel_id=1, source_target_pairs={{0,2},{1,3},{2,0},{3,1},{4,6},{5,7},{6,4},{7,5},{8,10},{9,11},{10,... | collective-permute-start | bytes 393224 | tf_op jit(solution)/shard_map/ppermute | solution.py:326
  100.7 2.0 %collective-permute-start.6 = (bf16[64,4096]{1,0:T(8,128)(2,1)S(1)}, bf16[64,4096]{1,0:T(8,128)(2,1)S(1)}, u32[]{:S(2)}, u32[]{:S(2)}) collective-permute-start(bf16[64,4096]{1,0:T(8,128)(2,1)S(1)} %get-tuple-element.21), channel_id=1, source_target_pairs={{0,1},{1,0},{2,3},{3,2},{4,5},{5,4},{6,7},{7,6},{8,9},{9,8},{10,11... | collective-permute-start | bytes 1572872 | tf_op jit(solution)/shard_map/ppermute | solution.py:326
  102.8 8.5 %copy-start.3 = (bf16[64,4096]{1,0:T(8,128)(2,1)S(1)}, bf16[64,4096]{1,0:T(8,128)(2,1)}, u32[]{:S(2)}) copy-start(bf16[64,4096]{1,0:T(8,128)(2,1)} %refs_6_.1) | copy-start | bytes 1572868
  102.9 8.4 %collective-permute-start.10 = (bf16[32,4096]{1,0:T(8,128)(2,1)S(1)}, bf16[32,4096]{1,0:T(8,128)(2,1)S(1)}, u32[]{:S(2)}, u32[]{:S(2)}) collective-permute-start(bf16[32,4096]{1,0:T(8,128)(2,1)S(1)} %select_convert_fusion), channel_id=1, source_target_pairs={{0,2},{1,3},{2,0},{3,1},{4,6},{5,7},{6,4},{7,5},{8,10},{9,11},{10,... | collective-permute-start | bytes 786440 | tf_op jit(solution)/shard_map/ppermute | solution.py:326

commit v6 on v5

--- a/solution.py
+++ b/solution.py
@@ -65,59 +65,73 @@
     return (1 - 2 * bit).astype(jnp.float32)
 
 
-def prepare_kernel(groups, token_rows, places, hidden_ref, signs_ref, *refs):
-    out_refs, (staged, flips, sems, flips_sem) = refs[:-4], refs[-4:]
-    width = hidden_ref.shape[1]
-    flips_copy = pltpu.make_async_copy(signs_ref, flips, flips_sem)
-    flips_copy.start()
-    copies, at = [], 0
-    for start, size in places:
+def flips_of(signs):
+    return (2 * signs - 1).astype(jnp.float32).reshape(1, signs.shape[0])
+
+
+def open_kernel(groups, token_rows, size, hidden_ref, signs_ref, out_ref, staged, flips, sems):
+    copies = [pltpu.make_async_copy(signs_ref, flips, sems.at[groups])]
+    for place, owner in enumerate(bit_reversed(groups)):
+        copies.append(
+            pltpu.make_async_copy(
+                hidden_ref.at[pl.ds(owner * token_rows, size), :],
+                staged.at[pl.ds(place * size, size), :],
+                sems.at[place],
+            )
+        )
+    for copy in copies:
+        copy.start()
+    for copy in copies:
+        copy.wait()
+    out_ref[...] = (staged[...].astype(jnp.float32) * flips_of(flips[...])).astype(jnp.bfloat16)
+
+
+def open_exchange(hidden, signs, groups, size):
+    rows, width = groups * size, hidden.shape[1]
+    return pl.pallas_call(
+        functools.partial(open_kernel, groups, hidden.shape[0] // groups, size),
+        out_shape=jax.ShapeDtypeStruct((rows, width), jnp.bfloat16),
+        in_specs=[HBM, HBM],
+        out_specs=VMEM,
+        scratch_shapes=[
+            pltpu.VMEM((rows, width), jnp.bfloat16),
+            pltpu.VMEM((width,), jnp.int32),
+            pltpu.SemaphoreType.DMA((groups + 1,)),
+        ],
+        compiler_params=pltpu.CompilerParams(vmem_limit_bytes=8 * 2**20),
+        cost_estimate=cost(rows * width),
+        name="open_exchange",
+    )(*[pltpu.with_memory_space_constraint(value, pltpu.HBM) for value in (hidden, signs)])
+
+
+def prepare_kernel(groups, places, hidden_ref, signs_ref, first_ref, *rest_refs):
+    token_rows = hidden_ref.shape[0] // groups
+    flips = flips_of(signs_ref[...])
+    at, out_ref = 0, first_ref
+    for chunk, (start, size) in enumerate(places):
+        if chunk == 1:
+            at, out_ref = 0, rest_refs[0]
         for owner in bit_reversed(groups):
-            copies.append(
-                pltpu.make_async_copy(
-                    hidden_ref.at[pl.ds(owner * token_rows + start, size), :],
-                    staged.at[pl.ds(at, size), :],
-                    sems.at[len(copies)],
-                )
-            )
-            copies[-1].start()
+            rows = hidden_ref[pl.ds(owner * token_rows + start, size), :]
+            out_ref[pl.ds(at, size), :] = (rows.astype(jnp.float32) * flips).astype(jnp.bfloat16)
             at += size
-    flips_copy.wait()
-    flip = (2 * flips[...] - 1).astype(jnp.float32).reshape(1, width)
-    first_rows = groups * places[0][1]
-    at = 0
-    for index, copy in enumerate(copies):
-        size = places[index // groups][1]
-        copy.wait()
-        value = (staged[pl.ds(at, size), :].astype(jnp.float32) * flip).astype(jnp.bfloat16)
-        if index < groups:
-            out_refs[0][pl.ds(at, size), :] = value
-        else:
-            out_refs[1][pl.ds(at - first_rows, size), :] = value
-        at += size
 
 
 def prepare(hidden, signs, groups, places):
     rows, width = hidden.shape
     first_rows = groups * places[0][1]
-    shapes = [pltpu.VMEM((first_rows, width), jnp.bfloat16)]
+    shapes = [pltpu.HBM((first_rows, width), jnp.bfloat16)]
     if len(places) > 1:
-        shapes.append(pltpu.VMEM((rows - first_rows, width), jnp.bfloat16))
-    return pl.pallas_call(
-        functools.partial(prepare_kernel, groups, rows // groups, places),
+        shapes.append(jax.ShapeDtypeStruct((rows - first_rows, width), jnp.bfloat16))
+    return pl.pallas_call(
+        functools.partial(prepare_kernel, groups, places),
         out_shape=shapes,
-        in_specs=[HBM, HBM],
+        in_specs=[VMEM, VMEM],
         out_specs=[VMEM] * len(shapes),
-        scratch_shapes=[
-            pltpu.VMEM((rows, width), jnp.bfloat16),
-            pltpu.VMEM((width,), jnp.int32),
-            pltpu.SemaphoreType.DMA((groups * len(places),)),
-            pltpu.SemaphoreType.DMA,
-        ],
         compiler_params=pltpu.CompilerParams(vmem_limit_bytes=8 * 2**20),
         cost_estimate=cost(rows * width),
         name="prepare",
-    )(*[pltpu.with_memory_space_constraint(value, pltpu.HBM) for value in (hidden, signs)])
+    )(hidden, signs)
 
 
 def rotate_blocks(mixed, table_ref, stacked_ref):
@@ -281,6 +295,31 @@
     )(me, *parts, *tables, scales, weights)
 
 
+def fold_kernel(bit, me_ref, keep_ref, got_ref, value_ref, send_ref):
+    half = value_ref.shape[0]
+    upper = jnp.right_shift(me_ref[0], bit) & 1 == 1
+    first = keep_ref[:half, :] + got_ref[:half, :].astype(jnp.float32)
+    second = keep_ref[half:, :] + got_ref[half:, :].astype(jnp.float32)
+    value_ref[...] = jnp.where(upper, second, first)
+    send_ref[...] = jnp.where(upper, first, second).astype(jnp.bfloat16)
+
+
+def fold(keep, got, me, bit):
+    rows, features = keep.shape
+    return pl.pallas_call(
+        functools.partial(fold_kernel, bit),
+        out_shape=(
+            jax.ShapeDtypeStruct((rows // 2, features), jnp.float32),
+            jax.ShapeDtypeStruct((rows // 2, features), jnp.bfloat16),
+        ),
+        in_specs=[SMEM, VMEM, VMEM],
+        out_specs=(VMEM, VMEM),
+        compiler_params=pltpu.CompilerParams(vmem_limit_bytes=4 * 2**20),
+        cost_estimate=cost(rows * features),
+        name="fold",
+    )(me, keep, got)
+
+
 def finish_kernel(sizes, scale, *refs):
     chunks = len(sizes)
     keeps, gots = refs[:chunks], refs[chunks : 2 * chunks]
@@ -329,10 +368,13 @@
         return jnp.right_shift(me, bit) & 1
 
     places = [(sum(sizes[:chunk]), sizes[chunk]) for chunk in range(chunks)]
+    opened = open_exchange(hidden, signs, groups, sizes[0])
     first, *sent = prepare(hidden, signs, groups, places)
     have = {0: first}
     for bit in reversed(range(bits)):
-        have.update({r ^ (1 << bit): swap(value, bit) for r, value in list(have.items())})
+        wide = bit == bits - 1 and bits > 1
+        source = {0: opened} if wide else have
+        have.update({r ^ (1 << bit): swap(value, bit) for r, value in list(source.items())})
     stages = [([have[r] for r in range(groups)], table)]
     if chunks > 1:
         other = swap(sent[0], 0)
@@ -355,11 +397,7 @@
         value, send = project(parts, where, maybe_table, scales, weights, unit)
         got = swap(send, 0)
         for bit in range(1, bits):
-            value = value + got.astype(jnp.float32)
-            half = value.shape[0] // 2
-            upper = bit_of(bit) == 1
-            send = jnp.where(upper, value[:half], value[half:]).astype(jnp.bfloat16)
-            value = jnp.where(upper, value[half:], value[:half])
+            value, send = fold(value, got, where, bit)
             got = swap(send, bit)
         keeps.append(value)
         gots.append(got)

time: 113 us -> 80.2 us (0.71)
  waiting for transfers between devices: 53 us -> 29.5 us
  local copies, waits for them, and re-layouts: 10.7 us -> 2.24 us
  other arithmetic: 1.57 us -> 0.05 us
    ppermute x12, waiting for transfers between devices: 53 us -> 29.5 us  [swap(): lax.ppermute(value, 'tensor', [(i, i ^ 1 << bit) for i in range(groups)])]
    unnamed x34 -> x16, local copies, waits for them, and re-layouts: 10.7 us -> 2.24 us
    add x3 -> x0, other arithmetic: 1.3 us -> none  [local(): value = value + got.astype(jnp.float32)]
    pallas_call x1 -> x5, Pallas kernels: 3.05 us -> 3.65 us  [the longest x1 1.97 us: open_exchange(): pl.pallas_call(functools.partial(open_kernel, groups, hidden.shape[0] //...]
  transfers between devices with their start and end apart: 12 -> 12, of which waited for: 6 -> 4; matrix products, arithmetic and copies ran while one was open for 1% -> 0% of each run, Pallas kernels for 18% -> 41%
where the time goes in v6:
time: 80.2 us; the launch traced here: 79.9 us
  Pallas kernels  35.8 us (45%)
  waiting for transfers between devices  29.5 us (37%)
  starting transfers between devices  11.6 us (14%)
  local copies, waits for them, and re-layouts  2.24 us (3%)
    ppermute x12, waiting for transfers between devices, swap(): lax.ppermute(value, 'tensor', [(i, i ^ 1 << bit) for i in range(groups)])  29.5 us
    pallas_call x3, Pallas kernels, project(): pl.pallas_call(functools.partial(project_kernel, count, unit, table is no...  22 us
    ppermute x12, starting transfers between devices, swap(): lax.ppermute(value, 'tensor', [(i, i ^ 1 << bit) for i in range(groups)])  11.6 us
    pallas_call x1, Pallas kernels, dequantize(): pl.pallas_call(dequantize_kernel, grid=(width // rows,), out_shape=jax.Sh...  5.56 us
    pallas_call x1, Pallas kernels, rotate(): pl.pallas_call(functools.partial(rotate_kernel, groups, places), out_shap...  3.32 us
    unnamed x16, local copies, waits for them, and re-layouts  2.24 us
    pallas_call x1, Pallas kernels, open_exchange(): pl.pallas_call(functools.partial(open_kernel, groups, hidden.shape[0] //...  1.97 us
  transfers between devices with their start and end apart: 12, of which 4 were waited for; matrix products, arithmetic and copies ran while one was open for 0% of the time, Pallas kernels for 41%

profile of v6, /device:TPU:0, one launch (start us, length us, event | category | flops | bytes accessed | tf_op | source)
XLA Modules:
  0.0 79.9 jit_solution(16953241870695473540)
XLA Ops:
  0.6 0.0 copy-start
  0.6 1.5 %copy-done = bf16[256,3584]{1,0:T(8,128)(2,1)S(1)} copy-done((bf16[256,3584]{1,0:T(8,128)(2,1)S(1)}, bf16[256,3584]{1,0:T(8,128)(2,1)}, u32[]{:S(2)}) %copy-start) | copy-done | bytes 1835032
  2.1 0.0 copy-start.4
  2.1 0.7 copy-done.4
  2.8 0.0 copy-start.1
  2.9 0.0 copy-start.2
  2.9 0.0 copy-start.5
  2.9 1.4 %prepare.1 = (bf16[64,3584]{1,0:T(8,128)(2,1)}, bf16[192,3584]{1,0:T(8,128)(2,1)}) custom-call(bf16[256,3584]{1,0:T(8,128)(2,1)S(1)} %copy-done, s32[3584]{0:T(1024)S(1)} %copy-done.4), custom_call_target="tpu_custom_call" | custom-call | flops 917504 | tf_op jit(solution)/shard_map/prepare/pallas_call | solution.py:126
  4.3 0.5 collective-permute-start.4
  4.8 0.0 collective-permute-start
  4.8 2.0 %open_exchange.1 = bf16[64,3584]{1,0:T(8,128)(2,1)} custom-call(bf16[256,3584]{1,0:T(8,128)(2,1)} %hidden_ref.5, s32[3584]{0:T(1024)} %signs_ref.5), custom_call_target="tpu_custom_call" | custom-call | flops 229376 | tf_op jit(solution)/shard_map/open_exchange/pallas_call | solution.py:91
  6.8 3.1 %collective-permute-start.1 = (bf16[64,3584]{1,0:T(8,128)(2,1)}, bf16[64,3584]{1,0:T(8,128)(2,1)}, u32[]{:S(2)}, u32[]{:S(2)}) collective-permute-start(bf16[64,3584]{1,0:T(8,128)(2,1)} %open_exchange.1), channel_id=1, source_target_pairs={{0,2},{1,3},{2,0},{3,1},{4,6},{5,7},{6,4},{7,5},{8,10},{9,11},{10,... | collective-permute-start | bytes 1376264 | tf_op jit(solution)/shard_map/ppermute | solution.py:365
  9.8 0.0 collective-permute-done.4.other_ref
  9.8 0.0 copy-done.1
  9.8 0.0 copy-done.2
  9.8 0.0 copy-done.5
  9.9 0.0 copy-start.7
  9.9 3.3 %rotate.1 = (f32[128,3584]{1,0:T(8,128)S(1)}, bf16[128,3584]{1,0:T(8,128)(2,1)S(1)}, f32[64,3584]{1,0:T(8,128)S(1)}, bf16[64,3584]{1,0:T(8,128)(2,1)S(1)}) custom-call(s32[1]{0:T(128)} %bitcast.me_ref, bf16[256,3584]{1,0:T(8,128)(2,1)S(1)} %copy-done.1, s32[3584]{0:T(1024)S(1)} %copy-done.5, bf16[192,3584]{1,0:T(8,128)(2,1)} %collective-permute-done.4.other_ref, ...), custom_call_target="tpu_custom_call" | custom-call | flops 1233125376 | tf_op jit(solution)/shard_map/rotate/pallas_call | solution.py:186
  13.2 1.0 %collective-permute-start.5 = (bf16[128,3584]{1,0:T(8,128)(2,1)S(1)}, bf16[128,3584]{1,0:T(8,128)(2,1)S(1)}, u32[]{:S(2)}, u32[]{:S(2)}) collective-permute-start(bf16[128,3584]{1,0:T(8,128)(2,1)S(1)} %get-tuple-element.26), channel_id=1, source_target_pairs={{0,2},{1,3},{2,0},{3,1},{4,6},{5,7},{6,4},{7,5},{8,10},{9,11},{10,... | collective-permute-start | bytes 2752520 | tf_op jit(solution)/shard_map/ppermute | solution.py:365
  14.1 0.0 copy-done.7
  14.2 7.3 %collective-permute-done.1.refs_2_ = bf16[64,3584]{1,0:T(8,128)(2,1)} collective-permute-done((bf16[64,3584]{1,0:T(8,128)(2,1)}, bf16[64,3584]{1,0:T(8,128)(2,1)}, u32[]{:S(2)}, u32[]{:S(2)}) %collective-permute-start.1) | collective-permute-done | bytes 458784 | tf_op jit(solution)/shard_map/ppermute | solution.py:365
  21.5 0.0 collective-permute-start.2
  21.5 5.6 %dequantize.1.refs_6_.refs_3_ = s8[4,3584,512]{2,1,0:T(32,128)(4,1)S(1)} custom-call(s32[3584,512]{1,0:T(8,128)} %packed_ref.1), custom_call_target="tpu_custom_call" | custom-call | flops 7516192768 | tf_op jit(solution)/shard_map/dequantize/pallas_call | solution.py:208
  27.1 2.1 %collective-permute-start.7 = (bf16[64,3584]{1,0:T(8,128)(2,1)S(1)}, bf16[64,3584]{1,0:T(8,128)(2,1)S(1)}, u32[]{:S(2)}, u32[]{:S(2)}) collective-permute-start(bf16[64,3584]{1,0:T(8,128)(2,1)S(1)} %get-tuple-element.31), channel_id=1, source_target_pairs={{0,2},{1,3},{2,0},{3,1},{4,6},{5,7},{6,4},{7,5},{8,10},{9,11},{10,... | collective-permute-start | bytes 1376264 | tf_op jit(solution)/shard_map/ppermute | solution.py:365
  29.2 11.9 %collective-permute-done.5.refs_1_ = bf16[128,3584]{1,0:T(8,128)(2,1)S(1)} collective-permute-done((bf16[128,3584]{1,0:T(8,128)(2,1)S(1)}, bf16[128,3584]{1,0:T(8,128)(2,1)S(1)}, u32[]{:S(2)}, u32[]{:S(2)}) %collective-permute-start.5) | collective-permute-done | bytes 917536 | tf_op jit(solution)/shard_map/ppermute | solution.py:365
  41.1 0.0 copy-start.6
  41.1 6.7 %project.4 = (f32[64,4096]{1,0:T(8,128)S(1)}, bf16[64,4096]{1,0:T(8,128)(2,1)S(1)}) custom-call(s32[1]{0:T(128)} %bitcast.me_ref, f32[128,3584]{1,0:T(8,128)S(1)} %get-tuple-element.25.refs_0_, bf16[128,3584]{1,0:T(8,128)(2,1)S(1)} %collective-permute-done.5.refs_1_, bf16[28,4096]{1,0:T(8,128)(2,1)S(1)} %multiply_convert_fusion.refs_5_.refs_2_, ...), custom_call_target="tpu_custom_call" | custom-call | flops 3758096384 | tf_op jit(solution)/shard_map/project/pallas_call | solution.py:280
  47.8 0.1 collective-permute-start.6
  47.8 0.0 collective-permute-done.refs_1_
  47.9 0.0 collective-permute-done.2.refs_3_
  47.9 0.0 copy-done.6
  47.9 8.7 %project.3 = (f32[32,4096]{1,0:T(8,128)S(1)}, bf16[32,4096]{1,0:T(8,128)(2,1)S(1)}) custom-call(s32[1]{0:T(128)} %bitcast.me_ref, bf16[64,3584]{1,0:T(8,128)(2,1)S(1)} %copy-done.6, bf16[64,3584]{1,0:T(8,128)(2,1)} %collective-permute-done.refs_1_, bf16[64,3584]{1,0:T(8,128)(2,1)} %collective-permute-done.1.refs_2_, ...), custom_call_target="tpu_custom_call" | custom-call | flops 3758096384 | tf_op jit(solution)/shard_map/project/pallas_call | solution.py:280
  56.6 0.5 collective-permute-start.3
  57.1 0.0 collective-permute-done.7.refs_1_
  57.1 6.7 %project.5 = (f32[32,4096]{1,0:T(8,128)S(1)}, bf16[32,4096]{1,0:T(8,128)(2,1)S(1)}) custom-call(s32[1]{0:T(128)} %bitcast.me_ref, f32[64,3584]{1,0:T(8,128)S(1)} %get-tuple-element.30.refs_0_, bf16[64,3584]{1,0:T(8,128)(2,1)S(1)} %collective-permute-done.7.refs_1_, bf16[28,4096]{1,0:T(8,128)(2,1)S(1)} %multiply_convert_fusion.refs_5_.refs_2_, ...), custom_call_target="tpu_custom_call" | custom-call | flops 3758096384 | tf_op jit(solution)/shard_map/project/pallas_call | solution.py:280
  63.8 0.0 copy-start.3
  63.8 0.1 collective-permute-start.8
  63.9 0.0 collective-permute-done.6.got_ref
  63.9 0.1 fold.4
  64.0 2.1 %collective-permute-start.10 = (bf16[32,4096]{1,0:T(8,128)(2,1)S(1)}, bf16[32,4096]{1,0:T(8,128)(2,1)S(1)}, u32[]{:S(2)}, u32[]{:S(2)}) collective-permute-start(bf16[32,4096]{1,0:T(8,128)(2,1)S(1)} %get-tuple-element.36), channel_id=1, source_target_pairs={{0,2},{1,3},{2,0},{3,1},{4,6},{5,7},{6,4},{7,5},{8,10},{9,11},{10,... | collective-permute-start | bytes 786440 | tf_op jit(solution)/shard_map/ppermute | solution.py:365
  66.1 0.0 collective-permute-done.3.got_ref
  66.1 0.1 fold.3
  66.2 0.1 collective-permute-start.9
  66.3 0.0 collective-permute-done.8.got_ref
  66.3 0.1 fold.5
  66.4 2.1 %collective-permute-start.11 = (bf16[16,4096]{1,0:T(8,128)(2,1)S(1)}, bf16[16,4096]{1,0:T(8,128)(2,1)S(1)}, u32[]{:S(2)}, u32[]{:S(2)}) collective-permute-start(bf16[16,4096]{1,0:T(8,128)(2,1)S(1)} %get-tuple-element.37), channel_id=1, source_target_pairs={{0,2},{1,3},{2,0},{3,1},{4,6},{5,7},{6,4},{7,5},{8,10},{9,11},{10,... | collective-permute-start | bytes 393224 | tf_op jit(solution)/shard_map/ppermute | solution.py:365
  68.4 7.7 %collective-permute-done.9.refs_3_ = bf16[16,4096]{1,0:T(8,128)(2,1)S(1)} collective-permute-done((bf16[16,4096]{1,0:T(8,128)(2,1)S(1)}, bf16[16,4096]{1,0:T(8,128)(2,1)S(1)}, u32[]{:S(2)}, u32[]{:S(2)}) %collective-permute-start.9) | collective-permute-done | bytes 131104 | tf_op jit(solution)/shard_map/ppermute | solution.py:365
  76.1 2.6 %collective-permute-done.11.refs_5_ = bf16[16,4096]{1,0:T(8,128)(2,1)S(1)} collective-permute-done((bf16[16,4096]{1,0:T(8,128)(2,1)S(1)}, bf16[16,4096]{1,0:T(8,128)(2,1)S(1)}, u32[]{:S(2)}, u32[]{:S(2)}) %collective-permute-start.11) | collective-permute-done | bytes 131104 | tf_op jit(solution)/shard_map/ppermute | solution.py:365
  78.7 0.0 collective-permute-done.10.refs_4_
  78.7 0.0 copy-done.3
  78.7 1.2 %finish.1 = (bf16[64,4096]{1,0:T(8,128)(2,1)}, bf16[64,4096]{1,0:T(8,128)(2,1)}) custom-call(f32[16,4096]{1,0:T(8,128)S(1)} %get-tuple-element.23.refs_0_, f32[32,4096]{1,0:T(8,128)S(1)} %get-tuple-element.29.refs_1_, f32[16,4096]{1,0:T(8,128)S(1)} %get-tuple-element.34.refs_2_, bf16[16,4096]{1,0:T(8,128)(2,1)S(1)} %collective-permute-done.9.refs_3_, ...), custom_call_target="tpu_custom_call" | custom-call | flops 268435456 | tf_op jit(solution)/shard_map/finish/pallas_call | solution.py:342
  (2 shorter events, 0.1 us)
Async XLA Ops:
  0.6 1.5 %copy-start = (bf16[256,3584]{1,0:T(8,128)(2,1)S(1)}, bf16[256,3584]{1,0:T(8,128)(2,1)}, u32[]{:S(2)}) copy-start(bf16[256,3584]{1,0:T(8,128)(2,1)} %hidden_ref.5) | copy-start | bytes 5505028
  2.1 0.7 copy-start.4
  2.8 7.0 %copy-start.1 = (bf16[256,3584]{1,0:T(8,128)(2,1)S(1)}, bf16[256,3584]{1,0:T(8,128)(2,1)}, u32[]{:S(2)}) copy-start(bf16[256,3584]{1,0:T(8,128)(2,1)} %hidden_ref.5) | copy-start | bytes 5505028
  2.9 7.0 %copy-start.2 = (bf16[896,896]{1,0:T(8,128)(2,1)S(1)}, bf16[896,896]{1,0:T(8,128)(2,1)}, u32[]{:S(2)}) copy-start(bf16[896,896]{1,0:T(8,128)(2,1)} %constant.42.clone.refs_4_.table_ref) | copy-start | bytes 4816900
  2.9 7.0 %copy-start.5 = (s32[3584]{0:T(1024)S(1)}, s32[3584]{0:T(1024)}, u32[]{:S(2)}) copy-start(s32[3584]{0:T(1024)} %signs_ref.5) | copy-start | bytes 43012
  4.3 5.6 %collective-permute-start.4 = (bf16[192,3584]{1,0:T(8,128)(2,1)}, bf16[192,3584]{1,0:T(8,128)(2,1)}, u32[]{:S(2)}, u32[]{:S(2)}) collective-permute-start(bf16[192,3584]{1,0:T(8,128)(2,1)} %get-tuple-element.24), channel_id=1, source_target_pairs={{0,1},{1,0},{2,3},{3,2},{4,5},{5,4},{6,7},{7,6},{8,9},{9,8},{10,11... | collective-permute-start | bytes 4128776 | tf_op jit(solution)/shard_map/ppermute | solution.py:365
  4.8 43.1 %collective-permute-start = (bf16[64,3584]{1,0:T(8,128)(2,1)}, bf16[64,3584]{1,0:T(8,128)(2,1)}, u32[]{:S(2)}, u32[]{:S(2)}) collective-permute-start(bf16[64,3584]{1,0:T(8,128)(2,1)} %get-tuple-element.20.refs_0_), channel_id=1, source_target_pairs={{0,1},{1,0},{2,3},{3,2},{4,5},{5,4},{6,7},{7,6},{8,9},{9,8},{10,11... | collective-permute-start | bytes 1376264 | tf_op jit(solution)/shard_map/ppermute | solution.py:365
  6.8 14.8 %collective-permute-start.1 = (bf16[64,3584]{1,0:T(8,128)(2,1)}, bf16[64,3584]{1,0:T(8,128)(2,1)}, u32[]{:S(2)}, u32[]{:S(2)}) collective-permute-start(bf16[64,3584]{1,0:T(8,128)(2,1)} %open_exchange.1), channel_id=1, source_target_pairs={{0,2},{1,3},{2,0},{3,1},{4,6},{5,7},{6,4},{7,5},{8,10},{9,11},{10,... | collective-permute-start | bytes 1376264 | tf_op jit(solution)/shard_map/ppermute | solution.py:365
  9.9 4.3 %copy-start.7 = (s32[28,4096]{1,0:T(8,128)S(1)}, s32[28,4096]{1,0:T(8,128)}, u32[]{:S(2)}) copy-start(s32[28,4096]{1,0:T(8,128)} %param.9) | copy-start | bytes 1376260
  13.2 27.9 %collective-permute-start.5 = (bf16[128,3584]{1,0:T(8,128)(2,1)S(1)}, bf16[128,3584]{1,0:T(8,128)(2,1)S(1)}, u32[]{:S(2)}, u32[]{:S(2)}) collective-permute-start(bf16[128,3584]{1,0:T(8,128)(2,1)S(1)} %get-tuple-element.26), channel_id=1, source_target_pairs={{0,2},{1,3},{2,0},{3,1},{4,6},{5,7},{6,4},{7,5},{8,10},{9,11},{10,... | collective-permute-start | bytes 2752520 | tf_op jit(solution)/shard_map/ppermute | solution.py:365
  21.5 26.3 %collective-permute-start.2 = (bf16[64,3584]{1,0:T(8,128)(2,1)}, bf16[64,3584]{1,0:T(8,128)(2,1)S(1)}, u32[]{:S(2)}, u32[]{:S(2)}) collective-permute-start(bf16[64,3584]{1,0:T(8,128)(2,1)} %collective-permute-done.1.refs_2_), channel_id=1, source_target_pairs={{0,1},{1,0},{2,3},{3,2},{4,5},{5,4},{6,7},{7,6},{8,9},{9,8},{10,11... | collective-permute-start | bytes 1376264 | tf_op jit(solution)/shard_map/ppermute | solution.py:365
  27.1 30.0 %collective-permute-start.7 = (bf16[64,3584]{1,0:T(8,128)(2,1)S(1)}, bf16[64,3584]{1,0:T(8,128)(2,1)S(1)}, u32[]{:S(2)}, u32[]{:S(2)}) collective-permute-start(bf16[64,3584]{1,0:T(8,128)(2,1)S(1)} %get-tuple-element.31), channel_id=1, source_target_pairs={{0,2},{1,3},{2,0},{3,1},{4,6},{5,7},{6,4},{7,5},{8,10},{9,11},{10,... | collective-permute-start | bytes 1376264 | tf_op jit(solution)/shard_map/ppermute | solution.py:365
  41.1 6.8 %copy-start.6 = (bf16[64,3584]{1,0:T(8,128)(2,1)S(1)}, bf16[64,3584]{1,0:T(8,128)(2,1)}, u32[]{:S(2)}) copy-start(bf16[64,3584]{1,0:T(8,128)(2,1)} %get-tuple-element.20.refs_0_) | copy-start | bytes 1376260
  47.8 16.1 %collective-permute-start.6 = (bf16[64,4096]{1,0:T(8,128)(2,1)S(1)}, bf16[64,4096]{1,0:T(8,128)(2,1)S(1)}, u32[]{:S(2)}, u32[]{:S(2)}) collective-permute-start(bf16[64,4096]{1,0:T(8,128)(2,1)S(1)} %get-tuple-element.28), channel_id=1, source_target_pairs={{0,1},{1,0},{2,3},{3,2},{4,5},{5,4},{6,7},{7,6},{8,9},{9,8},{10,11... | collective-permute-start | bytes 1572872 | tf_op jit(solution)/shard_map/ppermute | solution.py:365
  56.6 9.6 %collective-permute-start.3 = (bf16[32,4096]{1,0:T(8,128)(2,1)S(1)}, bf16[32,4096]{1,0:T(8,128)(2,1)S(1)}, u32[]{:S(2)}, u32[]{:S(2)}) collective-permute-start(bf16[32,4096]{1,0:T(8,128)(2,1)S(1)} %get-tuple-element.22), channel_id=1, source_target_pairs={{0,1},{1,0},{2,3},{3,2},{4,5},{5,4},{6,7},{7,6},{8,9},{9,8},{10,11... | collective-permute-start | bytes 786440 | tf_op jit(solution)/shard_map/ppermute | solution.py:365
  63.8 14.9 %copy-start.3 = (bf16[64,4096]{1,0:T(8,128)(2,1)S(1)}, bf16[64,4096]{1,0:T(8,128)(2,1)}, u32[]{:S(2)}) copy-start(bf16[64,4096]{1,0:T(8,128)(2,1)} %refs_6_.1) | copy-start | bytes 1572868
  63.8 2.5 %collective-permute-start.8 = (bf16[32,4096]{1,0:T(8,128)(2,1)S(1)}, bf16[32,4096]{1,0:T(8,128)(2,1)S(1)}, u32[]{:S(2)}, u32[]{:S(2)}) collective-permute-start(bf16[32,4096]{1,0:T(8,128)(2,1)S(1)} %get-tuple-element.33), channel_id=1, source_target_pairs={{0,1},{1,0},{2,3},{3,2},{4,5},{5,4},{6,7},{7,6},{8,9},{9,8},{10,11... | collective-permute-start | bytes 786440 | tf_op jit(solution)/shard_map/ppermute | solution.py:365
  64.0 14.6 %collective-permute-start.10 = (bf16[32,4096]{1,0:T(8,128)(2,1)S(1)}, bf16[32,4096]{1,0:T(8,128)(2,1)S(1)}, u32[]{:S(2)}, u32[]{:S(2)}) collective-permute-start(bf16[32,4096]{1,0:T(8,128)(2,1)S(1)} %get-tuple-element.36), channel_id=1, source_target_pairs={{0,2},{1,3},{2,0},{3,1},{4,6},{5,7},{6,4},{7,5},{8,10},{9,11},{10,... | collective-permute-start | bytes 786440 | tf_op jit(solution)/shard_map/ppermute | solution.py:365
  66.2 9.9 %collective-permute-start.9 = (bf16[16,4096]{1,0:T(8,128)(2,1)S(1)}, bf16[16,4096]{1,0:T(8,128)(2,1)S(1)}, u32[]{:S(2)}, u32[]{:S(2)}) collective-permute-start(bf16[16,4096]{1,0:T(8,128)(2,1)S(1)} %get-tuple-element.35), channel_id=1, source_target_pairs={{0,2},{1,3},{2,0},{3,1},{4,6},{5,7},{6,4},{7,5},{8,10},{9,11},{10,... | collective-permute-start | bytes 393224 | tf_op jit(solution)/shard_map/ppermute | solution.py:365
  66.4 12.3 %collective-permute-start.11 = (bf16[16,4096]{1,0:T(8,128)(2,1)S(1)}, bf16[16,4096]{1,0:T(8,128)(2,1)S(1)}, u32[]{:S(2)}, u32[]{:S(2)}) collective-permute-start(bf16[16,4096]{1,0:T(8,128)(2,1)S(1)} %get-tuple-element.37), channel_id=1, source_target_pairs={{0,2},{1,3},{2,0},{3,1},{4,6},{5,7},{6,4},{7,5},{8,10},{9,11},{10,... | collective-permute-start | bytes 393224 | tf_op jit(solution)/shard_map/ppermute | solution.py:365
